TPU v7x, 128 devices: a whole 4x4x4 slice. The times are simulated.
128 devices in a mesh: rep: 8 (over z, core), ep: 16 (over x, y).
Axes of the slice: x: 4, y: 4, z: 4, core: 2. Of those that a mesh axis runs over, the one named last changes fastest.
Arguments:
- latent_pages: bfloat16 [6144, 36864], P(('rep', 'ep')), may hold values from -4 to 4
- queries: bfloat16 [1024, 147456], P(('rep', 'ep')), may hold values from -4 to 4
- residual: bfloat16 [1024, 14336], P(('rep', 'ep')), may hold values from -6 to 6
- page_count: int32 [8, 16, 8], P(None, 'ep'), may hold values from 1 to 12, 48 in all within a row
- last_fill: int32 [8, 16, 8], P(None, 'ep'), may hold values from 4 to 64
- page_order: int32 [128, 48], P(('rep', 'ep')), may hold values from 0 to 47, each once within a row
- shed_slots: int32 [8, 16, 2], P(None, 'ep'), may hold values from 0 to 7, as said below
- shed_shift: int32 [16, 2], P('ep'), may hold values from 1 to 7
- expert_ids: int32 [4096, 8], P(('rep', 'ep')), may hold values from 0 to 127, all different within a row; in each aligned block of 32 rows (0 to 31, 32 to 63, ...) at most 4 rows name the same one
- gate_weight: float32 [4096, 8], P(('rep', 'ep')), may hold values from 0.05 to 0.5
- expert_home: int32 [128], replicated, may hold values from 0 to 127, each once
- norm_gain: float32 [3584], replicated, may hold values from 0.1 to 1.9
- value_up: bfloat16 [64, 512, 128], P('ep'), may hold values from -0.59765625 to 0.59765625
- out_weight: bfloat16 [8192, 3584], P('ep'), may hold values from -0.14941406 to 0.14941406
- expert_in: bfloat16 [128, 3584, 1024], P(('rep', 'ep')), may hold values from -0.09375 to 0.09375
- expert_out: bfloat16 [128, 1024, 3584], P(('rep', 'ep')), may hold values from -0.1875 to 0.1875
Outputs:
- attn_proj: bfloat16 [1024, 14336], P(('rep', 'ep'))
- layer_out: bfloat16 [1024, 14336], P(('rep', 'ep'))
Inputs may be any that keep to these rules, and one draw needn't show every extreme that they name: `shed_slots`: for each device, 2 different slots. `expert_ids`: each row names 8 different experts; in the rows of one device no expert is named by more than 4 rows.
All inputs are finite; a program needn't handle non-finite values.
Results may differ from a plain program's by a relative error of at most 0.015.
Values may be sent and summed in bfloat16 or wider, within the bound.
No kernel may reach another device: no remote copies, remote signals or barrier semaphores. Data moves between devices by JAX's collectives and lax.ppermute only.
A program may use at most 192 MiB of HBM per device.

v0:
```python
import functools

import jax
import jax.numpy as jnp
from jax import lax
from jax.experimental import pallas as pl
from jax.experimental.pallas import tpu as pltpu
from jax.sharding import Mesh
from jax.sharding import PartitionSpec as P

D = 3584
HALF = D // 2
HEADS = 64
LAT = 512
KVW = 576
VHEAD = 128
FFE = 1024
TOP = 8
PAGE = 64
SPEC = 4
MAXP = 12
REQ_DEV = 8
PAGES_DEV = 48
TOK_DEV = REQ_DEV * SPEC
N_EP = 16
HEADS_DEV = HEADS // N_EP
DEVICES = 128
CAP = 4
BAND = D // 4
KEYS = MAXP * PAGE
EP = ("ep_0", "ep_1")
REP_EP = ("rep", "ep_0", "ep_1")
SCORE_SCALE = 192.0 ** (-0.5)
NORM_EPS = 0.25
BF = jnp.bfloat16
F32 = jnp.float32


def iota2(rows, cols, dim):
    return lax.broadcasted_iota(jnp.int32, (rows, cols), dim)


def rows_first(source_of, size=256):
    return (iota2(size, size, 1) == source_of(iota2(size, size, 0))).astype(BF)


def mm(a, b):
    return jnp.dot(a, b, preferred_element_type=F32)


def near(value):
    return pltpu.with_memory_space_constraint(value, pltpu.VMEM)


def distant(value):
    return pltpu.with_memory_space_constraint(value, pltpu.HBM)


WINDOW = 12
SPAN = 8 * KVW


def attention_body(pick_ref, count_ref, fill_ref, query_hbm, page_hbm, out_hbm, *scratch):
    key_s, order_s, piece_s, query_s, page_v, query_v, out_ref = scratch[:7]
    page_sem, query_sem, out_sem = scratch[7:]

    def page_load(group):
        columns = pl.ds(pl.multiple_of(group * SPAN, 128), SPAN)
        return pltpu.make_async_copy(page_hbm.at[:, columns], page_v.at[group], page_sem.at[group])

    def query_load(position, pair):
        at = position * HEADS * KVW + pair * SPAN
        return pltpu.make_async_copy(
            query_hbm.at[:, pl.ds(pl.multiple_of(at, 128), SPAN)],
            query_v.at[pair, position],
            query_sem.at[pair, position],
        )

    def result_copy(i):
        rows = pl.ds(pl.multiple_of(i * 16, 16), 16)
        return pltpu.make_async_copy(out_ref.at[:, rows], out_hbm.at[:, rows], out_sem.at[i])

    for group in range(8):
        page_load(group).start()
    for pair in range(8):
        for position in range(SPEC):
            query_load(position, pair).start()
    shift = iota2(8, 128, 0) * PAGES_DEV
    for place in range(PAGES_DEV):
        order_s[place * 8 : place * 8 + 8, :] = shift + pick_ref[0, place]
    to_place = (iota2(384, 384, 1) == order_s[:, :1]).astype(BF)

    def regroup_keys(group, carry):
        page_load(group).wait()
        tokens = [page_v[group, :, t * KVW : (t + 1) * KVW] for t in range(8)]
        key_s[group] = mm(to_place, jnp.concatenate(tokens, axis=0))
        return carry

    lax.fori_loop(0, 8, regroup_keys, 0)
    row, col = iota2(REQ_DEV * 32, 256, 0), iota2(REQ_DEV * 32, 256, 1)
    by_request = (col == row % 32 * 8 + row // 32).astype(BF)

    def regroup_queries(pair, carry):
        for position in range(SPEC):
            query_load(position, pair).wait()
        for column in range(2):
            for position in range(SPEC):
                for head in range(HEADS_DEV):
                    at = (column * HEADS_DEV + head) * KVW
                    place = (column * SPEC + position) * HEADS_DEV + head
                    piece_s[place * 8 : place * 8 + 8, :] = query_v[
                        pair, position, :, at : at + KVW
                    ].astype(F32)
        rows = mm(by_request, piece_s[...].astype(BF)).astype(BF)
        query_s[:, pl.ds(pl.multiple_of(pair * 32, 32), 32), :] = rows.reshape(REQ_DEV, 32, KVW)
        return carry

    lax.fori_loop(0, 8, regroup_queries, 0)

    replica = lax.axis_index("rep")
    rows = SPEC * HEADS
    late = iota2(rows, 1, 0) // HEADS_DEV % SPEC - SPEC + 1
    key = iota2(1, KEYS, 1)
    place = key % (WINDOW * 8) // 8
    token = place * PAGE + key // (WINDOW * 8) * 8 + key % 8

    def request(i, offset):
        count = count_ref[replica, 0, i]
        length = (count - 1) * PAGE + fill_ref[replica, 0, i]
        start = jnp.minimum(offset, PAGES_DEV - WINDOW)
        skip = offset - start
        keys = key_s[:, pl.ds(pl.multiple_of(start * 8, 8), WINDOW * 8), :]
        keys = keys.reshape(KEYS, KVW).astype(BF)
        scores = lax.dot_general(
            query_s[i], keys, (((1,), (1,)), ((), ())), preferred_element_type=F32
        )
        at = jnp.where(place < skip, KEYS, token - skip * PAGE)
        scores = jnp.where(at < late + length, scores * SCORE_SCALE, -1e30)
        exponent = jnp.exp(scores - jnp.max(scores, axis=1, keepdims=True))
        total = jnp.sum(exponent, axis=1, keepdims=True)
        latent = mm(exponent.astype(BF), keys[:, :LAT]) / total
        out_ref[:, pl.ds(pl.multiple_of(i * 16, 16), 16), :] = latent.astype(BF).reshape(
            N_EP, 16, LAT
        )
        result_copy(i).start()
        return offset + count

    lax.fori_loop(0, REQ_DEV, request, jnp.int32(0))
    for i in range(REQ_DEV):
        result_copy(i).wait()


def attention(page_order, page_count, last_fill, queries, pages):
    few = pl.BlockSpec(memory_space=pltpu.SMEM)
    far = pl.BlockSpec(memory_space=pltpu.HBM)
    return pl.pallas_call(
        attention_body,
        in_specs=[few, few, few, far, far],
        out_specs=far,
        out_shape=pltpu.HBM((N_EP, REQ_DEV * 16, LAT), BF),
        scratch_shapes=[
            pltpu.VMEM((8, PAGES_DEV * 8, KVW), F32),
            pltpu.VMEM((PAGES_DEV * 8, 128), jnp.int32),
            pltpu.VMEM((256, KVW), F32),
            pltpu.VMEM((REQ_DEV, SPEC * HEADS, KVW), BF),
            pltpu.VMEM((8, PAGES_DEV, SPAN), BF),
            pltpu.VMEM((8, SPEC, REQ_DEV, SPAN), BF),
            pltpu.VMEM((N_EP, REQ_DEV * 16, LAT), BF),
            pltpu.SemaphoreType.DMA((8,)),
            pltpu.SemaphoreType.DMA((8, SPEC)),
            pltpu.SemaphoreType.DMA((REQ_DEV,)),
        ],
        cost_estimate=pl.CostEstimate(
            flops=7 << 30, bytes_accessed=8 << 20, transcendentals=8 * 256 * 768
        ),
        compiler_params=pltpu.CompilerParams(vmem_limit_bytes=40 << 20),
        name="attention",
    )(*[distant(each) for each in (page_order, page_count, last_fill, queries, pages)])


def weight_loads(weight_hbm, weight_ref, sems):
    loads = []
    for band in range(4):
        columns = pl.ds(band * BAND, BAND)
        loads.append(
            pltpu.make_async_copy(
                weight_hbm.at[:, columns], weight_ref.at[:, columns], sems.at[band]
            )
        )
        loads[-1].start()
    return loads


def part_of(order_ref, lifted_ref, picked_ref, weight_ref, load, band, first):
    for place in range(8):
        source = order_ref[band * N_EP + first + place]
        picked_ref[place * 32 : place * 32 + 32, :] = lifted_ref[source]
    load.wait()
    return mm(picked_ref[...], weight_ref[:, band * BAND : (band + 1) * BAND]).astype(BF)


def sent_body(order_ref, latent_ref, up_hbm, weight_hbm, *rest):
    outs, lifted_ref = rest[:4], rest[4]
    split_ref, picked_ref, part_ref, up_ref, weight_ref, in_sems, sems = rest[5:]
    up_load = pltpu.make_async_copy(up_hbm, up_ref, in_sems.at[4])
    up_load.start()
    loads = weight_loads(weight_hbm, weight_ref, in_sems)
    by_head = rows_first(lambda r: (r % 64) * 4 + r // 64)
    for step in range(8):
        both = mm(by_head, latent_ref[step]).astype(BF)
        for head in range(HEADS_DEV):
            split_ref[head, step * 64 : step * 64 + 64, :] = both[head * 64 : head * 64 + 64]
    up_load.wait()
    for head in range(HEADS_DEV):
        lifted = mm(split_ref[head], up_ref[head]).astype(BF)
        columns = slice(head * VHEAD, (head + 1) * VHEAD)
        lifted_ref[:, :, columns] = lifted.reshape(N_EP, 32, VHEAD)
    copies = []
    for band in range(4):
        part_ref[band] = part_of(
            order_ref, lifted_ref, picked_ref, weight_ref, loads[band], band, 8
        )
        copies.append(pltpu.make_async_copy(part_ref.at[band], outs[band], sems.at[band]))
        copies[-1].start()
    for copy in copies:
        copy.wait()


def kept_body(order_ref, lifted_ref, weight_hbm, out_ref, picked_ref, weight_ref, in_sems):
    loads = weight_loads(weight_hbm, weight_ref, in_sems)
    for band in range(4):
        out_ref[band] = part_of(
            order_ref, lifted_ref, picked_ref, weight_ref, loads[band], band, 0
        )


def project(order, latent, value_up, out_weight):
    few = pl.BlockSpec(memory_space=pltpu.SMEM)
    whole = pl.BlockSpec(memory_space=pltpu.VMEM)
    far = pl.BlockSpec(memory_space=pltpu.HBM)
    *sent, lifted = pl.pallas_call(
        sent_body,
        in_specs=[few, whole, far, far],
        out_specs=[far] * 4 + [whole],
        out_shape=[pltpu.HBM((256, BAND), BF)] * 4 + [pltpu.VMEM((N_EP, 32, 512), BF)],
        scratch_shapes=[
            pltpu.VMEM((HEADS_DEV, 512, LAT), BF),
            pltpu.VMEM((256, 512), BF),
            pltpu.VMEM((4, 256, BAND), BF),
            pltpu.VMEM((HEADS_DEV, LAT, VHEAD), BF),
            pltpu.VMEM((512, D), BF),
            pltpu.SemaphoreType.DMA((5,)),
            pltpu.SemaphoreType.DMA((4,)),
        ],
        cost_estimate=pl.CostEstimate(
            flops=2 << 30, bytes_accessed=8 << 20, transcendentals=0
        ),
        compiler_params=pltpu.CompilerParams(vmem_limit_bytes=20 << 20),
        name="project_sent",
    )(order, near(latent), distant(value_up), distant(out_weight))
    kept = pl.pallas_call(
        kept_body,
        in_specs=[few, whole, far],
        out_specs=whole,
        out_shape=pltpu.VMEM((4, 256, BAND), BF),
        scratch_shapes=[
            pltpu.VMEM((256, 512), BF),
            pltpu.VMEM((512, D), BF),
            pltpu.SemaphoreType.DMA((4,)),
        ],
        cost_estimate=pl.CostEstimate(
            flops=1 << 30, bytes_accessed=6 << 20, transcendentals=0
        ),
        compiler_params=pltpu.CompilerParams(vmem_limit_bytes=12 << 20),
        name="project_kept",
    )(order, near(lifted), distant(out_weight))
    return *sent, kept


def add_body(rows, split_at, joined, kept_ref, *rest):
    came, send, stay = rest[:split_at], rest[split_at:-1], rest[-1]
    split = 4 // split_at
    for band in range(4):
        piece = came[band // split]
        columns = slice(band % split * BAND, (band % split + 1) * BAND)
        total = kept_ref[band].astype(F32) + piece[:, columns].astype(F32)
        stay[band] = total[:rows]
        if joined:
            send[band // 2][:, band % 2 * BAND : (band % 2 + 1) * BAND] = total[rows:].astype(BF)
        else:
            send[band][...] = total[rows:].astype(BF)


def add_pieces(kept, came, joined):
    rows = kept.shape[1] // 2
    shape, count = ((rows, 2 * BAND), 2) if joined else ((rows, BAND), 4)
    whole = pl.BlockSpec(memory_space=pltpu.VMEM)
    outs = pl.pallas_call(
        functools.partial(add_body, rows, len(came), joined),
        in_specs=[whole] * (1 + len(came)),
        out_specs=[whole] * (count + 1),
        out_shape=[jax.ShapeDtypeStruct(shape, BF)] * count
        + [jax.ShapeDtypeStruct((4, rows, BAND), F32)],
        cost_estimate=pl.CostEstimate(
            flops=8 * rows * D, bytes_accessed=8 * rows * D, transcendentals=0
        ),
        compiler_params=pltpu.CompilerParams(vmem_limit_bytes=4 << 20),
        name="add_pieces",
    )(near(kept), *[near(piece) for piece in came])
    return outs[:-1], outs[-1]


def finish_body(pick_ref, kept_ref, first_ref, second_ref, own_ref, offer_ref):
    for band in range(4):
        piece = (first_ref, second_ref)[band // 2]
        columns = slice(band % 2 * BAND, (band % 2 + 1) * BAND)
        total = (kept_ref[band] + piece[:, columns].astype(F32)).astype(BF)
        own_ref[:, band * BAND : (band + 1) * BAND] = total
        offer_ref[:, band * BAND : (band + 1) * BAND] = mm(pick_ref[...], total).astype(BF)


def finish(pick, kept, first, second):
    whole = pl.BlockSpec(memory_space=pltpu.VMEM)
    return pl.pallas_call(
        finish_body,
        in_specs=[whole] * 4,
        out_specs=[whole] * 2,
        out_shape=[
            jax.ShapeDtypeStruct((TOK_DEV, D), BF),
            jax.ShapeDtypeStruct((2 * SPEC, D), BF),
        ],
        compiler_params=pltpu.CompilerParams(vmem_limit_bytes=4 << 20),
        cost_estimate=pl.CostEstimate(flops=4 << 20, bytes_accessed=1 << 20, transcendentals=0),
        name="finish",
    )(near(pick), near(kept), near(first), near(second))


def expert_body(x_ref, in_ref, out_ref, o_hbm, x_s, h_s, o_ref, sems):
    apart = rows_first(lambda r: (r % 128 // 4) * 8 + (r // 128) * 4 + r % 4)
    joined = rows_first(lambda r: (r // 4 % 2) * 128 + (r // 8) * 4 + r % 4)
    for step in range(4):
        block = mm(apart, x_ref[step * 256 : step * 256 + 256, :]).astype(BF)
        x_s[step * 128 : step * 128 + 128, :HALF] = block[:128]
        x_s[step * 128 : step * 128 + 128, HALF:] = block[128:]
    for at in range(0, FFE, 256):
        value = mm(x_s[...], in_ref[0, :, at : at + 256])
        h_s[:, at : at + 256] = (value / (1.0 + jnp.exp(-value))).astype(BF)
    copies = []
    for at in range(0, HALF, 256):
        halves = [
            mm(h_s[...], out_ref[0, :, first + at : first + at + 256]).astype(BF)
            for first in (0, HALF)
        ]
        for step in range(4):
            rows = slice(step * 128, step * 128 + 128)
            both = jnp.concatenate((halves[0][rows], halves[1][rows]), axis=0)
            o_ref[step * 256 : step * 256 + 256, at : at + 256] = mm(joined, both).astype(BF)
        copies.append(
            pltpu.make_async_copy(
                o_ref.at[:, pl.ds(at, 256)], o_hbm.at[:, pl.ds(at, 256)], sems.at[at // 256]
            )
        )
        copies[-1].start()
    for copy in copies:
        copy.wait()


def expert(incoming, expert_in, expert_out):
    whole = pl.BlockSpec(memory_space=pltpu.VMEM)
    return pl.pallas_call(
        expert_body,
        in_specs=[whole, whole, whole],
        out_specs=pl.BlockSpec(memory_space=pltpu.HBM),
        out_shape=pltpu.HBM((DEVICES * 8, HALF), BF),
        scratch_shapes=[
            pltpu.VMEM((512, D), BF),
            pltpu.VMEM((512, FFE), BF),
            pltpu.VMEM((DEVICES * 8, HALF), BF),
            pltpu.SemaphoreType.DMA((7,)),
        ],
        cost_estimate=pl.CostEstimate(
            flops=8 << 30, bytes_accessed=22 << 20, transcendentals=512 * 1024
        ),
        compiler_params=pltpu.CompilerParams(vmem_limit_bytes=24 << 20),
        name="expert",
    )(near(incoming), near(expert_in), near(expert_out))


NEAR = [(0, 1), (1, 0), (2, 3), (3, 2)]
FAR = [(0, 3), (3, 0), (1, 2), (2, 1)]
PAIRS = {1: NEAR, 3: FAR}
ROUTES = (
    (("ep_0", 1), ("ep_0", 3), ("ep_1", 1), ("ep_1", 3)),
    (("ep_0", 3), ("ep_0", 1), ("ep_1", 1), ("ep_1", 3)),
    (("ep_1", 1), ("ep_1", 3), ("ep_0", 1), ("ep_0", 3)),
    (("ep_1", 3), ("ep_1", 1), ("ep_0", 1), ("ep_0", 3)),
)


def block_order():
    first, second = [], []
    for route in ROUTES:
        places = [(0, 0)]
        for axis, flip in reversed(route):
            turn = (flip, 0) if axis == "ep_0" else (0, flip)
            places = places + [(a ^ turn[0], b ^ turn[1]) for a, b in places]
        first += [a for a, _ in places]
        second += [b for _, b in places]
    mine = lax.axis_index("ep_0"), lax.axis_index("ep_1")
    return (jnp.array(first, jnp.int32) ^ mine[0]) * 4 + (jnp.array(second, jnp.int32) ^ mine[1])


def exchange(pieces, step):
    every = 4 // len(pieces)
    out = []
    for at, piece in enumerate(pieces):
        axis, flip = ROUTES[at * every][step]
        out.append(lax.ppermute(piece, axis, PAIRS[flip]))
    return out


def sum_over_columns(pick, parts):
    *send, kept = parts
    for step in range(3):
        send, kept = add_pieces(kept, exchange(send, step), joined=step > 0)
    return finish(pick, kept, *exchange(send, 3))


def shifted(value, axis, steps):
    count = lax.axis_size(axis)
    return lax.ppermute(value, axis, [(s, (s + steps) % count) for s in range(count)])


def from_replicas(value):
    return jnp.concatenate([shifted(value, "rep", back) for back in range(1, 8)], axis=0)


def per_device(
    latent_pages,
    queries,
    residual,
    page_count,
    last_fill,
    page_order,
    shed_slots,
    shed_shift,
    expert_ids,
    gate_weight,
    expert_home,
    norm_gain,
    value_up,
    out_weight,
    expert_in,
    expert_out,
):
    replica = lax.axis_index("rep")
    latent = attention(page_order, page_count, last_fill, queries, latent_pages)
    latent = lax.all_to_all(latent, EP, split_axis=0, concat_axis=0, tiled=True)
    tokens = jnp.arange(TOK_DEV, dtype=jnp.int32)
    own_sheds = shed_slots[replica, 0, :]
    shed_rows = (own_sheds[:, None] * SPEC + jnp.arange(SPEC, dtype=jnp.int32)).reshape(-1)
    pick = shed_rows[:, None] == tokens[None, :]
    present = jnp.any(pick, axis=0)[:, None]
    wanted = jnp.arange(1, 8, dtype=jnp.int32)[:, None] == jnp.repeat(shed_shift[0], SPEC)[None, :]
    place = (wanted[:, :, None] & pick[None, :, :]).reshape(7 * 2 * SPEC, TOK_DEV).astype(BF)
    pick = pick.astype(BF)

    def served(own, came):
        taken = lax.dot_general(place, came, (((0,), (0,)), ((), ())), preferred_element_type=F32)
        return jnp.where(present, taken.astype(BF), own)

    own_residual = residual.reshape(TOK_DEV, D)
    came = from_replicas(mm(pick, own_residual).astype(BF))
    served_residual = served(own_residual, came)
    own_branch, offer = sum_over_columns(
        pick, project(block_order(), latent.reshape(8, 256, LAT), value_up, out_weight)
    )
    served_branch = served(own_branch, from_replicas(offer))
    mixed = served_residual.astype(F32) + served_branch.astype(F32)
    square = jnp.mean(mixed * mixed, axis=1, keepdims=True)
    normed = (mixed * lax.rsqrt(square + NORM_EPS) * norm_gain).astype(BF)

    target = expert_home[expert_ids.reshape(-1)]
    hits = (target[:, None] == jnp.arange(DEVICES, dtype=jnp.int32)[None, :]).astype(jnp.int32)
    before = jnp.sum((jnp.cumsum(hits, axis=0) - hits) * hits, axis=1)
    slot = (target * CAP + before).reshape(TOK_DEV, TOP)
    row = jnp.arange(DEVICES * 8, dtype=jnp.int32)
    row_slot = row // 8 * CAP + row % CAP
    row_half = row // CAP % 2
    both = jnp.arange(2 * TOK_DEV, dtype=jnp.int32)
    same_half = row_half[None, :] == (both // TOK_DEV)[:, None]
    landing = slot[:, :, None] == row_slot[None, None, :]
    chosen = jnp.any(landing, axis=1)
    chooser = (jnp.concatenate((chosen, chosen)) & same_half).astype(BF)
    gates = jnp.sum(jnp.where(landing, gate_weight[:, :, None], 0.0), axis=1)
    gates = jnp.where(same_half, jnp.concatenate((gates, gates)), 0.0)
    coarse = lax.reduce_precision(gates, 8, 7)
    gates = jnp.concatenate((coarse.astype(BF), (gates - coarse).astype(BF)))

    def halves(value):
        return jnp.concatenate((value[:, :HALF], value[:, HALF:]), axis=0)

    outgoing = lax.dot_general(
        chooser, halves(normed), (((0,), (0,)), ((), ())), preferred_element_type=F32
    ).astype(BF)
    incoming = lax.all_to_all(outgoing, REP_EP, split_axis=0, concat_axis=0, tiled=True)
    outer = expert(incoming, expert_in, expert_out)
    returned = lax.all_to_all(outer, REP_EP, split_axis=0, concat_axis=0, tiled=True)
    moe = mm(gates, returned)
    layer = (halves(mixed) + moe[: 2 * TOK_DEV] + moe[2 * TOK_DEV :]).astype(BF)
    layer_out = jnp.concatenate((layer[:TOK_DEV], layer[TOK_DEV:]), axis=1)
    return (
        served_branch.reshape(REQ_DEV, SPEC * D),
        layer_out.reshape(REQ_DEV, SPEC * D),
    )


def solution(mesh):
    torus = Mesh(mesh.devices.reshape(mesh.shape["rep"], 4, 4), ("rep", "ep_0", "ep_1"))

    return jax.shard_map(
        per_device,
        mesh=torus,
        in_specs=(
            P(REP_EP, None),
            P(REP_EP, None),
            P(REP_EP, None),
            P(None, EP, None),
            P(None, EP, None),
            P(REP_EP, None),
            P(None, EP, None),
            P(EP, None),
            P(REP_EP, None),
            P(REP_EP, None),
            P(),
            P(),
            P(EP, None, None),
            P(EP, None),
            P(REP_EP, None, None),
            P(REP_EP, None, None),
        ),
        out_specs=(P(REP_EP, None), P(REP_EP, None)),
        check_vma=False,
    )
```

profile of v0, /device:TPU:1, one launch (start us, length us, event | category | flops | bytes accessed | tf_op | source)
XLA Modules:
  0.0 246.7 jit_solution(3118818323717602794)
XLA Ops:
  0.7 0.9 multiply_reduce_fusion.1
  1.6 0.1 add.122
  1.7 1.1 reshape.229
  2.8 0.2 convolution_convert_fusion.2
  3.0 3.0 %collective-permute-start.19 = (bf16[8,3584]{1,0:T(8,128)(2,1)S(1)}, bf16[8,3584]{1,0:T(8,128)(2,1)S(1)}, u32[]{:S(2)}, u32[]{:S(2)}) collective-permute-start(bf16[8,3584]{1,0:T(8,128)(2,1)S(1)} %convolution_convert_fusion.2), channel_id=1, source_target_pairs={{0,16},{16,32},{32,48},{48,64},{64,80},{80,96},{96,112},{112,0},{1... | collective-permute-start | bytes 172040 | tf_op jit(solution)/shard_map/ppermute | solution.py:431
  6.1 1.6 collective-permute-start.20
  7.7 2.0 collective-permute-start.21
  9.7 18.0 %attention.1 = bf16[16,128,512]{2,1,0:T(8,128)(2,1)} custom-call(s32[1,48]{1,0:T(1,128)} %pick_ref.1, s32[8,1,8]{2,1,0:T(1,128)} %count_ref.1, s32[8,1,8]{2,1,0:T(1,128)} %fill_ref.1, bf16[8,147456]{1,0:T(8,128)(2,1)} %query_hbm.1, bf16[48,36864]{1,0:T(8,128)(2,1)} %page_hbm.1), custom_call_target="tpu_custom_call" | custom-call | flops 7516192768 | bytes 8388608 | tf_op jit(solution)/shard_map/attention/pallas_call | solution.py:156
  27.8 6.8 %all-to-all-start = ((bf16[16,128,512]{2,1,0:T(8,128)(2,1)}), bf16[16,128,512]{2,1,0:T(8,128)(2,1)S(1)}, u32[]{:S(2)}, u32[]{:S(2)}) async-start(bf16[16,128,512]{2,1,0:T(8,128)(2,1)} %attention.1), calls=%async_computation | async-start | bytes 4194304 | tf_op jit(solution)/shard_map/all_to_all | solution.py:458
  34.7 0.1 eq.103
  34.8 0.1 eq.105
  34.9 0.1 eq.102
  35.1 0.1 reshape.230
  35.2 1.9 gather_fusion
  37.1 0.1 copy.26
  37.2 0.2 fusion.19
  37.5 0.2 fusion.21
  37.8 0.4 compare_reduce_fusion
  38.3 0.1 iota_compare_fusion.1
  38.4 22.5 %all-to-all-done = bf16[16,128,512]{2,1,0:T(8,128)(2,1)S(1)} async-done(((bf16[16,128,512]{2,1,0:T(8,128)(2,1)}), bf16[16,128,512]{2,1,0:T(8,128)(2,1)S(1)}, u32[]{:S(2)}, u32[]{:S(2)}) %all-to-all-start) | async-done | bytes 2097184 | tf_op jit(solution)/shard_map/all_to_all | solution.py:458
  60.9 5.5 %project_sent.1 = (bf16[256,896]{1,0:T(8,128)(2,1)}, bf16[256,896]{1,0:T(8,128)(2,1)}, bf16[256,896]{1,0:T(8,128)(2,1)}, bf16[256,896]{1,0:T(8,128)(2,1)}, bf16[16,32,512]{2,1,0:T(8,128)(2,1)S(1)}) custom-call(s32[64]{0:T(128)S(1)} %xor_add_fusion.order_ref, bf16[8,256,512]{2,1,0:T(8,128)(2,1)S(1)} %bitcast.36, bf16[4,512,128]{2,1,0:T(8,128)(2,1)} %up_hbm.1, ...), custom_call_target="tpu_custom_call" | custom-call | flops 2147483648 | bytes 8388608 | tf_op jit(solution)/shard_map/project_sent/pallas_call | solution.py:241
  66.4 0.1 collective-permute-start
  66.5 2.1 collective-permute-start.1
  68.6 0.3 collective-permute-start.2
  68.9 2.5 %collective-permute-start.3 = (bf16[256,896]{1,0:T(8,128)(2,1)}, bf16[256,896]{1,0:T(8,128)(2,1)S(1)}, u32[]{:S(2)}, u32[]{:S(2)}) collective-permute-start(bf16[256,896]{1,0:T(8,128)(2,1)} %get-tuple-element.24), channel_id=1, source_target_pairs={{0,3},{3,0},{1,2},{2,1},{4,7},{7,4},{5,6},{6,5},{8,11},{11,8},{9,1... | collective-permute-start | bytes 1376264 | tf_op jit(solution)/shard_map/ppermute | solution.py:418
  71.4 3.6 %project_kept.1.kept_ref = bf16[4,256,896]{2,1,0:T(8,128)(2,1)S(1)} custom-call(s32[64]{0:T(128)S(1)} %xor_add_fusion.order_ref, bf16[16,32,512]{2,1,0:T(8,128)(2,1)S(1)} %get-tuple-element.20.lifted_ref, bf16[512,3584]{1,0:T(8,128)(2,1)} %weight_hbm.3), custom_call_target="tpu_custom_call" | custom-call | flops 1073741824 | bytes 6291456 | tf_op jit(solution)/shard_map/project_kept/pallas_call | solution.py:261
  75.0 8.1 %collective-permute-start.23 = (bf16[8,3584]{1,0:T(8,128)(2,1)S(1)}, bf16[8,3584]{1,0:T(8,128)(2,1)S(1)}, u32[]{:S(2)}, u32[]{:S(2)}) collective-permute-start(bf16[8,3584]{1,0:T(8,128)(2,1)S(1)} %convolution_convert_fusion.2), channel_id=1, source_target_pairs={{0,80},{16,96},{32,112},{48,0},{64,16},{80,32},{96,48},{112,64},{1... | collective-permute-start | bytes 172040 | tf_op jit(solution)/shard_map/ppermute | solution.py:431
  83.1 0.4 add_pieces.3
  83.5 0.3 collective-permute-start.4
  83.9 1.5 collective-permute-start.6
  85.3 0.3 collective-permute-start.7
  85.6 5.7 %collective-permute-done.4.rest_0_ = bf16[128,896]{1,0:T(8,128)(2,1)S(1)} collective-permute-done((bf16[128,896]{1,0:T(8,128)(2,1)S(1)}, bf16[128,896]{1,0:T(8,128)(2,1)S(1)}, u32[]{:S(2)}, u32[]{:S(2)}) %collective-permute-start.4) | collective-permute-done | bytes 229408 | tf_op jit(solution)/shard_map/ppermute | solution.py:418
  91.4 3.4 %collective-permute-start.24 = (bf16[8,3584]{1,0:T(8,128)(2,1)S(1)}, bf16[8,3584]{1,0:T(8,128)(2,1)S(1)}, u32[]{:S(2)}, u32[]{:S(2)}) collective-permute-start(bf16[8,3584]{1,0:T(8,128)(2,1)S(1)} %convolution_convert_fusion.2), channel_id=1, source_target_pairs={{0,96},{16,112},{32,0},{48,16},{64,32},{80,48},{96,64},{112,80},{1... | collective-permute-start | bytes 172040 | tf_op jit(solution)/shard_map/ppermute | solution.py:431
  94.8 0.9 collective-permute-start.25
  95.7 0.1 add_pieces.4
  95.9 0.1 collective-permute-start.8
  96.1 7.0 %collective-permute-done.8.rest_0_ = bf16[64,1792]{1,0:T(8,128)(2,1)S(1)} collective-permute-done((bf16[64,1792]{1,0:T(8,128)(2,1)S(1)}, bf16[64,1792]{1,0:T(8,128)(2,1)S(1)}, u32[]{:S(2)}, u32[]{:S(2)}) %collective-permute-start.8) | collective-permute-done | bytes 229408 | tf_op jit(solution)/shard_map/ppermute | solution.py:418
  103.2 2.3 collective-permute-start.10
  105.5 1.2 collective-permute-start.11
  106.7 1.5 collective-permute-done.10.first_ref
  108.1 2.2 collective-permute-done.11.second_ref
  110.3 0.2 finish.1
  110.5 1.2 collective-permute-start.12
  111.7 2.5 %collective-permute-start.13 = (bf16[8,3584]{1,0:T(8,128)(2,1)S(1)}, bf16[8,3584]{1,0:T(8,128)(2,1)S(1)}, u32[]{:S(2)}, u32[]{:S(2)}) collective-permute-start(bf16[8,3584]{1,0:T(8,128)(2,1)S(1)} %get-tuple-element.36), channel_id=1, source_target_pairs={{0,32},{16,48},{32,64},{48,80},{64,96},{80,112},{96,0},{112,16},{1... | collective-permute-start | bytes 172040 | tf_op jit(solution)/shard_map/ppermute | solution.py:431
  114.3 2.4 collective-permute-start.14
  116.7 2.6 %collective-permute-start.16 = (bf16[8,3584]{1,0:T(8,128)(2,1)S(1)}, bf16[8,3584]{1,0:T(8,128)(2,1)S(1)}, u32[]{:S(2)}, u32[]{:S(2)}) collective-permute-start(bf16[8,3584]{1,0:T(8,128)(2,1)S(1)} %get-tuple-element.36), channel_id=1, source_target_pairs={{0,80},{16,96},{32,112},{48,0},{64,16},{80,32},{96,48},{112,64},{1... | collective-permute-start | bytes 172040 | tf_op jit(solution)/shard_map/ppermute | solution.py:431
  119.3 0.5 collective-permute-start.17
  119.8 0.8 collective-permute-start.18
  120.7 1.2 collective-permute-done.15
  121.9 0.5 collective-permute-done.16
  122.4 1.7 collective-permute-done.18
  124.1 0.3 fusion
  124.4 0.5 multiply_reduce_fusion
  124.9 0.1 multiply_convert_fusion
  125.1 1.2 fusion.6
  126.3 53.9 %all_to_all.28 = bf16[128,8,1792]{2,1,0:T(8,128)(2,1)S(1)} all-to-all(bf16[128,8,1792]{2,1,0:T(8,128)(2,1)S(1)} %fusion.6), channel_id=1, replica_groups=mesh['rep'=8,'ep_0'=4,'ep_1'=4] {'rep','ep_0','ep_1'}, dimensions={0} | all-to-all | bytes 7340032 | tf_op jit(solution)/shard_map/all_to_all | solution.py:506
  180.3 11.2 %expert.1 = bf16[1024,1792]{1,0:T(8,128)(2,1)} custom-call(bf16[1024,1792]{1,0:T(8,128)(2,1)S(1)} %bitcast.35, bf16[1,3584,1024]{2,1,0:T(8,128)(2,1)S(1)} %bitcast.38, bf16[1,1024,3584]{2,1,0:T(8,128)(2,1)S(1)} %bitcast.40), custom_call_target="tpu_custom_call" | custom-call | flops 8589934592 | bytes 23068672 | tf_op jit(solution)/shard_map/expert/pallas_call | solution.py:370
  191.6 4.7 %all-to-all-start.2 = ((bf16[128,8,1792]{2,1,0:T(8,128)(2,1)}), bf16[128,8,1792]{2,1,0:T(8,128)(2,1)}, u32[]{:S(2)}, u32[]{:S(2)}) async-start(bf16[128,8,1792]{2,1,0:T(8,128)(2,1)} %bitcast.41), calls=%async_computation.2 | async-start | bytes 7340032 | tf_op jit(solution)/shard_map/all_to_all | solution.py:508
  196.4 0.4 fusion.7
  196.8 0.1 reduce-precision_convert_fusion
  196.9 0.9 reshape.228
  197.8 45.2 %all-to-all-done.2 = bf16[128,8,1792]{2,1,0:T(8,128)(2,1)} async-done(((bf16[128,8,1792]{2,1,0:T(8,128)(2,1)}), bf16[128,8,1792]{2,1,0:T(8,128)(2,1)}, u32[]{:S(2)}, u32[]{:S(2)}) %all-to-all-start.2) | async-done | bytes 3670048 | tf_op jit(solution)/shard_map/all_to_all | solution.py:508
  243.0 2.7 %fusion.4 = f32[128,1792]{1,0:T(8,128)S(1)} fusion(bf16[128,8,1792]{2,1,0:T(8,128)(2,1)} %all-to-all-done.2, bf16[64,1024]{1,0:T(8,128)(2,1)S(1)} %get-tuple-element.45, bf16[64,1024]{1,0:T(8,128)(2,1)S(1)} %get-tuple-element.44), kind=kOutput, calls=%fused_computation.9 | convolution fusion | flops 470286336 | bytes 4849664 | tf_op jit(solution)/shard_map/dot_general | solution.py:48
  245.8 0.9 reshape.232
  (90 shorter events, 1.2 us)
Async XLA Ops:
  0.6 34.6 %copy-start = (s32[128]{0:T(128)S(1)}, s32[128]{0:T(128)}, u32[]{:S(2)}) copy-start(s32[128]{0:T(128)} %param.28) | copy-start | bytes 1540
  3.0 35.3 %collective-permute-start.19 = (bf16[8,3584]{1,0:T(8,128)(2,1)S(1)}, bf16[8,3584]{1,0:T(8,128)(2,1)S(1)}, u32[]{:S(2)}, u32[]{:S(2)}) collective-permute-start(bf16[8,3584]{1,0:T(8,128)(2,1)S(1)} %convolution_convert_fusion.2), channel_id=1, source_target_pairs={{0,16},{16,32},{32,48},{48,64},{64,80},{80,96},{96,112},{112,0},{1... | collective-permute-start | bytes 172040 | tf_op jit(solution)/shard_map/ppermute | solution.py:431
  6.1 32.3 %collective-permute-start.20 = (bf16[8,3584]{1,0:T(8,128)(2,1)S(1)}, bf16[8,3584]{1,0:T(8,128)(2,1)S(1)}, u32[]{:S(2)}, u32[]{:S(2)}) collective-permute-start(bf16[8,3584]{1,0:T(8,128)(2,1)S(1)} %convolution_convert_fusion.2), channel_id=1, source_target_pairs={{0,32},{16,48},{32,64},{48,80},{64,96},{80,112},{96,0},{112,16},{1... | collective-permute-start | bytes 172040 | tf_op jit(solution)/shard_map/ppermute | solution.py:431
  7.7 61.2 %collective-permute-start.21 = (bf16[8,3584]{1,0:T(8,128)(2,1)S(1)}, bf16[8,3584]{1,0:T(8,128)(2,1)S(1)}, u32[]{:S(2)}, u32[]{:S(2)}) collective-permute-start(bf16[8,3584]{1,0:T(8,128)(2,1)S(1)} %convolution_convert_fusion.2), channel_id=1, source_target_pairs={{0,48},{16,64},{32,80},{48,96},{64,112},{80,0},{96,16},{112,32},{1... | collective-permute-start | bytes 172040 | tf_op jit(solution)/shard_map/ppermute | solution.py:431
  9.7 75.6 %collective-permute-start.22 = (bf16[8,3584]{1,0:T(8,128)(2,1)S(1)}, bf16[8,3584]{1,0:T(8,128)(2,1)S(1)}, u32[]{:S(2)}, u32[]{:S(2)}) collective-permute-start(bf16[8,3584]{1,0:T(8,128)(2,1)S(1)} %convolution_convert_fusion.2), channel_id=1, source_target_pairs={{0,64},{16,80},{32,96},{48,112},{64,0},{80,16},{96,32},{112,48},{1... | collective-permute-start | bytes 172040 | tf_op jit(solution)/shard_map/ppermute | solution.py:431
  27.7 6.9 %copy-start.6 = (s32[1,2]{1,0:T(1,128)S(1)}, s32[1,2]{1,0:T(1,128)}, u32[]{:S(2)}) copy-start(s32[1,2]{1,0:T(1,128)} %param.25) | copy-start | bytes 28
  27.7 7.3 %copy-start.2 = (s32[32,8]{0,1:T(8,128)S(1)}, s32[32,8]{0,1:T(8,128)}, u32[]{:S(2)}) copy-start(s32[32,8]{0,1:T(8,128)} %param.26) | copy-start | bytes 3076
  27.8 10.5 %copy-start.4 = (s32[64]{0:T(128)S(1)}, s32[64]{0:T(128)}, u32[]{:S(2)}) copy-start(s32[64]{0:T(128)} %constant.107.clone) | copy-start | bytes 772
  27.8 10.5 %copy-start.5 = (s32[64]{0:T(128)S(1)}, s32[64]{0:T(128)}, u32[]{:S(2)}) copy-start(s32[64]{0:T(128)} %constant.108.clone) | copy-start | bytes 772
  27.8 33.1 %all-to-all-start = ((bf16[16,128,512]{2,1,0:T(8,128)(2,1)}), bf16[16,128,512]{2,1,0:T(8,128)(2,1)S(1)}, u32[]{:S(2)}, u32[]{:S(2)}) async-start(bf16[16,128,512]{2,1,0:T(8,128)(2,1)} %attention.1), calls=%async_computation | async-start | bytes 4194304 | tf_op jit(solution)/shard_map/all_to_all | solution.py:458
  66.4 8.5 %collective-permute-start = (bf16[256,896]{1,0:T(8,128)(2,1)}, bf16[256,896]{1,0:T(8,128)(2,1)S(1)}, u32[]{:S(2)}, u32[]{:S(2)}) collective-permute-start(bf16[256,896]{1,0:T(8,128)(2,1)} %get-tuple-element.21), channel_id=1, source_target_pairs={{0,4},{4,0},{8,12},{12,8},{1,5},{5,1},{9,13},{13,9},{2,6},{6,2},{1... | collective-permute-start | bytes 1376264 | tf_op jit(solution)/shard_map/ppermute | solution.py:418
  66.5 16.6 %collective-permute-start.1 = (bf16[256,896]{1,0:T(8,128)(2,1)}, bf16[256,896]{1,0:T(8,128)(2,1)S(1)}, u32[]{:S(2)}, u32[]{:S(2)}) collective-permute-start(bf16[256,896]{1,0:T(8,128)(2,1)} %get-tuple-element.22), channel_id=1, source_target_pairs={{0,12},{12,0},{4,8},{8,4},{1,13},{13,1},{5,9},{9,5},{2,14},{14,2},... | collective-permute-start | bytes 1376264 | tf_op jit(solution)/shard_map/ppermute | solution.py:418
  68.6 14.5 %collective-permute-start.2 = (bf16[256,896]{1,0:T(8,128)(2,1)}, bf16[256,896]{1,0:T(8,128)(2,1)S(1)}, u32[]{:S(2)}, u32[]{:S(2)}) collective-permute-start(bf16[256,896]{1,0:T(8,128)(2,1)} %get-tuple-element.23), channel_id=1, source_target_pairs={{0,1},{1,0},{2,3},{3,2},{4,5},{5,4},{6,7},{7,6},{8,9},{9,8},{10,11... | collective-permute-start | bytes 1376264 | tf_op jit(solution)/shard_map/ppermute | solution.py:418
  68.9 14.2 %collective-permute-start.3 = (bf16[256,896]{1,0:T(8,128)(2,1)}, bf16[256,896]{1,0:T(8,128)(2,1)S(1)}, u32[]{:S(2)}, u32[]{:S(2)}) collective-permute-start(bf16[256,896]{1,0:T(8,128)(2,1)} %get-tuple-element.24), channel_id=1, source_target_pairs={{0,3},{3,0},{1,2},{2,1},{4,7},{7,4},{5,6},{6,5},{8,11},{11,8},{9,1... | collective-permute-start | bytes 1376264 | tf_op jit(solution)/shard_map/ppermute | solution.py:418
  75.0 21.1 %collective-permute-start.23 = (bf16[8,3584]{1,0:T(8,128)(2,1)S(1)}, bf16[8,3584]{1,0:T(8,128)(2,1)S(1)}, u32[]{:S(2)}, u32[]{:S(2)}) collective-permute-start(bf16[8,3584]{1,0:T(8,128)(2,1)S(1)} %convolution_convert_fusion.2), channel_id=1, source_target_pairs={{0,80},{16,96},{32,112},{48,0},{64,16},{80,32},{96,48},{112,64},{1... | collective-permute-start | bytes 172040 | tf_op jit(solution)/shard_map/ppermute | solution.py:431
  83.5 7.8 %collective-permute-start.4 = (bf16[128,896]{1,0:T(8,128)(2,1)S(1)}, bf16[128,896]{1,0:T(8,128)(2,1)S(1)}, u32[]{:S(2)}, u32[]{:S(2)}) collective-permute-start(bf16[128,896]{1,0:T(8,128)(2,1)S(1)} %get-tuple-element.26), channel_id=1, source_target_pairs={{0,12},{12,0},{4,8},{8,4},{1,13},{13,1},{5,9},{9,5},{2,14},{14,2},... | collective-permute-start | bytes 688136 | tf_op jit(solution)/shard_map/ppermute | solution.py:418
  83.8 10.9 %collective-permute-start.5 = (bf16[128,896]{1,0:T(8,128)(2,1)S(1)}, bf16[128,896]{1,0:T(8,128)(2,1)S(1)}, u32[]{:S(2)}, u32[]{:S(2)}) collective-permute-start(bf16[128,896]{1,0:T(8,128)(2,1)S(1)} %get-tuple-element.27), channel_id=1, source_target_pairs={{0,4},{4,0},{8,12},{12,8},{1,5},{5,1},{9,13},{13,9},{2,6},{6,2},{1... | collective-permute-start | bytes 688136 | tf_op jit(solution)/shard_map/ppermute | solution.py:418
  83.9 11.9 %collective-permute-start.6 = (bf16[128,896]{1,0:T(8,128)(2,1)S(1)}, bf16[128,896]{1,0:T(8,128)(2,1)S(1)}, u32[]{:S(2)}, u32[]{:S(2)}) collective-permute-start(bf16[128,896]{1,0:T(8,128)(2,1)S(1)} %get-tuple-element.28), channel_id=1, source_target_pairs={{0,3},{3,0},{1,2},{2,1},{4,7},{7,4},{5,6},{6,5},{8,11},{11,8},{9,1... | collective-permute-start | bytes 688136 | tf_op jit(solution)/shard_map/ppermute | solution.py:418
  85.3 10.4 %collective-permute-start.7 = (bf16[128,896]{1,0:T(8,128)(2,1)S(1)}, bf16[128,896]{1,0:T(8,128)(2,1)S(1)}, u32[]{:S(2)}, u32[]{:S(2)}) collective-permute-start(bf16[128,896]{1,0:T(8,128)(2,1)S(1)} %get-tuple-element.29), channel_id=1, source_target_pairs={{0,1},{1,0},{2,3},{3,2},{4,5},{5,4},{6,7},{7,6},{8,9},{9,8},{10,11... | collective-permute-start | bytes 688136 | tf_op jit(solution)/shard_map/ppermute | solution.py:418
  91.4 15.3 %collective-permute-start.24 = (bf16[8,3584]{1,0:T(8,128)(2,1)S(1)}, bf16[8,3584]{1,0:T(8,128)(2,1)S(1)}, u32[]{:S(2)}, u32[]{:S(2)}) collective-permute-start(bf16[8,3584]{1,0:T(8,128)(2,1)S(1)} %convolution_convert_fusion.2), channel_id=1, source_target_pairs={{0,96},{16,112},{32,0},{48,16},{64,32},{80,48},{96,64},{112,80},{1... | collective-permute-start | bytes 172040 | tf_op jit(solution)/shard_map/ppermute | solution.py:431
  94.8 17.0 %collective-permute-start.25 = (bf16[8,3584]{1,0:T(8,128)(2,1)S(1)}, bf16[8,3584]{1,0:T(8,128)(2,1)S(1)}, u32[]{:S(2)}, u32[]{:S(2)}) collective-permute-start(bf16[8,3584]{1,0:T(8,128)(2,1)S(1)} %convolution_convert_fusion.2), channel_id=1, source_target_pairs={{0,112},{16,0},{32,16},{48,32},{64,48},{80,64},{96,80},{112,96},{1... | collective-permute-start | bytes 172040 | tf_op jit(solution)/shard_map/ppermute | solution.py:431
  95.7 29.2 %copy-start.1 = (f32[3584]{0:T(1024)S(1)}, f32[3584]{0:T(1024)}, u32[]{:S(2)}) copy-start(f32[3584]{0:T(1024)} %param.29) | copy-start | bytes 43012
  95.7 84.6 %slice-start.2 = ((s8[7340032]{0:T(1024)(128)(4,1)}), s8[4194304]{0:T(1024)(128)(4,1)S(1)}, s32[]{:S(2)}) async-start(s8[7340032]{0:T(1024)(128)(4,1)} %bitcast.39), calls=%async_computation.5 | async-start | bytes 8388608
  95.9 7.2 %collective-permute-start.8 = (bf16[64,1792]{1,0:T(8,128)(2,1)S(1)}, bf16[64,1792]{1,0:T(8,128)(2,1)S(1)}, u32[]{:S(2)}, u32[]{:S(2)}) collective-permute-start(bf16[64,1792]{1,0:T(8,128)(2,1)S(1)} %get-tuple-element.31), channel_id=1, source_target_pairs={{0,1},{1,0},{2,3},{3,2},{4,5},{5,4},{6,7},{7,6},{8,9},{9,8},{10,11... | collective-permute-start | bytes 688136 | tf_op jit(solution)/shard_map/ppermute | solution.py:418
  96.0 7.1 %collective-permute-start.9 = (bf16[64,1792]{1,0:T(8,128)(2,1)S(1)}, bf16[64,1792]{1,0:T(8,128)(2,1)S(1)}, u32[]{:S(2)}, u32[]{:S(2)}) collective-permute-start(bf16[64,1792]{1,0:T(8,128)(2,1)S(1)} %get-tuple-element.32), channel_id=1, source_target_pairs={{0,4},{4,0},{8,12},{12,8},{1,5},{5,1},{9,13},{13,9},{2,6},{6,2},{1... | collective-permute-start | bytes 688136 | tf_op jit(solution)/shard_map/ppermute | solution.py:418
  103.2 4.9 %collective-permute-start.10 = (bf16[32,1792]{1,0:T(8,128)(2,1)S(1)}, bf16[32,1792]{1,0:T(8,128)(2,1)S(1)}, u32[]{:S(2)}, u32[]{:S(2)}) collective-permute-start(bf16[32,1792]{1,0:T(8,128)(2,1)S(1)} %get-tuple-element.34), channel_id=1, source_target_pairs={{0,3},{3,0},{1,2},{2,1},{4,7},{7,4},{5,6},{6,5},{8,11},{11,8},{9,1... | collective-permute-start | bytes 344072 | tf_op jit(solution)/shard_map/ppermute | solution.py:418
  105.5 4.9 %collective-permute-start.11 = (bf16[32,1792]{1,0:T(8,128)(2,1)S(1)}, bf16[32,1792]{1,0:T(8,128)(2,1)S(1)}, u32[]{:S(2)}, u32[]{:S(2)}) collective-permute-start(bf16[32,1792]{1,0:T(8,128)(2,1)S(1)} %get-tuple-element.35), channel_id=1, source_target_pairs={{0,12},{12,0},{4,8},{8,4},{1,13},{13,1},{5,9},{9,5},{2,14},{14,2},... | collective-permute-start | bytes 344072 | tf_op jit(solution)/shard_map/ppermute | solution.py:418
  110.5 8.8 %collective-permute-start.12 = (bf16[8,3584]{1,0:T(8,128)(2,1)S(1)}, bf16[8,3584]{1,0:T(8,128)(2,1)S(1)}, u32[]{:S(2)}, u32[]{:S(2)}) collective-permute-start(bf16[8,3584]{1,0:T(8,128)(2,1)S(1)} %get-tuple-element.36), channel_id=1, source_target_pairs={{0,16},{16,32},{32,48},{48,64},{64,80},{80,96},{96,112},{112,0},{1... | collective-permute-start | bytes 172040 | tf_op jit(solution)/shard_map/ppermute | solution.py:431
  111.7 8.1 %collective-permute-start.13 = (bf16[8,3584]{1,0:T(8,128)(2,1)S(1)}, bf16[8,3584]{1,0:T(8,128)(2,1)S(1)}, u32[]{:S(2)}, u32[]{:S(2)}) collective-permute-start(bf16[8,3584]{1,0:T(8,128)(2,1)S(1)} %get-tuple-element.36), channel_id=1, source_target_pairs={{0,32},{16,48},{32,64},{48,80},{64,96},{80,112},{96,0},{112,16},{1... | collective-permute-start | bytes 172040 | tf_op jit(solution)/shard_map/ppermute | solution.py:431
  114.3 6.4 %collective-permute-start.14 = (bf16[8,3584]{1,0:T(8,128)(2,1)S(1)}, bf16[8,3584]{1,0:T(8,128)(2,1)S(1)}, u32[]{:S(2)}, u32[]{:S(2)}) collective-permute-start(bf16[8,3584]{1,0:T(8,128)(2,1)S(1)} %get-tuple-element.36), channel_id=1, source_target_pairs={{0,48},{16,64},{32,80},{48,96},{64,112},{80,0},{96,16},{112,32},{1... | collective-permute-start | bytes 172040 | tf_op jit(solution)/shard_map/ppermute | solution.py:431
  116.6 5.2 %collective-permute-start.15 = (bf16[8,3584]{1,0:T(8,128)(2,1)S(1)}, bf16[8,3584]{1,0:T(8,128)(2,1)S(1)}, u32[]{:S(2)}, u32[]{:S(2)}) collective-permute-start(bf16[8,3584]{1,0:T(8,128)(2,1)S(1)} %get-tuple-element.36), channel_id=1, source_target_pairs={{0,64},{16,80},{32,96},{48,112},{64,0},{80,16},{96,32},{112,48},{1... | collective-permute-start | bytes 172040 | tf_op jit(solution)/shard_map/ppermute | solution.py:431
  116.7 5.7 %collective-permute-start.16 = (bf16[8,3584]{1,0:T(8,128)(2,1)S(1)}, bf16[8,3584]{1,0:T(8,128)(2,1)S(1)}, u32[]{:S(2)}, u32[]{:S(2)}) collective-permute-start(bf16[8,3584]{1,0:T(8,128)(2,1)S(1)} %get-tuple-element.36), channel_id=1, source_target_pairs={{0,80},{16,96},{32,112},{48,0},{64,16},{80,32},{96,48},{112,64},{1... | collective-permute-start | bytes 172040 | tf_op jit(solution)/shard_map/ppermute | solution.py:431
  119.3 3.1 %collective-permute-start.17 = (bf16[8,3584]{1,0:T(8,128)(2,1)S(1)}, bf16[8,3584]{1,0:T(8,128)(2,1)S(1)}, u32[]{:S(2)}, u32[]{:S(2)}) collective-permute-start(bf16[8,3584]{1,0:T(8,128)(2,1)S(1)} %get-tuple-element.36), channel_id=1, source_target_pairs={{0,96},{16,112},{32,0},{48,16},{64,32},{80,48},{96,64},{112,80},{1... | collective-permute-start | bytes 172040 | tf_op jit(solution)/shard_map/ppermute | solution.py:431
  119.8 60.5 %slice-start = ((s8[7340032]{0:T(1024)(128)(4,1)}), s8[4194304]{0:T(1024)(128)(4,1)S(1)}, s32[]{:S(2)}) async-start(s8[7340032]{0:T(1024)(128)(4,1)} %bitcast.37), calls=%async_computation.3 | async-start | bytes 8388608
  119.8 4.3 %collective-permute-start.18 = (bf16[8,3584]{1,0:T(8,128)(2,1)S(1)}, bf16[8,3584]{1,0:T(8,128)(2,1)S(1)}, u32[]{:S(2)}, u32[]{:S(2)}) collective-permute-start(bf16[8,3584]{1,0:T(8,128)(2,1)S(1)} %get-tuple-element.36), channel_id=1, source_target_pairs={{0,112},{16,0},{32,16},{48,32},{64,48},{80,64},{96,80},{112,96},{1... | collective-permute-start | bytes 172040 | tf_op jit(solution)/shard_map/ppermute | solution.py:431
  125.1 55.2 %slice-start.1 = ((s8[7340032]{0:T(1024)(128)(4,1)}), s8[3145728]{0:T(1024)(128)(4,1)S(1)}, s32[]{:S(2)}) async-start(s8[7340032]{0:T(1024)(128)(4,1)} %bitcast.37), calls=%async_computation.4 | async-start | bytes 6291456
  125.1 55.2 %slice-start.3 = ((s8[7340032]{0:T(1024)(128)(4,1)}), s8[3145728]{0:T(1024)(128)(4,1)S(1)}, s32[]{:S(2)}) async-start(s8[7340032]{0:T(1024)(128)(4,1)} %bitcast.39), calls=%async_computation.6 | async-start | bytes 6291456
  191.6 4.8 %copy-start.3 = (f32[32,8]{0,1:T(8,128)S(1)}, f32[32,8]{0,1:T(8,128)}, u32[]{:S(2)}) copy-start(f32[32,8]{0,1:T(8,128)} %param.27) | copy-start | bytes 3076
  191.6 51.4 %all-to-all-start.2 = ((bf16[128,8,1792]{2,1,0:T(8,128)(2,1)}), bf16[128,8,1792]{2,1,0:T(8,128)(2,1)}, u32[]{:S(2)}, u32[]{:S(2)}) async-start(bf16[128,8,1792]{2,1,0:T(8,128)(2,1)} %bitcast.41), calls=%async_computation.2 | async-start | bytes 7340032 | tf_op jit(solution)/shard_map/all_to_all | solution.py:508
where the time goes:
time: 247 us
  waiting for transfers between devices  87.5 us (35%)
  blocking collectives  53.9 us (22%)
  starting transfers between devices  51.5 us (21%)
  Pallas kernels  39.1 us (16%)
  local copies, waits for them, and re-layouts  5.93 us (2%)
  matrix products  4.91 us (2%)
  other arithmetic  2.6 us (1%)
    all_to_all x1, blocking collectives, per_device(): lax.all_to_all(outgoing, REP_EP, split_axis=0, concat_axis=0, tiled=True)  53.9 us
    all_to_all x1, waiting for transfers between devices, per_device(): lax.all_to_all(outer, REP_EP, split_axis=0, concat_axis=0, tiled=True)  45.2 us
    ppermute x14, starting transfers between devices, shifted(): lax.ppermute(value, axis, [(s, (s + steps) % count) for s in range(count)])  29.3 us
    all_to_all x1, waiting for transfers between devices, per_device(): latent = lax.all_to_all(latent, EP, split_axis=0, concat_axis=0, tiled=True)  22.5 us
    pallas_call x1, Pallas kernels, attention(): pl.pallas_call(attention_body, in_specs=[few, few, few, far, far], out_sp...  18 us
    ppermute x12, waiting for transfers between devices, exchange(): out.append(lax.ppermute(piece, axis, PAIRS[flip]))  16.4 us
    pallas_call x1, Pallas kernels, expert(): pl.pallas_call(expert_body, in_specs=[whole, whole, whole], out_specs=pl....  11.2 us
    ppermute x12, starting transfers between devices, exchange(): out.append(lax.ppermute(piece, axis, PAIRS[flip]))  10.6 us
  transfers between devices with their start and end apart: 28, of which 9 were waited for; matrix products, arithmetic and copies ran while one was open for 2% of the time, Pallas kernels for 11%

commit v1 on v0

--- a/solution.py
+++ b/solution.py
@@ -56,7 +56,7 @@
     return pltpu.with_memory_space_constraint(value, pltpu.HBM)
 
 
-WINDOW = 12
+WINDOWS = (4, 8, 12, 14)
 SPAN = 8 * KVW
 
 
@@ -85,15 +85,19 @@
     for pair in range(8):
         for position in range(SPEC):
             query_load(position, pair).start()
-    shift = iota2(8, 128, 0) * PAGES_DEV
-    for place in range(PAGES_DEV):
-        order_s[place * 8 : place * 8 + 8, :] = shift + pick_ref[0, place]
-    to_place = (iota2(384, 384, 1) == order_s[:, :1]).astype(BF)
+    row = iota2(8, 128, 0)
+    for place in range(0, PAGES_DEV, 2):
+        page = jnp.where(row < 4, pick_ref[0, place], pick_ref[0, place + 1])
+        order_s[place * 4 : place * 4 + 8, :] = row % 4 * PAGES_DEV + page
+    to_place = (iota2(192, 192, 1) == order_s[:, :1]).astype(BF)
 
     def regroup_keys(group, carry):
         page_load(group).wait()
-        tokens = [page_v[group, :, t * KVW : (t + 1) * KVW] for t in range(8)]
-        key_s[group] = mm(to_place, jnp.concatenate(tokens, axis=0))
+        for part in range(2):
+            tokens = [
+                page_v[group, :, t * KVW : (t + 1) * KVW] for t in range(4 * part, 4 * part + 4)
+            ]
+            key_s[group * 2 + part] = mm(to_place, jnp.concatenate(tokens, axis=0))
         return carry
 
     lax.fori_loop(0, 8, regroup_keys, 0)
@@ -120,21 +124,20 @@
     replica = lax.axis_index("rep")
     rows = SPEC * HEADS
     late = iota2(rows, 1, 0) // HEADS_DEV % SPEC - SPEC + 1
-    key = iota2(1, KEYS, 1)
-    place = key % (WINDOW * 8) // 8
-    token = place * PAGE + key // (WINDOW * 8) * 8 + key % 8
-
-    def request(i, offset):
-        count = count_ref[replica, 0, i]
-        length = (count - 1) * PAGE + fill_ref[replica, 0, i]
-        start = jnp.minimum(offset, PAGES_DEV - WINDOW)
+
+    def attend(i, offset, length, window):
+        start = jnp.minimum(offset // 2 * 2, PAGES_DEV - window)
         skip = offset - start
-        keys = key_s[:, pl.ds(pl.multiple_of(start * 8, 8), WINDOW * 8), :]
-        keys = keys.reshape(KEYS, KVW).astype(BF)
+        span = window * 4
+        keys = key_s[:, pl.ds(pl.multiple_of(start * 4, 8), span), :]
+        keys = keys.reshape(16 * span, KVW).astype(BF)
         scores = lax.dot_general(
             query_s[i], keys, (((1,), (1,)), ((), ())), preferred_element_type=F32
         )
-        at = jnp.where(place < skip, KEYS, token - skip * PAGE)
+        key = iota2(1, 16 * span, 1)
+        place = key % span // 4
+        token = (place - skip) * PAGE + key // span * 4 + key % 4
+        at = jnp.where(place < skip, KEYS, token)
         scores = jnp.where(at < late + length, scores * SCORE_SCALE, -1e30)
         exponent = jnp.exp(scores - jnp.max(scores, axis=1, keepdims=True))
         total = jnp.sum(exponent, axis=1, keepdims=True)
@@ -142,6 +145,15 @@
         out_ref[:, pl.ds(pl.multiple_of(i * 16, 16), 16), :] = latent.astype(BF).reshape(
             N_EP, 16, LAT
         )
+
+    def request(i, offset):
+        count = count_ref[replica, 0, i]
+        length = (count - 1) * PAGE + fill_ref[replica, 0, i]
+        need = count + offset % 2
+        for least, window in zip((0,) + WINDOWS, WINDOWS):
+            pl.when((need > least) & (need <= window))(
+                functools.partial(attend, i, offset, length, window)
+            )
         result_copy(i).start()
         return offset + count
 
@@ -159,8 +171,8 @@
         out_specs=far,
         out_shape=pltpu.HBM((N_EP, REQ_DEV * 16, LAT), BF),
         scratch_shapes=[
-            pltpu.VMEM((8, PAGES_DEV * 8, KVW), F32),
-            pltpu.VMEM((PAGES_DEV * 8, 128), jnp.int32),
+            pltpu.VMEM((16, PAGES_DEV * 4, KVW), F32),
+            pltpu.VMEM((PAGES_DEV * 4, 128), jnp.int32),
             pltpu.VMEM((256, KVW), F32),
             pltpu.VMEM((REQ_DEV, SPEC * HEADS, KVW), BF),
             pltpu.VMEM((8, PAGES_DEV, SPAN), BF),
@@ -205,7 +217,9 @@
     up_load = pltpu.make_async_copy(up_hbm, up_ref, in_sems.at[4])
     up_load.start()
     loads = weight_loads(weight_hbm, weight_ref, in_sems)
-    by_head = rows_first(lambda r: (r % 64) * 4 + r // 64)
+    by_head = rows_first(
+        lambda r: (r // 32 % 2) * 128 + (r % 8) * 16 + (r // 8 % 4) * 4 + r // 64
+    )
     for step in range(8):
         both = mm(by_head, latent_ref[step]).astype(BF)
         for head in range(HEADS_DEV):
@@ -431,8 +445,19 @@
     return lax.ppermute(value, axis, [(s, (s + steps) % count) for s in range(count)])
 
 
-def from_replicas(value):
-    return jnp.concatenate([shifted(value, "rep", back) for back in range(1, 8)], axis=0)
+def from_replicas(value, odd):
+    crossed = lax.ppermute(value, "rep", [(i, i ^ 1) for i in range(8)])
+    value = jnp.where(odd, crossed, value)
+    planes = [shifted(value, "rep", 2 * back) for back in range(1, 4)]
+    return jnp.concatenate([value] + planes, axis=0)
+
+
+def by_position(value):
+    return jnp.concatenate([value[:, s * D : (s + 1) * D] for s in range(SPEC)], axis=0)
+
+
+def by_slot(value):
+    return jnp.concatenate([value[s * REQ_DEV : (s + 1) * REQ_DEV] for s in range(SPEC)], axis=1)
 
 
 def per_device(
@@ -458,29 +483,36 @@
     latent = lax.all_to_all(latent, EP, split_axis=0, concat_axis=0, tiled=True)
     tokens = jnp.arange(TOK_DEV, dtype=jnp.int32)
     own_sheds = shed_slots[replica, 0, :]
-    shed_rows = (own_sheds[:, None] * SPEC + jnp.arange(SPEC, dtype=jnp.int32)).reshape(-1)
+    shed_rows = (jnp.arange(SPEC, dtype=jnp.int32) * REQ_DEV + own_sheds[:, None]).reshape(-1)
     pick = shed_rows[:, None] == tokens[None, :]
     present = jnp.any(pick, axis=0)[:, None]
-    wanted = jnp.arange(1, 8, dtype=jnp.int32)[:, None] == jnp.repeat(shed_shift[0], SPEC)[None, :]
-    place = (wanted[:, :, None] & pick[None, :, :]).reshape(7 * 2 * SPEC, TOK_DEV).astype(BF)
+    row_shifts = jnp.repeat(shed_shift[0], SPEC)
+    odd = (row_shifts % 2 == 1)[:, None]
+    planes = (row_shifts + 1 - replica % 2) // 2 % 4
+    wanted = jnp.arange(4, dtype=jnp.int32)[:, None] == planes[None, :]
+    place = (wanted[:, :, None] & pick[None, :, :]).reshape(4 * 2 * SPEC, TOK_DEV).astype(BF)
     pick = pick.astype(BF)
 
     def served(own, came):
         taken = lax.dot_general(place, came, (((0,), (0,)), ((), ())), preferred_element_type=F32)
         return jnp.where(present, taken.astype(BF), own)
 
-    own_residual = residual.reshape(TOK_DEV, D)
-    came = from_replicas(mm(pick, own_residual).astype(BF))
+    own_residual = by_position(residual)
+    came = from_replicas(mm(pick, own_residual).astype(BF), odd)
     served_residual = served(own_residual, came)
     own_branch, offer = sum_over_columns(
         pick, project(block_order(), latent.reshape(8, 256, LAT), value_up, out_weight)
     )
-    served_branch = served(own_branch, from_replicas(offer))
+    served_branch = served(own_branch, from_replicas(offer, odd))
     mixed = served_residual.astype(F32) + served_branch.astype(F32)
     square = jnp.mean(mixed * mixed, axis=1, keepdims=True)
     normed = (mixed * lax.rsqrt(square + NORM_EPS) * norm_gain).astype(BF)
 
-    target = expert_home[expert_ids.reshape(-1)]
+    def routed(value):
+        return value.reshape(REQ_DEV, SPEC, TOP).transpose(1, 0, 2).reshape(TOK_DEV, TOP)
+
+    gate_weight = routed(gate_weight)
+    target = expert_home[routed(expert_ids).reshape(-1)]
     hits = (target[:, None] == jnp.arange(DEVICES, dtype=jnp.int32)[None, :]).astype(jnp.int32)
     before = jnp.sum((jnp.cumsum(hits, axis=0) - hits) * hits, axis=1)
     slot = (target * CAP + before).reshape(TOK_DEV, TOP)
@@ -509,10 +541,7 @@
     moe = mm(gates, returned)
     layer = (halves(mixed) + moe[: 2 * TOK_DEV] + moe[2 * TOK_DEV :]).astype(BF)
     layer_out = jnp.concatenate((layer[:TOK_DEV], layer[TOK_DEV:]), axis=1)
-    return (
-        served_branch.reshape(REQ_DEV, SPEC * D),
-        layer_out.reshape(REQ_DEV, SPEC * D),
-    )
+    return by_slot(served_branch), by_slot(layer_out)
 
 
 def solution(mesh):

time: 247 us -> 241 us (0.976)
  starting transfers between devices: 51.5 us -> 44.1 us
    ppermute x14 -> x6, starting transfers between devices: 29.3 us -> 10.6 us  [shifted(): lax.ppermute(value, axis, [(s, (s + steps) % count) for s in range(count)])]
    ppermute x0 -> x2, starting transfers between devices: none -> 8.52 us  [from_replicas(): crossed = lax.ppermute(value, 'rep', [(i, i ^ 1) for i in range(8)])]
    unnamed x37 -> x27, local copies, waits for them, and re-layouts: 0.29 us -> 3.31 us
    reshape x4 -> x1, local copies, waits for them, and re-layouts: 3.01 us -> 0.08 us  [per_device(): row_shifts = jnp.repeat(shed_shift[0], SPEC)]
  transfers between devices with their start and end apart: 28 -> 22, of which waited for: 9 -> 14; matrix products, arithmetic and copies ran while one was open for 2% -> 2% of each run, Pallas kernels for 11% -> 4%
where the time goes in v1:
time: 241 us
  waiting for transfers between devices  89.8 us (37%)
  blocking collectives  54.9 us (23%)
  starting transfers between devices  44.1 us (18%)
  Pallas kernels  37.2 us (15%)
  local copies, waits for them, and re-layouts  6.19 us (3%)
  matrix products  4.9 us (2%)
  other arithmetic  2.64 us (1%)
    all_to_all x1, blocking collectives, per_device(): lax.all_to_all(outgoing, REP_EP, split_axis=0, concat_axis=0, tiled=True)  54.9 us
    all_to_all x1, waiting for transfers between devices, per_device(): lax.all_to_all(outer, REP_EP, split_axis=0, concat_axis=0, tiled=True)  46 us
    all_to_all x1, waiting for transfers between devices, per_device(): latent = lax.all_to_all(latent, EP, split_axis=0, concat_axis=0, tiled=True)  24.1 us
    ppermute x12, waiting for transfers between devices, exchange(): out.append(lax.ppermute(piece, axis, PAIRS[flip]))  16.9 us
    pallas_call x1, Pallas kernels, attention(): pl.pallas_call(attention_body, in_specs=[few, few, few, far, far], out_sp...  16 us
    ppermute x12, starting transfers between devices, exchange(): out.append(lax.ppermute(piece, axis, PAIRS[flip]))  12.3 us
    pallas_call x1, Pallas kernels, expert(): pl.pallas_call(expert_body, in_specs=[whole, whole, whole], out_specs=pl....  11.3 us
    ppermute x6, starting transfers between devices, shifted(): lax.ppermute(value, axis, [(s, (s + steps) % count) for s in range(count)])  10.6 us
  transfers between devices with their start and end apart: 22, of which 14 were waited for; matrix products, arithmetic and copies ran while one was open for 2% of the time, Pallas kernels for 4%

profile of v1, /device:TPU:1, one launch (start us, length us, event | category | flops | bytes accessed | tf_op | source)
XLA Modules:
  0.0 240.8 jit_solution(4025375509847128125)
XLA Ops:
  0.6 16.0 %attention.1 = bf16[16,128,512]{2,1,0:T(8,128)(2,1)} custom-call(s32[1,48]{1,0:T(1,128)} %pick_ref.1, s32[8,1,8]{2,1,0:T(1,128)} %count_ref.1, s32[8,1,8]{2,1,0:T(1,128)} %fill_ref.1, bf16[8,147456]{1,0:T(8,128)(2,1)} %query_hbm.1, bf16[48,36864]{1,0:T(8,128)(2,1)} %page_hbm.1), custom_call_target="tpu_custom_call" | custom-call | flops 7516192768 | bytes 8388608 | tf_op jit(solution)/shard_map/attention/pallas_call | solution.py:168
  16.7 7.9 %all-to-all-start = ((bf16[16,128,512]{2,1,0:T(8,128)(2,1)}), bf16[16,128,512]{2,1,0:T(8,128)(2,1)S(1)}, u32[]{:S(2)}, u32[]{:S(2)}) async-start(bf16[16,128,512]{2,1,0:T(8,128)(2,1)} %attention.1), calls=%async_computation | async-start | bytes 4194304 | tf_op jit(solution)/shard_map/all_to_all | solution.py:483
  24.7 0.2 dynamic-slice_reduce_fusion
  25.0 0.1 add.152
  25.1 0.2 convolution_convert_fusion.2
  25.3 1.0 collective-permute-start.16
  26.3 0.1 reshape.261
  26.5 0.1 reshape_reshape.3
  26.6 1.9 gather_fusion
  28.5 0.1 copy.29
  28.6 0.2 fusion.34
  29.0 24.1 %all-to-all-done = bf16[16,128,512]{2,1,0:T(8,128)(2,1)S(1)} async-done(((bf16[16,128,512]{2,1,0:T(8,128)(2,1)}), bf16[16,128,512]{2,1,0:T(8,128)(2,1)S(1)}, u32[]{:S(2)}, u32[]{:S(2)}) %all-to-all-start) | async-done | bytes 2097184 | tf_op jit(solution)/shard_map/all_to_all | solution.py:483
  53.1 5.5 %project_sent.1 = (bf16[256,896]{1,0:T(8,128)(2,1)}, bf16[256,896]{1,0:T(8,128)(2,1)}, bf16[256,896]{1,0:T(8,128)(2,1)}, bf16[256,896]{1,0:T(8,128)(2,1)}, bf16[16,32,512]{2,1,0:T(8,128)(2,1)S(1)}) custom-call(s32[64]{0:T(128)S(1)} %xor_add_fusion.order_ref, bf16[8,256,512]{2,1,0:T(8,128)(2,1)S(1)} %bitcast.42, bf16[4,512,128]{2,1,0:T(8,128)(2,1)} %up_hbm.1, ...), custom_call_target="tpu_custom_call" | custom-call | flops 2147483648 | bytes 8388608 | tf_op jit(solution)/shard_map/project_sent/pallas_call | solution.py:255
  58.6 0.1 collective-permute-start
  58.7 0.7 collective-permute-start.1
  59.4 0.3 collective-permute-start.2
  59.7 2.0 collective-permute-start.3
  61.7 3.6 %project_kept.1.kept_ref = bf16[4,256,896]{2,1,0:T(8,128)(2,1)S(1)} custom-call(s32[64]{0:T(128)S(1)} %xor_add_fusion.order_ref, bf16[16,32,512]{2,1,0:T(8,128)(2,1)S(1)} %get-tuple-element.20.lifted_ref, bf16[512,3584]{1,0:T(8,128)(2,1)} %weight_hbm.3), custom_call_target="tpu_custom_call" | custom-call | flops 1073741824 | bytes 6291456 | tf_op jit(solution)/shard_map/project_kept/pallas_call | solution.py:275
  65.3 2.7 %collective-permute-done.rest_0_ = bf16[256,896]{1,0:T(8,128)(2,1)S(1)} collective-permute-done((bf16[256,896]{1,0:T(8,128)(2,1)}, bf16[256,896]{1,0:T(8,128)(2,1)S(1)}, u32[]{:S(2)}, u32[]{:S(2)}) %collective-permute-start) | collective-permute-done | bytes 458784 | tf_op jit(solution)/shard_map/ppermute | solution.py:432
  68.0 1.3 collective-permute-done.1.rest_1_
  69.3 0.4 add_pieces.3
  69.7 2.5 %collective-permute-start.4 = (bf16[128,896]{1,0:T(8,128)(2,1)S(1)}, bf16[128,896]{1,0:T(8,128)(2,1)S(1)}, u32[]{:S(2)}, u32[]{:S(2)}) collective-permute-start(bf16[128,896]{1,0:T(8,128)(2,1)S(1)} %get-tuple-element.26), channel_id=1, source_target_pairs={{0,12},{12,0},{4,8},{8,4},{1,13},{13,1},{5,9},{9,5},{2,14},{14,2},... | collective-permute-start | bytes 688136 | tf_op jit(solution)/shard_map/ppermute | solution.py:432
  72.1 2.9 %collective-permute-start.6 = (bf16[128,896]{1,0:T(8,128)(2,1)S(1)}, bf16[128,896]{1,0:T(8,128)(2,1)S(1)}, u32[]{:S(2)}, u32[]{:S(2)}) collective-permute-start(bf16[128,896]{1,0:T(8,128)(2,1)S(1)} %get-tuple-element.28), channel_id=1, source_target_pairs={{0,3},{3,0},{1,2},{2,1},{4,7},{7,4},{5,6},{6,5},{8,11},{11,8},{9,1... | collective-permute-start | bytes 688136 | tf_op jit(solution)/shard_map/ppermute | solution.py:432
  75.1 0.2 fusion.36
  75.3 0.6 collective-permute-done.4.rest_0_
  75.8 1.2 collective-permute-done.5.rest_1_
  77.0 1.5 collective-permute-done.6.rest_2_
  78.5 1.8 collective-permute-done.7.rest_3_
  80.2 0.2 add_pieces.4
  80.4 0.1 collective-permute-start.8
  80.5 1.5 collective-permute-start.9
  82.0 0.1 eq.114
  82.1 0.1 eq.112
  82.2 0.1 add.163
  82.3 0.1 iota_compare_fusion.1
  82.4 4.2 %collective-permute-done.8.rest_0_ = bf16[64,1792]{1,0:T(8,128)(2,1)S(1)} collective-permute-done((bf16[64,1792]{1,0:T(8,128)(2,1)S(1)}, bf16[64,1792]{1,0:T(8,128)(2,1)S(1)}, u32[]{:S(2)}, u32[]{:S(2)}) %collective-permute-start.8) | collective-permute-done | bytes 229408 | tf_op jit(solution)/shard_map/ppermute | solution.py:432
  86.6 1.5 collective-permute-start.10
  88.2 0.6 collective-permute-start.11
  88.8 0.4 compare_reduce_fusion
  89.2 2.4 collective-permute-done.10.first_ref
  91.6 1.5 collective-permute-done.11.second_ref
  93.1 0.2 finish.1
  93.2 7.6 %collective-permute-start.12 = (bf16[8,3584]{1,0:T(8,128)(2,1)S(1)}, bf16[8,3584]{1,0:T(8,128)(2,1)S(1)}, u32[]{:S(2)}, u32[]{:S(2)}) collective-permute-start(bf16[8,3584]{1,0:T(8,128)(2,1)S(1)} %get-tuple-element.36), channel_id=1, source_target_pairs={{0,16},{16,0},{32,48},{48,32},{64,80},{80,64},{96,112},{112,96},{1... | collective-permute-start | bytes 172040 | tf_op jit(solution)/shard_map/ppermute | solution.py:449
  100.8 0.9 collective-permute-done.12
  101.7 0.1 broadcast_select_fusion
  101.8 1.1 collective-permute-start.13
  102.9 5.7 %collective-permute-start.14 = (bf16[8,3584]{1,0:T(8,128)(2,1)S(1)}, bf16[8,3584]{1,0:T(8,128)(2,1)S(1)}, u32[]{:S(2)}, u32[]{:S(2)}) collective-permute-start(bf16[8,3584]{1,0:T(8,128)(2,1)S(1)} %get-tuple-element.58), channel_id=1, source_target_pairs={{0,64},{16,80},{32,96},{48,112},{64,0},{80,16},{96,32},{112,48},{1... | collective-permute-start | bytes 172040 | tf_op jit(solution)/shard_map/ppermute | solution.py:445
  108.6 1.5 collective-permute-start.17
  110.0 2.4 collective-permute-start.19
  112.4 0.3 fusion
  112.8 0.3 collective-permute-done.17
  113.1 1.6 collective-permute-done.18
  114.7 0.5 multiply_reduce_fusion
  115.1 0.1 multiply_convert_fusion
  115.3 1.2 fusion.6
  116.5 54.9 %all_to_all.28 = bf16[128,8,1792]{2,1,0:T(8,128)(2,1)S(1)} all-to-all(bf16[128,8,1792]{2,1,0:T(8,128)(2,1)S(1)} %fusion.6), channel_id=1, replica_groups=mesh['rep'=8,'ep_0'=4,'ep_1'=4] {'rep','ep_0','ep_1'}, dimensions={0} | all-to-all | bytes 7340032 | tf_op jit(solution)/shard_map/all_to_all | solution.py:538
  171.4 3.1 %copy-done.1 = bf16[1,1024,3584]{2,1,0:T(8,128)(2,1)S(1)} copy-done((bf16[1,1024,3584]{2,1,0:T(8,128)(2,1)S(1)}, bf16[1,1024,3584]{2,1,0:T(8,128)(2,1)}, u32[]{:S(2)}) %copy-start.1) | copy-done | bytes 7340056
  174.5 11.3 %expert.1 = bf16[1024,1792]{1,0:T(8,128)(2,1)} custom-call(bf16[1024,1792]{1,0:T(8,128)(2,1)S(1)} %bitcast.41, bf16[1,3584,1024]{2,1,0:T(8,128)(2,1)S(1)} %bitcast.44, bf16[1,1024,3584]{2,1,0:T(8,128)(2,1)S(1)} %copy-done.1), custom_call_target="tpu_custom_call" | custom-call | flops 8589934592 | bytes 23068672 | tf_op jit(solution)/shard_map/expert/pallas_call | solution.py:384
  185.8 4.7 %all-to-all-start.2 = ((bf16[128,8,1792]{2,1,0:T(8,128)(2,1)}), bf16[128,8,1792]{2,1,0:T(8,128)(2,1)}, u32[]{:S(2)}, u32[]{:S(2)}) async-start(bf16[128,8,1792]{2,1,0:T(8,128)(2,1)} %bitcast.45), calls=%async_computation.2 | async-start | bytes 7340032 | tf_op jit(solution)/shard_map/all_to_all | solution.py:540
  190.6 0.4 fusion.7
  191.0 0.1 reduce-precision_convert_fusion
  191.2 46.0 %all-to-all-done.2 = bf16[128,8,1792]{2,1,0:T(8,128)(2,1)} async-done(((bf16[128,8,1792]{2,1,0:T(8,128)(2,1)}), bf16[128,8,1792]{2,1,0:T(8,128)(2,1)}, u32[]{:S(2)}, u32[]{:S(2)}) %all-to-all-start.2) | async-done | bytes 3670048 | tf_op jit(solution)/shard_map/all_to_all | solution.py:540
  237.2 2.7 %fusion.4 = f32[128,1792]{1,0:T(8,128)S(1)} fusion(bf16[128,8,1792]{2,1,0:T(8,128)(2,1)} %all-to-all-done.2, bf16[64,1024]{1,0:T(8,128)(2,1)S(1)} %get-tuple-element.56, bf16[64,1024]{1,0:T(8,128)(2,1)S(1)} %get-tuple-element.55), kind=kOutput, calls=%fused_computation.9 | convolution fusion | flops 470286336 | bytes 4849664 | tf_op jit(solution)/shard_map/dot_general | solution.py:48
  240.0 0.8 fusion.16
  (70 shorter events, 0.8 us)
Async XLA Ops:
  0.6 24.1 %copy-start = (s32[8,1,2]{0,2,1:T(2,128)S(1)}, s32[8,1,2]{0,2,1:T(2,128)}, u32[]{:S(2)}) copy-start(s32[8,1,2]{0,2,1:T(2,128)} %param.24) | copy-start | bytes 196
  16.7 8.4 %copy-start.3 = (bf16[8,14336]{1,0:T(8,128)(2,1)S(1)}, bf16[8,14336]{1,0:T(8,128)(2,1)}, u32[]{:S(2)}) copy-start(bf16[8,14336]{1,0:T(8,128)(2,1)} %param.20) | copy-start | bytes 688132
  16.7 9.6 %copy-start.9 = (s32[1,2]{1,0:T(1,128)S(1)}, s32[1,2]{1,0:T(1,128)}, u32[]{:S(2)}) copy-start(s32[1,2]{1,0:T(1,128)} %param.25) | copy-start | bytes 28
  16.7 9.7 %copy-start.5 = (s32[32,8]{0,1:T(8,128)S(1)}, s32[32,8]{0,1:T(8,128)}, u32[]{:S(2)}) copy-start(s32[32,8]{0,1:T(8,128)} %param.26) | copy-start | bytes 3076
  16.7 9.9 %copy-start.2 = (s32[128]{0:T(128)S(1)}, s32[128]{0:T(128)}, u32[]{:S(2)}) copy-start(s32[128]{0:T(128)} %param.28) | copy-start | bytes 1540
  16.7 12.2 %copy-start.7 = (s32[64]{0:T(128)S(1)}, s32[64]{0:T(128)}, u32[]{:S(2)}) copy-start(s32[64]{0:T(128)} %constant.136.clone) | copy-start | bytes 772
  16.7 12.2 %copy-start.8 = (s32[64]{0:T(128)S(1)}, s32[64]{0:T(128)}, u32[]{:S(2)}) copy-start(s32[64]{0:T(128)} %constant.137.clone) | copy-start | bytes 772
  16.7 36.3 %all-to-all-start = ((bf16[16,128,512]{2,1,0:T(8,128)(2,1)}), bf16[16,128,512]{2,1,0:T(8,128)(2,1)S(1)}, u32[]{:S(2)}, u32[]{:S(2)}) async-start(bf16[16,128,512]{2,1,0:T(8,128)(2,1)} %attention.1), calls=%async_computation | async-start | bytes 4194304 | tf_op jit(solution)/shard_map/all_to_all | solution.py:483
  25.3 75.5 %collective-permute-start.16 = (bf16[8,3584]{1,0:T(8,128)(2,1)S(1)}, bf16[8,3584]{1,0:T(8,128)(2,1)S(1)}, u32[]{:S(2)}, u32[]{:S(2)}) collective-permute-start(bf16[8,3584]{1,0:T(8,128)(2,1)S(1)} %convolution_convert_fusion.2), channel_id=1, source_target_pairs={{0,16},{16,0},{32,48},{48,32},{64,80},{80,64},{96,112},{112,96},{1... | collective-permute-start | bytes 172040 | tf_op jit(solution)/shard_map/ppermute | solution.py:449
  58.6 9.4 %collective-permute-start = (bf16[256,896]{1,0:T(8,128)(2,1)}, bf16[256,896]{1,0:T(8,128)(2,1)S(1)}, u32[]{:S(2)}, u32[]{:S(2)}) collective-permute-start(bf16[256,896]{1,0:T(8,128)(2,1)} %get-tuple-element.21), channel_id=1, source_target_pairs={{0,4},{4,0},{8,12},{12,8},{1,5},{5,1},{9,13},{13,9},{2,6},{6,2},{1... | collective-permute-start | bytes 1376264 | tf_op jit(solution)/shard_map/ppermute | solution.py:432
  58.7 10.6 %collective-permute-start.1 = (bf16[256,896]{1,0:T(8,128)(2,1)}, bf16[256,896]{1,0:T(8,128)(2,1)S(1)}, u32[]{:S(2)}, u32[]{:S(2)}) collective-permute-start(bf16[256,896]{1,0:T(8,128)(2,1)} %get-tuple-element.22), channel_id=1, source_target_pairs={{0,12},{12,0},{4,8},{8,4},{1,13},{13,1},{5,9},{9,5},{2,14},{14,2},... | collective-permute-start | bytes 1376264 | tf_op jit(solution)/shard_map/ppermute | solution.py:432
  59.4 9.9 %collective-permute-start.2 = (bf16[256,896]{1,0:T(8,128)(2,1)}, bf16[256,896]{1,0:T(8,128)(2,1)S(1)}, u32[]{:S(2)}, u32[]{:S(2)}) collective-permute-start(bf16[256,896]{1,0:T(8,128)(2,1)} %get-tuple-element.23), channel_id=1, source_target_pairs={{0,1},{1,0},{2,3},{3,2},{4,5},{5,4},{6,7},{7,6},{8,9},{9,8},{10,11... | collective-permute-start | bytes 1376264 | tf_op jit(solution)/shard_map/ppermute | solution.py:432
  59.7 9.6 %collective-permute-start.3 = (bf16[256,896]{1,0:T(8,128)(2,1)}, bf16[256,896]{1,0:T(8,128)(2,1)S(1)}, u32[]{:S(2)}, u32[]{:S(2)}) collective-permute-start(bf16[256,896]{1,0:T(8,128)(2,1)} %get-tuple-element.24), channel_id=1, source_target_pairs={{0,3},{3,0},{1,2},{2,1},{4,7},{7,4},{5,6},{6,5},{8,11},{11,8},{9,1... | collective-permute-start | bytes 1376264 | tf_op jit(solution)/shard_map/ppermute | solution.py:432
  69.7 6.2 %collective-permute-start.4 = (bf16[128,896]{1,0:T(8,128)(2,1)S(1)}, bf16[128,896]{1,0:T(8,128)(2,1)S(1)}, u32[]{:S(2)}, u32[]{:S(2)}) collective-permute-start(bf16[128,896]{1,0:T(8,128)(2,1)S(1)} %get-tuple-element.26), channel_id=1, source_target_pairs={{0,12},{12,0},{4,8},{8,4},{1,13},{13,1},{5,9},{9,5},{2,14},{14,2},... | collective-permute-start | bytes 688136 | tf_op jit(solution)/shard_map/ppermute | solution.py:432
  72.1 4.9 %collective-permute-start.5 = (bf16[128,896]{1,0:T(8,128)(2,1)S(1)}, bf16[128,896]{1,0:T(8,128)(2,1)S(1)}, u32[]{:S(2)}, u32[]{:S(2)}) collective-permute-start(bf16[128,896]{1,0:T(8,128)(2,1)S(1)} %get-tuple-element.27), channel_id=1, source_target_pairs={{0,4},{4,0},{8,12},{12,8},{1,5},{5,1},{9,13},{13,9},{2,6},{6,2},{1... | collective-permute-start | bytes 688136 | tf_op jit(solution)/shard_map/ppermute | solution.py:432
  72.1 6.3 %collective-permute-start.6 = (bf16[128,896]{1,0:T(8,128)(2,1)S(1)}, bf16[128,896]{1,0:T(8,128)(2,1)S(1)}, u32[]{:S(2)}, u32[]{:S(2)}) collective-permute-start(bf16[128,896]{1,0:T(8,128)(2,1)S(1)} %get-tuple-element.28), channel_id=1, source_target_pairs={{0,3},{3,0},{1,2},{2,1},{4,7},{7,4},{5,6},{6,5},{8,11},{11,8},{9,1... | collective-permute-start | bytes 688136 | tf_op jit(solution)/shard_map/ppermute | solution.py:432
  75.1 5.2 %collective-permute-start.7 = (bf16[128,896]{1,0:T(8,128)(2,1)S(1)}, bf16[128,896]{1,0:T(8,128)(2,1)S(1)}, u32[]{:S(2)}, u32[]{:S(2)}) collective-permute-start(bf16[128,896]{1,0:T(8,128)(2,1)S(1)} %get-tuple-element.29), channel_id=1, source_target_pairs={{0,1},{1,0},{2,3},{3,2},{4,5},{5,4},{6,7},{7,6},{8,9},{9,8},{10,11... | collective-permute-start | bytes 688136 | tf_op jit(solution)/shard_map/ppermute | solution.py:432
  80.2 34.9 %copy-start.4 = (f32[3584]{0:T(1024)S(1)}, f32[3584]{0:T(1024)}, u32[]{:S(2)}) copy-start(f32[3584]{0:T(1024)} %param.29) | copy-start | bytes 43012
  80.4 6.2 %collective-permute-start.8 = (bf16[64,1792]{1,0:T(8,128)(2,1)S(1)}, bf16[64,1792]{1,0:T(8,128)(2,1)S(1)}, u32[]{:S(2)}, u32[]{:S(2)}) collective-permute-start(bf16[64,1792]{1,0:T(8,128)(2,1)S(1)} %get-tuple-element.31), channel_id=1, source_target_pairs={{0,1},{1,0},{2,3},{3,2},{4,5},{5,4},{6,7},{7,6},{8,9},{9,8},{10,11... | collective-permute-start | bytes 688136 | tf_op jit(solution)/shard_map/ppermute | solution.py:432
  80.5 6.1 %collective-permute-start.9 = (bf16[64,1792]{1,0:T(8,128)(2,1)S(1)}, bf16[64,1792]{1,0:T(8,128)(2,1)S(1)}, u32[]{:S(2)}, u32[]{:S(2)}) collective-permute-start(bf16[64,1792]{1,0:T(8,128)(2,1)S(1)} %get-tuple-element.32), channel_id=1, source_target_pairs={{0,4},{4,0},{8,12},{12,8},{1,5},{5,1},{9,13},{13,9},{2,6},{6,2},{1... | collective-permute-start | bytes 688136 | tf_op jit(solution)/shard_map/ppermute | solution.py:432
  86.6 4.9 %collective-permute-start.10 = (bf16[32,1792]{1,0:T(8,128)(2,1)S(1)}, bf16[32,1792]{1,0:T(8,128)(2,1)S(1)}, u32[]{:S(2)}, u32[]{:S(2)}) collective-permute-start(bf16[32,1792]{1,0:T(8,128)(2,1)S(1)} %get-tuple-element.34), channel_id=1, source_target_pairs={{0,3},{3,0},{1,2},{2,1},{4,7},{7,4},{5,6},{6,5},{8,11},{11,8},{9,1... | collective-permute-start | bytes 344072 | tf_op jit(solution)/shard_map/ppermute | solution.py:432
  88.2 4.9 %collective-permute-start.11 = (bf16[32,1792]{1,0:T(8,128)(2,1)S(1)}, bf16[32,1792]{1,0:T(8,128)(2,1)S(1)}, u32[]{:S(2)}, u32[]{:S(2)}) collective-permute-start(bf16[32,1792]{1,0:T(8,128)(2,1)S(1)} %get-tuple-element.35), channel_id=1, source_target_pairs={{0,12},{12,0},{4,8},{8,4},{1,13},{13,1},{5,9},{9,5},{2,14},{14,2},... | collective-permute-start | bytes 344072 | tf_op jit(solution)/shard_map/ppermute | solution.py:432
  93.2 8.5 %collective-permute-start.12 = (bf16[8,3584]{1,0:T(8,128)(2,1)S(1)}, bf16[8,3584]{1,0:T(8,128)(2,1)S(1)}, u32[]{:S(2)}, u32[]{:S(2)}) collective-permute-start(bf16[8,3584]{1,0:T(8,128)(2,1)S(1)} %get-tuple-element.36), channel_id=1, source_target_pairs={{0,16},{16,0},{32,48},{48,32},{64,80},{80,64},{96,112},{112,96},{1... | collective-permute-start | bytes 172040 | tf_op jit(solution)/shard_map/ppermute | solution.py:449
  101.8 8.3 %collective-permute-start.13 = (bf16[8,3584]{1,0:T(8,128)(2,1)S(1)}, bf16[8,3584]{1,0:T(8,128)(2,1)S(1)}, u32[]{:S(2)}, u32[]{:S(2)}) collective-permute-start(bf16[8,3584]{1,0:T(8,128)(2,1)S(1)} %get-tuple-element.58), channel_id=1, source_target_pairs={{0,32},{16,48},{32,64},{48,80},{64,96},{80,112},{96,0},{112,16},{1... | collective-permute-start | bytes 172040 | tf_op jit(solution)/shard_map/ppermute | solution.py:445
  102.9 9.5 %collective-permute-start.14 = (bf16[8,3584]{1,0:T(8,128)(2,1)S(1)}, bf16[8,3584]{1,0:T(8,128)(2,1)S(1)}, u32[]{:S(2)}, u32[]{:S(2)}) collective-permute-start(bf16[8,3584]{1,0:T(8,128)(2,1)S(1)} %get-tuple-element.58), channel_id=1, source_target_pairs={{0,64},{16,80},{32,96},{48,112},{64,0},{80,16},{96,32},{112,48},{1... | collective-permute-start | bytes 172040 | tf_op jit(solution)/shard_map/ppermute | solution.py:445
  108.6 3.9 %collective-permute-start.15 = (bf16[8,3584]{1,0:T(8,128)(2,1)S(1)}, bf16[8,3584]{1,0:T(8,128)(2,1)S(1)}, u32[]{:S(2)}, u32[]{:S(2)}) collective-permute-start(bf16[8,3584]{1,0:T(8,128)(2,1)S(1)} %get-tuple-element.58), channel_id=1, source_target_pairs={{0,96},{16,112},{32,0},{48,16},{64,32},{80,48},{96,64},{112,80},{1... | collective-permute-start | bytes 172040 | tf_op jit(solution)/shard_map/ppermute | solution.py:445
  108.6 4.5 %collective-permute-start.17 = (bf16[8,3584]{1,0:T(8,128)(2,1)S(1)}, bf16[8,3584]{1,0:T(8,128)(2,1)S(1)}, u32[]{:S(2)}, u32[]{:S(2)}) collective-permute-start(bf16[8,3584]{1,0:T(8,128)(2,1)S(1)} %get-tuple-element.57), channel_id=1, source_target_pairs={{0,32},{16,48},{32,64},{48,80},{64,96},{80,112},{96,0},{112,16},{1... | collective-permute-start | bytes 172040 | tf_op jit(solution)/shard_map/ppermute | solution.py:445
  110.0 4.6 %collective-permute-start.18 = (bf16[8,3584]{1,0:T(8,128)(2,1)S(1)}, bf16[8,3584]{1,0:T(8,128)(2,1)S(1)}, u32[]{:S(2)}, u32[]{:S(2)}) collective-permute-start(bf16[8,3584]{1,0:T(8,128)(2,1)S(1)} %get-tuple-element.57), channel_id=1, source_target_pairs={{0,64},{16,80},{32,96},{48,112},{64,0},{80,16},{96,32},{112,48},{1... | collective-permute-start | bytes 172040 | tf_op jit(solution)/shard_map/ppermute | solution.py:445
  110.0 4.6 %collective-permute-start.19 = (bf16[8,3584]{1,0:T(8,128)(2,1)S(1)}, bf16[8,3584]{1,0:T(8,128)(2,1)S(1)}, u32[]{:S(2)}, u32[]{:S(2)}) collective-permute-start(bf16[8,3584]{1,0:T(8,128)(2,1)S(1)} %get-tuple-element.57), channel_id=1, source_target_pairs={{0,96},{16,112},{32,0},{48,16},{64,32},{80,48},{96,64},{112,80},{1... | collective-permute-start | bytes 172040 | tf_op jit(solution)/shard_map/ppermute | solution.py:445
  112.4 59.0 %slice-start = ((s8[7340032]{0:T(1024)(128)(4,1)}), s8[4194304]{0:T(1024)(128)(4,1)S(1)}, s32[]{:S(2)}) async-start(s8[7340032]{0:T(1024)(128)(4,1)} %bitcast.43), calls=%async_computation.3 | async-start | bytes 8388608
  115.3 56.1 %slice-start.1 = ((s8[7340032]{0:T(1024)(128)(4,1)}), s8[3145728]{0:T(1024)(128)(4,1)S(1)}, s32[]{:S(2)}) async-start(s8[7340032]{0:T(1024)(128)(4,1)} %bitcast.43), calls=%async_computation.4 | async-start | bytes 6291456
  171.4 3.1 %copy-start.1 = (bf16[1,1024,3584]{2,1,0:T(8,128)(2,1)S(1)}, bf16[1,1024,3584]{2,1,0:T(8,128)(2,1)}, u32[]{:S(2)}) copy-start(bf16[1,1024,3584]{2,1,0:T(8,128)(2,1)} %out_ref.1) | copy-start | bytes 22020100
  185.8 4.8 %copy-start.6 = (f32[32,8]{0,1:T(8,128)S(1)}, f32[32,8]{0,1:T(8,128)}, u32[]{:S(2)}) copy-start(f32[32,8]{0,1:T(8,128)} %param.27) | copy-start | bytes 3076
  185.8 51.4 %all-to-all-start.2 = ((bf16[128,8,1792]{2,1,0:T(8,128)(2,1)}), bf16[128,8,1792]{2,1,0:T(8,128)(2,1)}, u32[]{:S(2)}, u32[]{:S(2)}) async-start(bf16[128,8,1792]{2,1,0:T(8,128)(2,1)} %bitcast.45), calls=%async_computation.2 | async-start | bytes 7340032 | tf_op jit(solution)/shard_map/all_to_all | solution.py:540

commit v2 on v1

--- a/solution.py
+++ b/solution.py
@@ -18,7 +18,6 @@
 TOP = 8
 PAGE = 64
 SPEC = 4
-MAXP = 12
 REQ_DEV = 8
 PAGES_DEV = 48
 TOK_DEV = REQ_DEV * SPEC
@@ -27,7 +26,6 @@
 DEVICES = 128
 CAP = 4
 BAND = D // 4
-KEYS = MAXP * PAGE
 EP = ("ep_0", "ep_1")
 REP_EP = ("rep", "ep_0", "ep_1")
 SCORE_SCALE = 192.0 ** (-0.5)
@@ -56,13 +54,30 @@
     return pltpu.with_memory_space_constraint(value, pltpu.HBM)
 
 
-WINDOWS = (4, 8, 12, 14)
+WINDOWS = (4, 8, 12)
 SPAN = 8 * KVW
+LANES = 5
+KEY_STEP = 49
+ASK_STEP = 9
+
+
+def store_lanes(ref, row, extra, value):
+    count = value.shape[0]
+    value = jnp.concatenate((value.astype(F32), jnp.zeros((count, LANES * 128 - KVW), F32)), axis=1)
+    for tile in range(LANES):
+        ref[tile, pl.ds(row + extra, count), :] = value[:, tile * 128 : tile * 128 + 128]
+
+
+def load_lanes(ref, starts, stride):
+    tiles = [
+        jnp.concatenate([ref[tile, pl.ds(at, 8, stride=stride), :] for at in starts], axis=0)
+        for tile in range(LANES)
+    ]
+    return jnp.concatenate([tile.astype(BF) for tile in tiles], axis=1)
 
 
 def attention_body(pick_ref, count_ref, fill_ref, query_hbm, page_hbm, out_hbm, *scratch):
-    key_s, order_s, piece_s, query_s, page_v, query_v, out_ref = scratch[:7]
-    page_sem, query_sem, out_sem = scratch[7:]
+    key_s, query_s, page_v, query_v, out_ref, page_sem, query_sem, out_sem = scratch
 
     def page_load(group):
         columns = pl.ds(pl.multiple_of(group * SPAN, 128), SPAN)
@@ -85,26 +100,21 @@
     for pair in range(8):
         for position in range(SPEC):
             query_load(position, pair).start()
-    row = iota2(8, 128, 0)
-    for place in range(0, PAGES_DEV, 2):
-        page = jnp.where(row < 4, pick_ref[0, place], pick_ref[0, place + 1])
-        order_s[place * 4 : place * 4 + 8, :] = row % 4 * PAGES_DEV + page
-    to_place = (iota2(192, 192, 1) == order_s[:, :1]).astype(BF)
-
-    def regroup_keys(group, carry):
+
+    def spread_keys(group, carry):
         page_load(group).wait()
-        for part in range(2):
-            tokens = [
-                page_v[group, :, t * KVW : (t + 1) * KVW] for t in range(4 * part, 4 * part + 4)
-            ]
-            key_s[group * 2 + part] = mm(to_place, jnp.concatenate(tokens, axis=0))
+        for t in range(8):
+            store_lanes(
+                key_s,
+                pl.multiple_of(group * 8 * KEY_STEP, 8),
+                t * KEY_STEP,
+                page_v[group, :, t * KVW : (t + 1) * KVW],
+            )
         return carry
 
-    lax.fori_loop(0, 8, regroup_keys, 0)
-    row, col = iota2(REQ_DEV * 32, 256, 0), iota2(REQ_DEV * 32, 256, 1)
-    by_request = (col == row % 32 * 8 + row // 32).astype(BF)
-
-    def regroup_queries(pair, carry):
+    lax.fori_loop(0, 8, spread_keys, 0)
+
+    def spread_queries(pair, carry):
         for position in range(SPEC):
             query_load(position, pair).wait()
         for column in range(2):
@@ -112,33 +122,37 @@
                 for head in range(HEADS_DEV):
                     at = (column * HEADS_DEV + head) * KVW
                     place = (column * SPEC + position) * HEADS_DEV + head
-                    piece_s[place * 8 : place * 8 + 8, :] = query_v[
-                        pair, position, :, at : at + KVW
-                    ].astype(F32)
-        rows = mm(by_request, piece_s[...].astype(BF)).astype(BF)
-        query_s[:, pl.ds(pl.multiple_of(pair * 32, 32), 32), :] = rows.reshape(REQ_DEV, 32, KVW)
+                    store_lanes(
+                        query_s,
+                        pl.multiple_of(pair * 32 * ASK_STEP, 8),
+                        place * ASK_STEP,
+                        query_v[pair, position, :, at : at + KVW],
+                    )
         return carry
 
-    lax.fori_loop(0, 8, regroup_queries, 0)
+    lax.fori_loop(0, 8, spread_queries, 0)
 
     replica = lax.axis_index("rep")
     rows = SPEC * HEADS
     late = iota2(rows, 1, 0) // HEADS_DEV % SPEC - SPEC + 1
 
     def attend(i, offset, length, window):
-        start = jnp.minimum(offset // 2 * 2, PAGES_DEV - window)
-        skip = offset - start
-        span = window * 4
-        keys = key_s[:, pl.ds(pl.multiple_of(start * 4, 8), span), :]
-        keys = keys.reshape(16 * span, KVW).astype(BF)
+        held = [pick_ref[0, jnp.minimum(offset + j, PAGES_DEV - 1)] for j in range(window)]
+        keys = load_lanes(
+            key_s,
+            [group * 8 * KEY_STEP + page for group in range(8) for page in held],
+            KEY_STEP,
+        )
+        asked = load_lanes(
+            query_s, [block * 8 * ASK_STEP + i for block in range(rows // 8)], ASK_STEP
+        )
         scores = lax.dot_general(
-            query_s[i], keys, (((1,), (1,)), ((), ())), preferred_element_type=F32
-        )
-        key = iota2(1, 16 * span, 1)
-        place = key % span // 4
-        token = (place - skip) * PAGE + key // span * 4 + key % 4
-        at = jnp.where(place < skip, KEYS, token)
-        scores = jnp.where(at < late + length, scores * SCORE_SCALE, -1e30)
+            asked, keys, (((1,), (1,)), ((), ())), preferred_element_type=F32
+        )
+        span = window * 8
+        key = iota2(1, 8 * span, 1)
+        token = key % span // 8 * PAGE + key // span * 8 + key % 8
+        scores = jnp.where(token < late + length, scores * SCORE_SCALE, -1e30)
         exponent = jnp.exp(scores - jnp.max(scores, axis=1, keepdims=True))
         total = jnp.sum(exponent, axis=1, keepdims=True)
         latent = mm(exponent.astype(BF), keys[:, :LAT]) / total
@@ -149,9 +163,8 @@
     def request(i, offset):
         count = count_ref[replica, 0, i]
         length = (count - 1) * PAGE + fill_ref[replica, 0, i]
-        need = count + offset % 2
         for least, window in zip((0,) + WINDOWS, WINDOWS):
-            pl.when((need > least) & (need <= window))(
+            pl.when((count > least) & (count <= window))(
                 functools.partial(attend, i, offset, length, window)
             )
         result_copy(i).start()
@@ -171,10 +184,8 @@
         out_specs=far,
         out_shape=pltpu.HBM((N_EP, REQ_DEV * 16, LAT), BF),
         scratch_shapes=[
-            pltpu.VMEM((16, PAGES_DEV * 4, KVW), F32),
-            pltpu.VMEM((PAGES_DEV * 4, 128), jnp.int32),
-            pltpu.VMEM((256, KVW), F32),
-            pltpu.VMEM((REQ_DEV, SPEC * HEADS, KVW), BF),
+            pltpu.VMEM((LANES, PAGE * KEY_STEP, 128), F32),
+            pltpu.VMEM((LANES, SPEC * HEADS * ASK_STEP, 128), F32),
             pltpu.VMEM((8, PAGES_DEV, SPAN), BF),
             pltpu.VMEM((8, SPEC, REQ_DEV, SPAN), BF),
             pltpu.VMEM((N_EP, REQ_DEV * 16, LAT), BF),
@@ -349,7 +360,14 @@
     )(near(pick), near(kept), near(first), near(second))
 
 
-def expert_body(x_ref, in_ref, out_ref, o_hbm, x_s, h_s, o_ref, sems):
+def expert_body(x_ref, in_ref, out_hbm, o_hbm, x_s, h_s, o_ref, out_ref, sems, out_sem):
+    loads = []
+    for step in range(4):
+        rows = pl.ds(step * 256, 256)
+        loads.append(
+            pltpu.make_async_copy(out_hbm.at[0, rows], out_ref.at[rows], out_sem.at[step])
+        )
+        loads[-1].start()
     apart = rows_first(lambda r: (r % 128 // 4) * 8 + (r // 128) * 4 + r % 4)
     joined = rows_first(lambda r: (r // 4 % 2) * 128 + (r // 8) * 4 + r % 4)
     for step in range(4):
@@ -359,10 +377,12 @@
     for at in range(0, FFE, 256):
         value = mm(x_s[...], in_ref[0, :, at : at + 256])
         h_s[:, at : at + 256] = (value / (1.0 + jnp.exp(-value))).astype(BF)
+    for load in loads:
+        load.wait()
     copies = []
     for at in range(0, HALF, 256):
         halves = [
-            mm(h_s[...], out_ref[0, :, first + at : first + at + 256]).astype(BF)
+            mm(h_s[...], out_ref[:, first + at : first + at + 256]).astype(BF)
             for first in (0, HALF)
         ]
         for step in range(4):
@@ -381,23 +401,26 @@
 
 def expert(incoming, expert_in, expert_out):
     whole = pl.BlockSpec(memory_space=pltpu.VMEM)
+    far = pl.BlockSpec(memory_space=pltpu.HBM)
     return pl.pallas_call(
         expert_body,
-        in_specs=[whole, whole, whole],
-        out_specs=pl.BlockSpec(memory_space=pltpu.HBM),
+        in_specs=[whole, whole, far],
+        out_specs=far,
         out_shape=pltpu.HBM((DEVICES * 8, HALF), BF),
         scratch_shapes=[
             pltpu.VMEM((512, D), BF),
             pltpu.VMEM((512, FFE), BF),
             pltpu.VMEM((DEVICES * 8, HALF), BF),
+            pltpu.VMEM((FFE, D), BF),
             pltpu.SemaphoreType.DMA((7,)),
+            pltpu.SemaphoreType.DMA((4,)),
         ],
         cost_estimate=pl.CostEstimate(
             flops=8 << 30, bytes_accessed=22 << 20, transcendentals=512 * 1024
         ),
-        compiler_params=pltpu.CompilerParams(vmem_limit_bytes=24 << 20),
+        compiler_params=pltpu.CompilerParams(vmem_limit_bytes=32 << 20),
         name="expert",
-    )(near(incoming), near(expert_in), near(expert_out))
+    )(near(incoming), near(expert_in), distant(expert_out))
 
 
 NEAR = [(0, 1), (1, 0), (2, 3), (3, 2)]
@@ -499,6 +522,7 @@
 
     own_residual = by_position(residual)
     came = from_replicas(mm(pick, own_residual).astype(BF), odd)
+    latent, came = lax.optimization_barrier((latent, came))
     served_residual = served(own_residual, came)
     own_branch, offer = sum_over_columns(
         pick, project(block_order(), latent.reshape(8, 256, LAT), value_up, out_weight)

time: 241 us -> 239 us (level)
    all_to_all x1, waiting for transfers between devices: 24.1 us -> 18.3 us  [per_device(): latent = lax.all_to_all(latent, EP, split_axis=0, concat_axis=0, tiled=True)]
    pallas_call x1, Pallas kernels: 16 us -> 12.4 us  [attention(): pl.pallas_call(attention_body, in_specs=[few, few, few, far, far], out_sp...]
    ppermute x6, waiting for transfers between devices: 1.9 us -> 4.94 us  [shifted(): lax.ppermute(value, axis, [(s, (s + steps) % count) for s in range(count)])]
    pallas_call x1, Pallas kernels: 11.3 us -> 14.1 us  [expert(): pl.pallas_call(expert_body, in_specs=[whole, whole, far], out_specs=far,...]
    unnamed x27 -> x23, local copies, waits for them, and re-layouts: 3.31 us -> 0.87 us
  transfers between devices with their start and end apart: 22 -> 22, of which waited for: 14 -> 19; matrix products, arithmetic and copies ran while one was open for 2% -> 2% of each run, Pallas kernels for 4% -> 7%
where the time goes in v2:
time: 239 us; the launch traced here: 238 us
  waiting for transfers between devices  87.5 us (37%)
  blocking collectives  55.9 us (23%)
  starting transfers between devices  45 us (19%)
  Pallas kernels  36.4 us (15%)
  matrix products  4.9 us (2%)
  local copies, waits for them, and re-layouts  4.65 us (2%)
  other arithmetic  2.72 us (1%)
    all_to_all x1, blocking collectives, per_device(): lax.all_to_all(outgoing, REP_EP, split_axis=0, concat_axis=0, tiled=True)  55.9 us
    all_to_all x1, waiting for transfers between devices, per_device(): lax.all_to_all(outer, REP_EP, split_axis=0, concat_axis=0, tiled=True)  46 us
    all_to_all x1, waiting for transfers between devices, per_device(): latent = lax.all_to_all(latent, EP, split_axis=0, concat_axis=0, tiled=True)  18.3 us
    ppermute x12, waiting for transfers between devices, exchange(): out.append(lax.ppermute(piece, axis, PAIRS[flip]))  17.3 us
    pallas_call x1, Pallas kernels, expert(): pl.pallas_call(expert_body, in_specs=[whole, whole, far], out_specs=far,...  14.1 us
    ppermute x12, starting transfers between devices, exchange(): out.append(lax.ppermute(piece, axis, PAIRS[flip]))  12.8 us
    pallas_call x1, Pallas kernels, attention(): pl.pallas_call(attention_body, in_specs=[few, few, few, far, far], out_sp...  12.4 us
    ppermute x6, starting transfers between devices, shifted(): lax.ppermute(value, axis, [(s, (s + steps) % count) for s in range(count)])  11.4 us
  transfers between devices with their start and end apart: 22, of which 19 were waited for; matrix products, arithmetic and copies ran while one was open for 2% of the time, Pallas kernels for 7%

profile of v2, /device:TPU:1, one launch (start us, length us, event | category | flops | bytes accessed | tf_op | source)
XLA Modules:
  0.0 238.1 jit_solution(11802023103376699426)
XLA Ops:
  0.7 0.7 copy-done
  1.3 0.2 dynamic-slice_reduce_fusion
  1.7 0.9 fusion.67
  2.6 0.2 convolution_convert_fusion.2
  2.8 1.5 collective-permute-start
  4.3 12.4 %attention.1 = bf16[16,128,512]{2,1,0:T(8,128)(2,1)} custom-call(s32[1,48]{1,0:T(1,128)} %pick_ref.1, s32[8,1,8]{2,1,0:T(1,128)} %count_ref.1, s32[8,1,8]{2,1,0:T(1,128)} %fill_ref.1, bf16[8,147456]{1,0:T(8,128)(2,1)} %query_hbm.1, bf16[48,36864]{1,0:T(8,128)(2,1)} %page_hbm.1), custom_call_target="tpu_custom_call" | custom-call | flops 7516192768 | bytes 8388608 | tf_op jit(solution)/shard_map/attention/pallas_call | solution.py:181
  16.7 7.1 %all-to-all-start = ((bf16[16,128,512]{2,1,0:T(8,128)(2,1)}), bf16[16,128,512]{2,1,0:T(8,128)(2,1)S(1)}, u32[]{:S(2)}, u32[]{:S(2)}) async-start(bf16[16,128,512]{2,1,0:T(8,128)(2,1)} %attention.1), calls=%async_computation | async-start | bytes 4194304 | tf_op jit(solution)/shard_map/all_to_all | solution.py:506
  24.0 0.1 reshape_reshape.3
  24.2 1.9 gather_fusion
  26.0 0.1 copy.29
  26.2 0.2 fusion.26
  26.5 1.6 collective-permute-start.1
  28.1 3.3 %collective-permute-start.2 = (bf16[8,3584]{1,0:T(8,128)(2,1)S(1)}, bf16[8,3584]{1,0:T(8,128)(2,1)S(1)}, u32[]{:S(2)}, u32[]{:S(2)}) collective-permute-start(bf16[8,3584]{1,0:T(8,128)(2,1)S(1)} %broadcast_select_fusion.1), channel_id=1, source_target_pairs={{0,64},{16,80},{32,96},{48,112},{64,0},{80,16},{96,32},{112,48},{1... | collective-permute-start | bytes 172040 | tf_op jit(solution)/shard_map/ppermute | solution.py:468
  31.4 0.7 collective-permute-start.3
  32.1 0.1 collective-permute-done.1
  32.2 2.1 collective-permute-done.2
  34.4 0.4 collective-permute-done.3
  34.7 18.3 %all-to-all-done = bf16[16,128,512]{2,1,0:T(8,128)(2,1)S(1)} async-done(((bf16[16,128,512]{2,1,0:T(8,128)(2,1)}), bf16[16,128,512]{2,1,0:T(8,128)(2,1)S(1)}, u32[]{:S(2)}, u32[]{:S(2)}) %all-to-all-start) | async-done | bytes 2097184 | tf_op jit(solution)/shard_map/all_to_all | solution.py:506
  53.0 5.5 %project_sent.1 = (bf16[256,896]{1,0:T(8,128)(2,1)}, bf16[256,896]{1,0:T(8,128)(2,1)}, bf16[256,896]{1,0:T(8,128)(2,1)}, bf16[256,896]{1,0:T(8,128)(2,1)}, bf16[16,32,512]{2,1,0:T(8,128)(2,1)S(1)}) custom-call(s32[64]{0:T(128)S(1)} %xor_add_fusion.order_ref, bf16[8,256,512]{2,1,0:T(8,128)(2,1)S(1)} %bitcast.43, bf16[4,512,128]{2,1,0:T(8,128)(2,1)} %up_hbm.1, ...), custom_call_target="tpu_custom_call" | custom-call | flops 2147483648 | bytes 8388608 | tf_op jit(solution)/shard_map/project_sent/pallas_call | solution.py:266
  58.5 0.1 collective-permute-start.4
  58.6 2.1 collective-permute-start.5
  60.7 3.1 %collective-permute-start.7 = (bf16[256,896]{1,0:T(8,128)(2,1)}, bf16[256,896]{1,0:T(8,128)(2,1)S(1)}, u32[]{:S(2)}, u32[]{:S(2)}) collective-permute-start(bf16[256,896]{1,0:T(8,128)(2,1)} %get-tuple-element.27), channel_id=1, source_target_pairs={{0,3},{3,0},{1,2},{2,1},{4,7},{7,4},{5,6},{6,5},{8,11},{11,8},{9,1... | collective-permute-start | bytes 1376264 | tf_op jit(solution)/shard_map/ppermute | solution.py:455
  63.8 3.6 %project_kept.1.kept_ref = bf16[4,256,896]{2,1,0:T(8,128)(2,1)S(1)} custom-call(s32[64]{0:T(128)S(1)} %xor_add_fusion.order_ref, bf16[16,32,512]{2,1,0:T(8,128)(2,1)S(1)} %get-tuple-element.23.lifted_ref, bf16[512,3584]{1,0:T(8,128)(2,1)} %weight_hbm.3), custom_call_target="tpu_custom_call" | custom-call | flops 1073741824 | bytes 6291456 | tf_op jit(solution)/shard_map/project_kept/pallas_call | solution.py:286
  67.4 1.8 collective-permute-done.4.rest_0_
  69.2 0.7 collective-permute-done.5.rest_1_
  69.9 0.7 collective-permute-done.6.rest_2_
  70.6 1.6 collective-permute-done.7.rest_3_
  72.2 0.4 add_pieces.3
  72.6 3.2 %collective-permute-start.10 = (bf16[128,896]{1,0:T(8,128)(2,1)S(1)}, bf16[128,896]{1,0:T(8,128)(2,1)S(1)}, u32[]{:S(2)}, u32[]{:S(2)}) collective-permute-start(bf16[128,896]{1,0:T(8,128)(2,1)S(1)} %get-tuple-element.31), channel_id=1, source_target_pairs={{0,3},{3,0},{1,2},{2,1},{4,7},{7,4},{5,6},{6,5},{8,11},{11,8},{9,1... | collective-permute-start | bytes 688136 | tf_op jit(solution)/shard_map/ppermute | solution.py:455
  75.8 1.1 collective-permute-start.8
  76.9 0.2 fusion.28
  77.1 2.1 collective-permute-done.10.rest_2_
  79.2 1.8 collective-permute-done.11.rest_3_
  80.9 1.2 collective-permute-done.8.rest_0_
  82.2 0.2 add_pieces.4
  82.3 1.6 collective-permute-start.12
  84.2 0.1 iota_compare_fusion.1
  84.3 3.1 %collective-permute-done.12.rest_0_ = bf16[64,1792]{1,0:T(8,128)(2,1)S(1)} collective-permute-done((bf16[64,1792]{1,0:T(8,128)(2,1)S(1)}, bf16[64,1792]{1,0:T(8,128)(2,1)S(1)}, u32[]{:S(2)}, u32[]{:S(2)}) %collective-permute-start.12) | collective-permute-done | bytes 229408 | tf_op jit(solution)/shard_map/ppermute | solution.py:455
  87.5 1.4 collective-permute-done.13.rest_1_
  88.9 0.2 collective-permute-start.14
  89.1 1.5 collective-permute-start.15
  90.6 0.4 compare_reduce_fusion
  90.9 2.9 %collective-permute-done.14.first_ref = bf16[32,1792]{1,0:T(8,128)(2,1)S(1)} collective-permute-done((bf16[32,1792]{1,0:T(8,128)(2,1)S(1)}, bf16[32,1792]{1,0:T(8,128)(2,1)S(1)}, u32[]{:S(2)}, u32[]{:S(2)}) %collective-permute-start.14) | collective-permute-done | bytes 114720 | tf_op jit(solution)/shard_map/ppermute | solution.py:455
  93.8 0.1 collective-permute-done.15.second_ref
  93.9 0.2 finish.1
  94.1 7.5 %collective-permute-start.16 = (bf16[8,3584]{1,0:T(8,128)(2,1)S(1)}, bf16[8,3584]{1,0:T(8,128)(2,1)S(1)}, u32[]{:S(2)}, u32[]{:S(2)}) collective-permute-start(bf16[8,3584]{1,0:T(8,128)(2,1)S(1)} %get-tuple-element.39), channel_id=1, source_target_pairs={{0,16},{16,0},{32,48},{48,32},{64,80},{80,64},{96,112},{112,96},{1... | collective-permute-start | bytes 172040 | tf_op jit(solution)/shard_map/ppermute | solution.py:472
  101.6 0.9 collective-permute-done.16
  102.6 1.7 collective-permute-start.17
  104.3 3.2 %collective-permute-start.18 = (bf16[8,3584]{1,0:T(8,128)(2,1)S(1)}, bf16[8,3584]{1,0:T(8,128)(2,1)S(1)}, u32[]{:S(2)}, u32[]{:S(2)}) collective-permute-start(bf16[8,3584]{1,0:T(8,128)(2,1)S(1)} %broadcast_select_fusion), channel_id=1, source_target_pairs={{0,64},{16,80},{32,96},{48,112},{64,0},{80,16},{96,32},{112,48},{1... | collective-permute-start | bytes 172040 | tf_op jit(solution)/shard_map/ppermute | solution.py:468
  107.5 1.0 collective-permute-start.19
  108.4 1.6 collective-permute-done.18
  110.1 0.7 collective-permute-done.19
  110.8 0.3 fusion
  111.1 0.5 multiply_reduce_fusion
  111.6 0.1 multiply_convert_fusion
  111.8 1.2 fusion.5
  113.0 55.9 %all_to_all.28 = bf16[128,8,1792]{2,1,0:T(8,128)(2,1)S(1)} all-to-all(bf16[128,8,1792]{2,1,0:T(8,128)(2,1)S(1)} %fusion.5), channel_id=1, replica_groups=mesh['rep'=8,'ep_0'=4,'ep_1'=4] {'rep','ep_0','ep_1'}, dimensions={0} | all-to-all | bytes 7340032 | tf_op jit(solution)/shard_map/all_to_all | solution.py:562
  169.0 14.1 %expert.1 = bf16[1024,1792]{1,0:T(8,128)(2,1)} custom-call(bf16[1024,1792]{1,0:T(8,128)(2,1)S(1)} %bitcast.42, bf16[1,3584,1024]{2,1,0:T(8,128)(2,1)S(1)} %bitcast.45, bf16[1,1024,3584]{2,1,0:T(8,128)(2,1)} %out_hbm.1), custom_call_target="tpu_custom_call" | custom-call | flops 8589934592 | bytes 23068672 | tf_op jit(solution)/shard_map/expert/pallas_call | solution.py:405
  183.1 4.7 %all-to-all-start.2 = ((bf16[128,8,1792]{2,1,0:T(8,128)(2,1)}), bf16[128,8,1792]{2,1,0:T(8,128)(2,1)}, u32[]{:S(2)}, u32[]{:S(2)}) async-start(bf16[128,8,1792]{2,1,0:T(8,128)(2,1)} %bitcast.46), calls=%async_computation.2 | async-start | bytes 7340032 | tf_op jit(solution)/shard_map/all_to_all | solution.py:564
  187.9 0.4 fusion.6
  188.3 0.1 reduce-precision_convert_fusion
  188.5 46.0 %all-to-all-done.2 = bf16[128,8,1792]{2,1,0:T(8,128)(2,1)} async-done(((bf16[128,8,1792]{2,1,0:T(8,128)(2,1)}), bf16[128,8,1792]{2,1,0:T(8,128)(2,1)}, u32[]{:S(2)}, u32[]{:S(2)}) %all-to-all-start.2) | async-done | bytes 3670048 | tf_op jit(solution)/shard_map/all_to_all | solution.py:564
  234.5 2.7 %fusion.3 = f32[128,1792]{1,0:T(8,128)S(1)} fusion(bf16[128,8,1792]{2,1,0:T(8,128)(2,1)} %all-to-all-done.2, bf16[64,1024]{1,0:T(8,128)(2,1)S(1)} %get-tuple-element.60, bf16[64,1024]{1,0:T(8,128)(2,1)S(1)} %get-tuple-element.59), kind=kOutput, calls=%fused_computation.8 | convolution fusion | flops 470286336 | bytes 4849664 | tf_op jit(solution)/shard_map/dot_general | solution.py:46
  237.3 0.8 fusion.15
  (68 shorter events, 1.4 us)
Async XLA Ops:
  0.6 0.7 copy-start
  2.8 23.6 %collective-permute-start = (bf16[8,3584]{1,0:T(8,128)(2,1)S(1)}, bf16[8,3584]{1,0:T(8,128)(2,1)S(1)}, u32[]{:S(2)}, u32[]{:S(2)}) collective-permute-start(bf16[8,3584]{1,0:T(8,128)(2,1)S(1)} %convolution_convert_fusion.2), channel_id=1, source_target_pairs={{0,16},{16,0},{32,48},{48,32},{64,80},{80,64},{96,112},{112,96},{1... | collective-permute-start | bytes 172040 | tf_op jit(solution)/shard_map/ppermute | solution.py:472
  16.7 7.1 %copy-start.7 = (s32[1,2]{1,0:T(1,128)S(1)}, s32[1,2]{1,0:T(1,128)}, u32[]{:S(2)}) copy-start(s32[1,2]{1,0:T(1,128)} %param.25) | copy-start | bytes 28
  16.7 7.3 %copy-start.3 = (s32[32,8]{0,1:T(8,128)S(1)}, s32[32,8]{0,1:T(8,128)}, u32[]{:S(2)}) copy-start(s32[32,8]{0,1:T(8,128)} %param.26) | copy-start | bytes 3076
  16.7 7.5 %copy-start.1 = (s32[128]{0:T(128)S(1)}, s32[128]{0:T(128)}, u32[]{:S(2)}) copy-start(s32[128]{0:T(128)} %param.28) | copy-start | bytes 1540
  16.7 15.4 %copy-start.5 = (s32[64]{0:T(128)S(1)}, s32[64]{0:T(128)}, u32[]{:S(2)}) copy-start(s32[64]{0:T(128)} %constant.136.clone) | copy-start | bytes 772
  16.7 15.4 %copy-start.6 = (s32[64]{0:T(128)S(1)}, s32[64]{0:T(128)}, u32[]{:S(2)}) copy-start(s32[64]{0:T(128)} %constant.137.clone) | copy-start | bytes 772
  16.7 36.3 %all-to-all-start = ((bf16[16,128,512]{2,1,0:T(8,128)(2,1)}), bf16[16,128,512]{2,1,0:T(8,128)(2,1)S(1)}, u32[]{:S(2)}, u32[]{:S(2)}) async-start(bf16[16,128,512]{2,1,0:T(8,128)(2,1)} %attention.1), calls=%async_computation | async-start | bytes 4194304 | tf_op jit(solution)/shard_map/all_to_all | solution.py:506
  26.5 5.7 %collective-permute-start.1 = (bf16[8,3584]{1,0:T(8,128)(2,1)S(1)}, bf16[8,3584]{1,0:T(8,128)(2,1)S(1)}, u32[]{:S(2)}, u32[]{:S(2)}) collective-permute-start(bf16[8,3584]{1,0:T(8,128)(2,1)S(1)} %broadcast_select_fusion.1), channel_id=1, source_target_pairs={{0,32},{16,48},{32,64},{48,80},{64,96},{80,112},{96,0},{112,16},{1... | collective-permute-start | bytes 172040 | tf_op jit(solution)/shard_map/ppermute | solution.py:468
  28.1 6.3 %collective-permute-start.2 = (bf16[8,3584]{1,0:T(8,128)(2,1)S(1)}, bf16[8,3584]{1,0:T(8,128)(2,1)S(1)}, u32[]{:S(2)}, u32[]{:S(2)}) collective-permute-start(bf16[8,3584]{1,0:T(8,128)(2,1)S(1)} %broadcast_select_fusion.1), channel_id=1, source_target_pairs={{0,64},{16,80},{32,96},{48,112},{64,0},{80,16},{96,32},{112,48},{1... | collective-permute-start | bytes 172040 | tf_op jit(solution)/shard_map/ppermute | solution.py:468
  31.4 3.3 %collective-permute-start.3 = (bf16[8,3584]{1,0:T(8,128)(2,1)S(1)}, bf16[8,3584]{1,0:T(8,128)(2,1)S(1)}, u32[]{:S(2)}, u32[]{:S(2)}) collective-permute-start(bf16[8,3584]{1,0:T(8,128)(2,1)S(1)} %broadcast_select_fusion.1), channel_id=1, source_target_pairs={{0,96},{16,112},{32,0},{48,16},{64,32},{80,48},{96,64},{112,80},{1... | collective-permute-start | bytes 172040 | tf_op jit(solution)/shard_map/ppermute | solution.py:468
  58.5 10.7 %collective-permute-start.4 = (bf16[256,896]{1,0:T(8,128)(2,1)}, bf16[256,896]{1,0:T(8,128)(2,1)S(1)}, u32[]{:S(2)}, u32[]{:S(2)}) collective-permute-start(bf16[256,896]{1,0:T(8,128)(2,1)} %get-tuple-element.24), channel_id=1, source_target_pairs={{0,4},{4,0},{8,12},{12,8},{1,5},{5,1},{9,13},{13,9},{2,6},{6,2},{1... | collective-permute-start | bytes 1376264 | tf_op jit(solution)/shard_map/ppermute | solution.py:455
  58.6 11.3 %collective-permute-start.5 = (bf16[256,896]{1,0:T(8,128)(2,1)}, bf16[256,896]{1,0:T(8,128)(2,1)S(1)}, u32[]{:S(2)}, u32[]{:S(2)}) collective-permute-start(bf16[256,896]{1,0:T(8,128)(2,1)} %get-tuple-element.25), channel_id=1, source_target_pairs={{0,12},{12,0},{4,8},{8,4},{1,13},{13,1},{5,9},{9,5},{2,14},{14,2},... | collective-permute-start | bytes 1376264 | tf_op jit(solution)/shard_map/ppermute | solution.py:455
  60.7 9.9 %collective-permute-start.6 = (bf16[256,896]{1,0:T(8,128)(2,1)}, bf16[256,896]{1,0:T(8,128)(2,1)S(1)}, u32[]{:S(2)}, u32[]{:S(2)}) collective-permute-start(bf16[256,896]{1,0:T(8,128)(2,1)} %get-tuple-element.26), channel_id=1, source_target_pairs={{0,1},{1,0},{2,3},{3,2},{4,5},{5,4},{6,7},{7,6},{8,9},{9,8},{10,11... | collective-permute-start | bytes 1376264 | tf_op jit(solution)/shard_map/ppermute | solution.py:455
  60.7 11.5 %collective-permute-start.7 = (bf16[256,896]{1,0:T(8,128)(2,1)}, bf16[256,896]{1,0:T(8,128)(2,1)S(1)}, u32[]{:S(2)}, u32[]{:S(2)}) collective-permute-start(bf16[256,896]{1,0:T(8,128)(2,1)} %get-tuple-element.27), channel_id=1, source_target_pairs={{0,3},{3,0},{1,2},{2,1},{4,7},{7,4},{5,6},{6,5},{8,11},{11,8},{9,1... | collective-permute-start | bytes 1376264 | tf_op jit(solution)/shard_map/ppermute | solution.py:455
  72.6 6.6 %collective-permute-start.10 = (bf16[128,896]{1,0:T(8,128)(2,1)S(1)}, bf16[128,896]{1,0:T(8,128)(2,1)S(1)}, u32[]{:S(2)}, u32[]{:S(2)}) collective-permute-start(bf16[128,896]{1,0:T(8,128)(2,1)S(1)} %get-tuple-element.31), channel_id=1, source_target_pairs={{0,3},{3,0},{1,2},{2,1},{4,7},{7,4},{5,6},{6,5},{8,11},{11,8},{9,1... | collective-permute-start | bytes 688136 | tf_op jit(solution)/shard_map/ppermute | solution.py:455
  75.8 5.2 %collective-permute-start.11 = (bf16[128,896]{1,0:T(8,128)(2,1)S(1)}, bf16[128,896]{1,0:T(8,128)(2,1)S(1)}, u32[]{:S(2)}, u32[]{:S(2)}) collective-permute-start(bf16[128,896]{1,0:T(8,128)(2,1)S(1)} %get-tuple-element.32), channel_id=1, source_target_pairs={{0,1},{1,0},{2,3},{3,2},{4,5},{5,4},{6,7},{7,6},{8,9},{9,8},{10,11... | collective-permute-start | bytes 688136 | tf_op jit(solution)/shard_map/ppermute | solution.py:455
  75.8 6.4 %collective-permute-start.8 = (bf16[128,896]{1,0:T(8,128)(2,1)S(1)}, bf16[128,896]{1,0:T(8,128)(2,1)S(1)}, u32[]{:S(2)}, u32[]{:S(2)}) collective-permute-start(bf16[128,896]{1,0:T(8,128)(2,1)S(1)} %get-tuple-element.29), channel_id=1, source_target_pairs={{0,12},{12,0},{4,8},{8,4},{1,13},{13,1},{5,9},{9,5},{2,14},{14,2},... | collective-permute-start | bytes 688136 | tf_op jit(solution)/shard_map/ppermute | solution.py:455
  76.9 5.3 %collective-permute-start.9 = (bf16[128,896]{1,0:T(8,128)(2,1)S(1)}, bf16[128,896]{1,0:T(8,128)(2,1)S(1)}, u32[]{:S(2)}, u32[]{:S(2)}) collective-permute-start(bf16[128,896]{1,0:T(8,128)(2,1)S(1)} %get-tuple-element.30), channel_id=1, source_target_pairs={{0,4},{4,0},{8,12},{12,8},{1,5},{5,1},{9,13},{13,9},{2,6},{6,2},{1... | collective-permute-start | bytes 688136 | tf_op jit(solution)/shard_map/ppermute | solution.py:455
  82.2 29.4 %copy-start.2 = (f32[3584]{0:T(1024)S(1)}, f32[3584]{0:T(1024)}, u32[]{:S(2)}) copy-start(f32[3584]{0:T(1024)} %param.29) | copy-start | bytes 43012
  82.3 5.1 %collective-permute-start.12 = (bf16[64,1792]{1,0:T(8,128)(2,1)S(1)}, bf16[64,1792]{1,0:T(8,128)(2,1)S(1)}, u32[]{:S(2)}, u32[]{:S(2)}) collective-permute-start(bf16[64,1792]{1,0:T(8,128)(2,1)S(1)} %get-tuple-element.34), channel_id=1, source_target_pairs={{0,1},{1,0},{2,3},{3,2},{4,5},{5,4},{6,7},{7,6},{8,9},{9,8},{10,11... | collective-permute-start | bytes 688136 | tf_op jit(solution)/shard_map/ppermute | solution.py:455
  84.0 4.9 %collective-permute-start.13 = (bf16[64,1792]{1,0:T(8,128)(2,1)S(1)}, bf16[64,1792]{1,0:T(8,128)(2,1)S(1)}, u32[]{:S(2)}, u32[]{:S(2)}) collective-permute-start(bf16[64,1792]{1,0:T(8,128)(2,1)S(1)} %get-tuple-element.35), channel_id=1, source_target_pairs={{0,4},{4,0},{8,12},{12,8},{1,5},{5,1},{9,13},{13,9},{2,6},{6,2},{1... | collective-permute-start | bytes 688136 | tf_op jit(solution)/shard_map/ppermute | solution.py:455
  88.9 4.9 %collective-permute-start.14 = (bf16[32,1792]{1,0:T(8,128)(2,1)S(1)}, bf16[32,1792]{1,0:T(8,128)(2,1)S(1)}, u32[]{:S(2)}, u32[]{:S(2)}) collective-permute-start(bf16[32,1792]{1,0:T(8,128)(2,1)S(1)} %get-tuple-element.37), channel_id=1, source_target_pairs={{0,3},{3,0},{1,2},{2,1},{4,7},{7,4},{5,6},{6,5},{8,11},{11,8},{9,1... | collective-permute-start | bytes 344072 | tf_op jit(solution)/shard_map/ppermute | solution.py:455
  89.1 4.9 %collective-permute-start.15 = (bf16[32,1792]{1,0:T(8,128)(2,1)S(1)}, bf16[32,1792]{1,0:T(8,128)(2,1)S(1)}, u32[]{:S(2)}, u32[]{:S(2)}) collective-permute-start(bf16[32,1792]{1,0:T(8,128)(2,1)S(1)} %get-tuple-element.38), channel_id=1, source_target_pairs={{0,12},{12,0},{4,8},{8,4},{1,13},{13,1},{5,9},{9,5},{2,14},{14,2},... | collective-permute-start | bytes 344072 | tf_op jit(solution)/shard_map/ppermute | solution.py:455
  94.1 8.4 %collective-permute-start.16 = (bf16[8,3584]{1,0:T(8,128)(2,1)S(1)}, bf16[8,3584]{1,0:T(8,128)(2,1)S(1)}, u32[]{:S(2)}, u32[]{:S(2)}) collective-permute-start(bf16[8,3584]{1,0:T(8,128)(2,1)S(1)} %get-tuple-element.39), channel_id=1, source_target_pairs={{0,16},{16,0},{32,48},{48,32},{64,80},{80,64},{96,112},{112,96},{1... | collective-permute-start | bytes 172040 | tf_op jit(solution)/shard_map/ppermute | solution.py:472
  102.6 5.9 %collective-permute-start.17 = (bf16[8,3584]{1,0:T(8,128)(2,1)S(1)}, bf16[8,3584]{1,0:T(8,128)(2,1)S(1)}, u32[]{:S(2)}, u32[]{:S(2)}) collective-permute-start(bf16[8,3584]{1,0:T(8,128)(2,1)S(1)} %broadcast_select_fusion), channel_id=1, source_target_pairs={{0,32},{16,48},{32,64},{48,80},{64,96},{80,112},{96,0},{112,16},{1... | collective-permute-start | bytes 172040 | tf_op jit(solution)/shard_map/ppermute | solution.py:468
  104.3 5.8 %collective-permute-start.18 = (bf16[8,3584]{1,0:T(8,128)(2,1)S(1)}, bf16[8,3584]{1,0:T(8,128)(2,1)S(1)}, u32[]{:S(2)}, u32[]{:S(2)}) collective-permute-start(bf16[8,3584]{1,0:T(8,128)(2,1)S(1)} %broadcast_select_fusion), channel_id=1, source_target_pairs={{0,64},{16,80},{32,96},{48,112},{64,0},{80,16},{96,32},{112,48},{1... | collective-permute-start | bytes 172040 | tf_op jit(solution)/shard_map/ppermute | solution.py:468
  107.5 3.3 %collective-permute-start.19 = (bf16[8,3584]{1,0:T(8,128)(2,1)S(1)}, bf16[8,3584]{1,0:T(8,128)(2,1)S(1)}, u32[]{:S(2)}, u32[]{:S(2)}) collective-permute-start(bf16[8,3584]{1,0:T(8,128)(2,1)S(1)} %broadcast_select_fusion), channel_id=1, source_target_pairs={{0,96},{16,112},{32,0},{48,16},{64,32},{80,48},{96,64},{112,80},{1... | collective-permute-start | bytes 172040 | tf_op jit(solution)/shard_map/ppermute | solution.py:468
  110.8 58.2 %slice-start = ((s8[7340032]{0:T(1024)(128)(4,1)}), s8[4194304]{0:T(1024)(128)(4,1)S(1)}, s32[]{:S(2)}) async-start(s8[7340032]{0:T(1024)(128)(4,1)} %bitcast.44), calls=%async_computation.3 | async-start | bytes 8388608
  111.7 57.2 %slice-start.1 = ((s8[7340032]{0:T(1024)(128)(4,1)}), s8[3145728]{0:T(1024)(128)(4,1)S(1)}, s32[]{:S(2)}) async-start(s8[7340032]{0:T(1024)(128)(4,1)} %bitcast.44), calls=%async_computation.4 | async-start | bytes 6291456
  183.1 4.8 %copy-start.4 = (f32[32,8]{0,1:T(8,128)S(1)}, f32[32,8]{0,1:T(8,128)}, u32[]{:S(2)}) copy-start(f32[32,8]{0,1:T(8,128)} %param.27) | copy-start | bytes 3076
  183.1 51.4 %all-to-all-start.2 = ((bf16[128,8,1792]{2,1,0:T(8,128)(2,1)}), bf16[128,8,1792]{2,1,0:T(8,128)(2,1)}, u32[]{:S(2)}, u32[]{:S(2)}) async-start(bf16[128,8,1792]{2,1,0:T(8,128)(2,1)} %bitcast.46), calls=%async_computation.2 | async-start | bytes 7340032 | tf_op jit(solution)/shard_map/all_to_all | solution.py:564

commit v3 on v2

--- a/solution.py
+++ b/solution.py
@@ -231,10 +231,17 @@
     by_head = rows_first(
         lambda r: (r // 32 % 2) * 128 + (r % 8) * 16 + (r // 8 % 4) * 4 + r // 64
     )
-    for step in range(8):
-        both = mm(by_head, latent_ref[step]).astype(BF)
-        for head in range(HEADS_DEV):
-            split_ref[head, step * 64 : step * 64 + 64, :] = both[head * 64 : head * 64 + 64]
+
+    def split(turn, carry):
+        for part in range(4):
+            step = turn * 4 + part
+            both = mm(by_head, latent_ref[step]).astype(BF)
+            at = pl.multiple_of(step * 64, 64)
+            for head in range(HEADS_DEV):
+                split_ref[head, pl.ds(at, 64), :] = both[head * 64 : head * 64 + 64]
+        return carry
+
+    lax.fori_loop(0, 2, split, 0)
     up_load.wait()
     for head in range(HEADS_DEV):
         lifted = mm(split_ref[head], up_ref[head]).astype(BF)
@@ -361,22 +368,22 @@
 
 
 def expert_body(x_ref, in_ref, out_hbm, o_hbm, x_s, h_s, o_ref, out_ref, sems, out_sem):
-    loads = []
-    for step in range(4):
-        rows = pl.ds(step * 256, 256)
-        loads.append(
-            pltpu.make_async_copy(out_hbm.at[0, rows], out_ref.at[rows], out_sem.at[step])
-        )
-        loads[-1].start()
+    loads = [pltpu.make_async_copy(out_hbm.at[0], out_ref, out_sem.at[0])]
+    loads[0].start()
     apart = rows_first(lambda r: (r % 128 // 4) * 8 + (r // 128) * 4 + r % 4)
     joined = rows_first(lambda r: (r // 4 % 2) * 128 + (r // 8) * 4 + r % 4)
     for step in range(4):
         block = mm(apart, x_ref[step * 256 : step * 256 + 256, :]).astype(BF)
         x_s[step * 128 : step * 128 + 128, :HALF] = block[:128]
         x_s[step * 128 : step * 128 + 128, HALF:] = block[128:]
-    for at in range(0, FFE, 256):
-        value = mm(x_s[...], in_ref[0, :, at : at + 256])
-        h_s[:, at : at + 256] = (value / (1.0 + jnp.exp(-value))).astype(BF)
+
+    def inner(step, carry):
+        columns = pl.ds(pl.multiple_of(step * 512, 512), 512)
+        value = mm(x_s[...], in_ref[0, :, columns])
+        h_s[:, columns] = (value / (1.0 + jnp.exp(-value))).astype(BF)
+        return carry
+
+    lax.fori_loop(0, 2, inner, 0)
     for load in loads:
         load.wait()
     copies = []

time: 239 us -> 236 us (0.987)
  Pallas kernels: 36.4 us -> 33.7 us
where the time goes in v3:
time: 236 us; the launch traced here: 235 us
  waiting for transfers between devices  87.4 us (37%)
  blocking collectives  56.1 us (24%)
  starting transfers between devices  44.8 us (19%)
  Pallas kernels  33.7 us (14%)
  matrix products  4.9 us (2%)
  local copies, waits for them, and re-layouts  4.65 us (2%)
  other arithmetic  2.72 us (1%)
    all_to_all x1, blocking collectives, per_device(): lax.all_to_all(outgoing, REP_EP, split_axis=0, concat_axis=0, tiled=True)  56.1 us
    all_to_all x1, waiting for transfers between devices, per_device(): lax.all_to_all(outer, REP_EP, split_axis=0, concat_axis=0, tiled=True)  46 us
    all_to_all x1, waiting for transfers between devices, per_device(): latent = lax.all_to_all(latent, EP, split_axis=0, concat_axis=0, tiled=True)  18.3 us
    ppermute x12, waiting for transfers between devices, exchange(): out.append(lax.ppermute(piece, axis, PAIRS[flip]))  17.3 us
    ppermute x12, starting transfers between devices, exchange(): out.append(lax.ppermute(piece, axis, PAIRS[flip]))  12.6 us
    pallas_call x1, Pallas kernels, attention(): pl.pallas_call(attention_body, in_specs=[few, few, few, far, far], out_sp...  12.4 us
    pallas_call x1, Pallas kernels, expert(): pl.pallas_call(expert_body, in_specs=[whole, whole, far], out_specs=far,...  11.9 us
    ppermute x6, starting transfers between devices, shifted(): lax.ppermute(value, axis, [(s, (s + steps) % count) for s in range(count)])  11.5 us
  transfers between devices with their start and end apart: 22, of which 19 were waited for; matrix products, arithmetic and copies ran while one was open for 2% of the time, Pallas kernels for 7%

profile of v3, /device:TPU:1, one launch (start us, length us, event | category | flops | bytes accessed | tf_op | source)
XLA Modules:
  0.0 235.3 jit_solution(15924047712333598552)
XLA Ops:
  0.7 0.7 copy-done
  1.3 0.2 dynamic-slice_reduce_fusion
  1.7 0.9 fusion.67
  2.6 0.2 convolution_convert_fusion.2
  2.8 1.5 collective-permute-start
  4.3 12.4 %attention.1 = bf16[16,128,512]{2,1,0:T(8,128)(2,1)} custom-call(s32[1,48]{1,0:T(1,128)} %pick_ref.1, s32[8,1,8]{2,1,0:T(1,128)} %count_ref.1, s32[8,1,8]{2,1,0:T(1,128)} %fill_ref.1, bf16[8,147456]{1,0:T(8,128)(2,1)} %query_hbm.1, bf16[48,36864]{1,0:T(8,128)(2,1)} %page_hbm.1), custom_call_target="tpu_custom_call" | custom-call | flops 7516192768 | bytes 8388608 | tf_op jit(solution)/shard_map/attention/pallas_call | solution.py:181
  16.7 7.1 %all-to-all-start = ((bf16[16,128,512]{2,1,0:T(8,128)(2,1)}), bf16[16,128,512]{2,1,0:T(8,128)(2,1)S(1)}, u32[]{:S(2)}, u32[]{:S(2)}) async-start(bf16[16,128,512]{2,1,0:T(8,128)(2,1)} %attention.1), calls=%async_computation | async-start | bytes 4194304 | tf_op jit(solution)/shard_map/all_to_all | solution.py:513
  24.0 0.1 reshape_reshape.3
  24.2 1.9 gather_fusion
  26.0 0.1 copy.29
  26.2 0.2 fusion.26
  26.5 1.6 collective-permute-start.1
  28.1 3.3 %collective-permute-start.2 = (bf16[8,3584]{1,0:T(8,128)(2,1)S(1)}, bf16[8,3584]{1,0:T(8,128)(2,1)S(1)}, u32[]{:S(2)}, u32[]{:S(2)}) collective-permute-start(bf16[8,3584]{1,0:T(8,128)(2,1)S(1)} %broadcast_select_fusion.1), channel_id=1, source_target_pairs={{0,64},{16,80},{32,96},{48,112},{64,0},{80,16},{96,32},{112,48},{1... | collective-permute-start | bytes 172040 | tf_op jit(solution)/shard_map/ppermute | solution.py:475
  31.4 0.7 collective-permute-start.3
  32.1 0.1 collective-permute-done.1
  32.2 2.1 collective-permute-done.2
  34.4 0.4 collective-permute-done.3
  34.7 18.3 %all-to-all-done = bf16[16,128,512]{2,1,0:T(8,128)(2,1)S(1)} async-done(((bf16[16,128,512]{2,1,0:T(8,128)(2,1)}), bf16[16,128,512]{2,1,0:T(8,128)(2,1)S(1)}, u32[]{:S(2)}, u32[]{:S(2)}) %all-to-all-start) | async-done | bytes 2097184 | tf_op jit(solution)/shard_map/all_to_all | solution.py:513
  53.0 5.0 %project_sent.1 = (bf16[256,896]{1,0:T(8,128)(2,1)}, bf16[256,896]{1,0:T(8,128)(2,1)}, bf16[256,896]{1,0:T(8,128)(2,1)}, bf16[256,896]{1,0:T(8,128)(2,1)}, bf16[16,32,512]{2,1,0:T(8,128)(2,1)S(1)}) custom-call(s32[64]{0:T(128)S(1)} %xor_add_fusion.order_ref, bf16[8,256,512]{2,1,0:T(8,128)(2,1)S(1)} %bitcast.43, bf16[4,512,128]{2,1,0:T(8,128)(2,1)} %up_hbm.1, ...), custom_call_target="tpu_custom_call" | custom-call | flops 2147483648 | bytes 8388608 | tf_op jit(solution)/shard_map/project_sent/pallas_call | solution.py:273
  58.0 0.1 collective-permute-start.4
  58.1 2.1 collective-permute-start.5
  60.2 3.1 %collective-permute-start.7 = (bf16[256,896]{1,0:T(8,128)(2,1)}, bf16[256,896]{1,0:T(8,128)(2,1)S(1)}, u32[]{:S(2)}, u32[]{:S(2)}) collective-permute-start(bf16[256,896]{1,0:T(8,128)(2,1)} %get-tuple-element.27), channel_id=1, source_target_pairs={{0,3},{3,0},{1,2},{2,1},{4,7},{7,4},{5,6},{6,5},{8,11},{11,8},{9,1... | collective-permute-start | bytes 1376264 | tf_op jit(solution)/shard_map/ppermute | solution.py:462
  63.3 3.6 %project_kept.1.kept_ref = bf16[4,256,896]{2,1,0:T(8,128)(2,1)S(1)} custom-call(s32[64]{0:T(128)S(1)} %xor_add_fusion.order_ref, bf16[16,32,512]{2,1,0:T(8,128)(2,1)S(1)} %get-tuple-element.23.lifted_ref, bf16[512,3584]{1,0:T(8,128)(2,1)} %weight_hbm.3), custom_call_target="tpu_custom_call" | custom-call | flops 1073741824 | bytes 6291456 | tf_op jit(solution)/shard_map/project_kept/pallas_call | solution.py:293
  66.9 1.8 collective-permute-done.4.rest_0_
  68.7 0.7 collective-permute-done.5.rest_1_
  69.4 0.7 collective-permute-done.6.rest_2_
  70.1 1.6 collective-permute-done.7.rest_3_
  71.7 0.4 add_pieces.3
  72.1 3.2 %collective-permute-start.10 = (bf16[128,896]{1,0:T(8,128)(2,1)S(1)}, bf16[128,896]{1,0:T(8,128)(2,1)S(1)}, u32[]{:S(2)}, u32[]{:S(2)}) collective-permute-start(bf16[128,896]{1,0:T(8,128)(2,1)S(1)} %get-tuple-element.31), channel_id=1, source_target_pairs={{0,3},{3,0},{1,2},{2,1},{4,7},{7,4},{5,6},{6,5},{8,11},{11,8},{9,1... | collective-permute-start | bytes 688136 | tf_op jit(solution)/shard_map/ppermute | solution.py:462
  75.3 1.1 collective-permute-start.8
  76.4 0.2 fusion.28
  76.6 2.1 collective-permute-done.10.rest_2_
  78.7 1.8 collective-permute-done.11.rest_3_
  80.4 1.2 collective-permute-done.8.rest_0_
  81.7 0.2 add_pieces.4
  81.8 1.5 collective-permute-start.12
  83.6 0.1 iota_compare_fusion.1
  83.7 3.1 %collective-permute-done.12.rest_0_ = bf16[64,1792]{1,0:T(8,128)(2,1)S(1)} collective-permute-done((bf16[64,1792]{1,0:T(8,128)(2,1)S(1)}, bf16[64,1792]{1,0:T(8,128)(2,1)S(1)}, u32[]{:S(2)}, u32[]{:S(2)}) %collective-permute-start.12) | collective-permute-done | bytes 229408 | tf_op jit(solution)/shard_map/ppermute | solution.py:462
  86.8 1.4 collective-permute-done.13.rest_1_
  88.2 0.2 collective-permute-start.14
  88.4 1.5 collective-permute-start.15
  89.9 0.4 compare_reduce_fusion
  90.3 2.9 %collective-permute-done.14.first_ref = bf16[32,1792]{1,0:T(8,128)(2,1)S(1)} collective-permute-done((bf16[32,1792]{1,0:T(8,128)(2,1)S(1)}, bf16[32,1792]{1,0:T(8,128)(2,1)S(1)}, u32[]{:S(2)}, u32[]{:S(2)}) %collective-permute-start.14) | collective-permute-done | bytes 114720 | tf_op jit(solution)/shard_map/ppermute | solution.py:462
  93.2 0.1 collective-permute-done.15.second_ref
  93.3 0.2 finish.1
  93.4 7.5 %collective-permute-start.16 = (bf16[8,3584]{1,0:T(8,128)(2,1)S(1)}, bf16[8,3584]{1,0:T(8,128)(2,1)S(1)}, u32[]{:S(2)}, u32[]{:S(2)}) collective-permute-start(bf16[8,3584]{1,0:T(8,128)(2,1)S(1)} %get-tuple-element.39), channel_id=1, source_target_pairs={{0,16},{16,0},{32,48},{48,32},{64,80},{80,64},{96,112},{112,96},{1... | collective-permute-start | bytes 172040 | tf_op jit(solution)/shard_map/ppermute | solution.py:479
  100.9 0.9 collective-permute-done.16
  101.9 1.7 collective-permute-start.17
  103.6 3.2 %collective-permute-start.18 = (bf16[8,3584]{1,0:T(8,128)(2,1)S(1)}, bf16[8,3584]{1,0:T(8,128)(2,1)S(1)}, u32[]{:S(2)}, u32[]{:S(2)}) collective-permute-start(bf16[8,3584]{1,0:T(8,128)(2,1)S(1)} %broadcast_select_fusion), channel_id=1, source_target_pairs={{0,64},{16,80},{32,96},{48,112},{64,0},{80,16},{96,32},{112,48},{1... | collective-permute-start | bytes 172040 | tf_op jit(solution)/shard_map/ppermute | solution.py:475
  106.8 1.0 collective-permute-start.19
  107.8 1.6 collective-permute-done.18
  109.4 0.7 collective-permute-done.19
  110.1 0.3 fusion
  110.4 0.5 multiply_reduce_fusion
  110.9 0.1 multiply_convert_fusion
  111.1 1.2 fusion.5
  112.3 56.1 %all_to_all.28 = bf16[128,8,1792]{2,1,0:T(8,128)(2,1)S(1)} all-to-all(bf16[128,8,1792]{2,1,0:T(8,128)(2,1)S(1)} %fusion.5), channel_id=1, replica_groups=mesh['rep'=8,'ep_0'=4,'ep_1'=4] {'rep','ep_0','ep_1'}, dimensions={0} | all-to-all | bytes 7340032 | tf_op jit(solution)/shard_map/all_to_all | solution.py:569
  168.4 11.9 %expert.1 = bf16[1024,1792]{1,0:T(8,128)(2,1)} custom-call(bf16[1024,1792]{1,0:T(8,128)(2,1)S(1)} %bitcast.42, bf16[1,3584,1024]{2,1,0:T(8,128)(2,1)S(1)} %bitcast.45, bf16[1,1024,3584]{2,1,0:T(8,128)(2,1)} %out_hbm.1), custom_call_target="tpu_custom_call" | custom-call | flops 8589934592 | bytes 23068672 | tf_op jit(solution)/shard_map/expert/pallas_call | solution.py:412
  180.3 4.7 %all-to-all-start.2 = ((bf16[128,8,1792]{2,1,0:T(8,128)(2,1)}), bf16[128,8,1792]{2,1,0:T(8,128)(2,1)}, u32[]{:S(2)}, u32[]{:S(2)}) async-start(bf16[128,8,1792]{2,1,0:T(8,128)(2,1)} %bitcast.46), calls=%async_computation.2 | async-start | bytes 7340032 | tf_op jit(solution)/shard_map/all_to_all | solution.py:571
  185.2 0.4 fusion.6
  185.5 0.1 reduce-precision_convert_fusion
  185.7 46.0 %all-to-all-done.2 = bf16[128,8,1792]{2,1,0:T(8,128)(2,1)} async-done(((bf16[128,8,1792]{2,1,0:T(8,128)(2,1)}), bf16[128,8,1792]{2,1,0:T(8,128)(2,1)}, u32[]{:S(2)}, u32[]{:S(2)}) %all-to-all-start.2) | async-done | bytes 3670048 | tf_op jit(solution)/shard_map/all_to_all | solution.py:571
  231.7 2.7 %fusion.3 = f32[128,1792]{1,0:T(8,128)S(1)} fusion(bf16[128,8,1792]{2,1,0:T(8,128)(2,1)} %all-to-all-done.2, bf16[64,1024]{1,0:T(8,128)(2,1)S(1)} %get-tuple-element.60, bf16[64,1024]{1,0:T(8,128)(2,1)S(1)} %get-tuple-element.59), kind=kOutput, calls=%fused_computation.8 | convolution fusion | flops 470286336 | bytes 4849664 | tf_op jit(solution)/shard_map/dot_general | solution.py:46
  234.5 0.8 fusion.15
  (68 shorter events, 1.4 us)
Async XLA Ops:
  0.6 0.7 copy-start
  2.8 23.6 %collective-permute-start = (bf16[8,3584]{1,0:T(8,128)(2,1)S(1)}, bf16[8,3584]{1,0:T(8,128)(2,1)S(1)}, u32[]{:S(2)}, u32[]{:S(2)}) collective-permute-start(bf16[8,3584]{1,0:T(8,128)(2,1)S(1)} %convolution_convert_fusion.2), channel_id=1, source_target_pairs={{0,16},{16,0},{32,48},{48,32},{64,80},{80,64},{96,112},{112,96},{1... | collective-permute-start | bytes 172040 | tf_op jit(solution)/shard_map/ppermute | solution.py:479
  16.7 7.1 %copy-start.7 = (s32[1,2]{1,0:T(1,128)S(1)}, s32[1,2]{1,0:T(1,128)}, u32[]{:S(2)}) copy-start(s32[1,2]{1,0:T(1,128)} %param.25) | copy-start | bytes 28
  16.7 7.3 %copy-start.3 = (s32[32,8]{0,1:T(8,128)S(1)}, s32[32,8]{0,1:T(8,128)}, u32[]{:S(2)}) copy-start(s32[32,8]{0,1:T(8,128)} %param.26) | copy-start | bytes 3076
  16.7 7.5 %copy-start.1 = (s32[128]{0:T(128)S(1)}, s32[128]{0:T(128)}, u32[]{:S(2)}) copy-start(s32[128]{0:T(128)} %param.28) | copy-start | bytes 1540
  16.7 15.4 %copy-start.5 = (s32[64]{0:T(128)S(1)}, s32[64]{0:T(128)}, u32[]{:S(2)}) copy-start(s32[64]{0:T(128)} %constant.136.clone) | copy-start | bytes 772
  16.7 15.4 %copy-start.6 = (s32[64]{0:T(128)S(1)}, s32[64]{0:T(128)}, u32[]{:S(2)}) copy-start(s32[64]{0:T(128)} %constant.137.clone) | copy-start | bytes 772
  16.7 36.3 %all-to-all-start = ((bf16[16,128,512]{2,1,0:T(8,128)(2,1)}), bf16[16,128,512]{2,1,0:T(8,128)(2,1)S(1)}, u32[]{:S(2)}, u32[]{:S(2)}) async-start(bf16[16,128,512]{2,1,0:T(8,128)(2,1)} %attention.1), calls=%async_computation | async-start | bytes 4194304 | tf_op jit(solution)/shard_map/all_to_all | solution.py:513
  26.5 5.7 %collective-permute-start.1 = (bf16[8,3584]{1,0:T(8,128)(2,1)S(1)}, bf16[8,3584]{1,0:T(8,128)(2,1)S(1)}, u32[]{:S(2)}, u32[]{:S(2)}) collective-permute-start(bf16[8,3584]{1,0:T(8,128)(2,1)S(1)} %broadcast_select_fusion.1), channel_id=1, source_target_pairs={{0,32},{16,48},{32,64},{48,80},{64,96},{80,112},{96,0},{112,16},{1... | collective-permute-start | bytes 172040 | tf_op jit(solution)/shard_map/ppermute | solution.py:475
  28.1 6.3 %collective-permute-start.2 = (bf16[8,3584]{1,0:T(8,128)(2,1)S(1)}, bf16[8,3584]{1,0:T(8,128)(2,1)S(1)}, u32[]{:S(2)}, u32[]{:S(2)}) collective-permute-start(bf16[8,3584]{1,0:T(8,128)(2,1)S(1)} %broadcast_select_fusion.1), channel_id=1, source_target_pairs={{0,64},{16,80},{32,96},{48,112},{64,0},{80,16},{96,32},{112,48},{1... | collective-permute-start | bytes 172040 | tf_op jit(solution)/shard_map/ppermute | solution.py:475
  31.4 3.3 %collective-permute-start.3 = (bf16[8,3584]{1,0:T(8,128)(2,1)S(1)}, bf16[8,3584]{1,0:T(8,128)(2,1)S(1)}, u32[]{:S(2)}, u32[]{:S(2)}) collective-permute-start(bf16[8,3584]{1,0:T(8,128)(2,1)S(1)} %broadcast_select_fusion.1), channel_id=1, source_target_pairs={{0,96},{16,112},{32,0},{48,16},{64,32},{80,48},{96,64},{112,80},{1... | collective-permute-start | bytes 172040 | tf_op jit(solution)/shard_map/ppermute | solution.py:475
  58.0 10.7 %collective-permute-start.4 = (bf16[256,896]{1,0:T(8,128)(2,1)}, bf16[256,896]{1,0:T(8,128)(2,1)S(1)}, u32[]{:S(2)}, u32[]{:S(2)}) collective-permute-start(bf16[256,896]{1,0:T(8,128)(2,1)} %get-tuple-element.24), channel_id=1, source_target_pairs={{0,4},{4,0},{8,12},{12,8},{1,5},{5,1},{9,13},{13,9},{2,6},{6,2},{1... | collective-permute-start | bytes 1376264 | tf_op jit(solution)/shard_map/ppermute | solution.py:462
  58.1 11.3 %collective-permute-start.5 = (bf16[256,896]{1,0:T(8,128)(2,1)}, bf16[256,896]{1,0:T(8,128)(2,1)S(1)}, u32[]{:S(2)}, u32[]{:S(2)}) collective-permute-start(bf16[256,896]{1,0:T(8,128)(2,1)} %get-tuple-element.25), channel_id=1, source_target_pairs={{0,12},{12,0},{4,8},{8,4},{1,13},{13,1},{5,9},{9,5},{2,14},{14,2},... | collective-permute-start | bytes 1376264 | tf_op jit(solution)/shard_map/ppermute | solution.py:462
  60.2 9.9 %collective-permute-start.6 = (bf16[256,896]{1,0:T(8,128)(2,1)}, bf16[256,896]{1,0:T(8,128)(2,1)S(1)}, u32[]{:S(2)}, u32[]{:S(2)}) collective-permute-start(bf16[256,896]{1,0:T(8,128)(2,1)} %get-tuple-element.26), channel_id=1, source_target_pairs={{0,1},{1,0},{2,3},{3,2},{4,5},{5,4},{6,7},{7,6},{8,9},{9,8},{10,11... | collective-permute-start | bytes 1376264 | tf_op jit(solution)/shard_map/ppermute | solution.py:462
  60.2 11.5 %collective-permute-start.7 = (bf16[256,896]{1,0:T(8,128)(2,1)}, bf16[256,896]{1,0:T(8,128)(2,1)S(1)}, u32[]{:S(2)}, u32[]{:S(2)}) collective-permute-start(bf16[256,896]{1,0:T(8,128)(2,1)} %get-tuple-element.27), channel_id=1, source_target_pairs={{0,3},{3,0},{1,2},{2,1},{4,7},{7,4},{5,6},{6,5},{8,11},{11,8},{9,1... | collective-permute-start | bytes 1376264 | tf_op jit(solution)/shard_map/ppermute | solution.py:462
  72.1 6.6 %collective-permute-start.10 = (bf16[128,896]{1,0:T(8,128)(2,1)S(1)}, bf16[128,896]{1,0:T(8,128)(2,1)S(1)}, u32[]{:S(2)}, u32[]{:S(2)}) collective-permute-start(bf16[128,896]{1,0:T(8,128)(2,1)S(1)} %get-tuple-element.31), channel_id=1, source_target_pairs={{0,3},{3,0},{1,2},{2,1},{4,7},{7,4},{5,6},{6,5},{8,11},{11,8},{9,1... | collective-permute-start | bytes 688136 | tf_op jit(solution)/shard_map/ppermute | solution.py:462
  75.3 5.2 %collective-permute-start.11 = (bf16[128,896]{1,0:T(8,128)(2,1)S(1)}, bf16[128,896]{1,0:T(8,128)(2,1)S(1)}, u32[]{:S(2)}, u32[]{:S(2)}) collective-permute-start(bf16[128,896]{1,0:T(8,128)(2,1)S(1)} %get-tuple-element.32), channel_id=1, source_target_pairs={{0,1},{1,0},{2,3},{3,2},{4,5},{5,4},{6,7},{7,6},{8,9},{9,8},{10,11... | collective-permute-start | bytes 688136 | tf_op jit(solution)/shard_map/ppermute | solution.py:462
  75.3 6.4 %collective-permute-start.8 = (bf16[128,896]{1,0:T(8,128)(2,1)S(1)}, bf16[128,896]{1,0:T(8,128)(2,1)S(1)}, u32[]{:S(2)}, u32[]{:S(2)}) collective-permute-start(bf16[128,896]{1,0:T(8,128)(2,1)S(1)} %get-tuple-element.29), channel_id=1, source_target_pairs={{0,12},{12,0},{4,8},{8,4},{1,13},{13,1},{5,9},{9,5},{2,14},{14,2},... | collective-permute-start | bytes 688136 | tf_op jit(solution)/shard_map/ppermute | solution.py:462
  76.4 5.2 %collective-permute-start.9 = (bf16[128,896]{1,0:T(8,128)(2,1)S(1)}, bf16[128,896]{1,0:T(8,128)(2,1)S(1)}, u32[]{:S(2)}, u32[]{:S(2)}) collective-permute-start(bf16[128,896]{1,0:T(8,128)(2,1)S(1)} %get-tuple-element.30), channel_id=1, source_target_pairs={{0,4},{4,0},{8,12},{12,8},{1,5},{5,1},{9,13},{13,9},{2,6},{6,2},{1... | collective-permute-start | bytes 688136 | tf_op jit(solution)/shard_map/ppermute | solution.py:462
  81.7 29.3 %copy-start.2 = (f32[3584]{0:T(1024)S(1)}, f32[3584]{0:T(1024)}, u32[]{:S(2)}) copy-start(f32[3584]{0:T(1024)} %param.29) | copy-start | bytes 43012
  81.8 5.0 %collective-permute-start.12 = (bf16[64,1792]{1,0:T(8,128)(2,1)S(1)}, bf16[64,1792]{1,0:T(8,128)(2,1)S(1)}, u32[]{:S(2)}, u32[]{:S(2)}) collective-permute-start(bf16[64,1792]{1,0:T(8,128)(2,1)S(1)} %get-tuple-element.34), channel_id=1, source_target_pairs={{0,1},{1,0},{2,3},{3,2},{4,5},{5,4},{6,7},{7,6},{8,9},{9,8},{10,11... | collective-permute-start | bytes 688136 | tf_op jit(solution)/shard_map/ppermute | solution.py:462
  83.3 4.9 %collective-permute-start.13 = (bf16[64,1792]{1,0:T(8,128)(2,1)S(1)}, bf16[64,1792]{1,0:T(8,128)(2,1)S(1)}, u32[]{:S(2)}, u32[]{:S(2)}) collective-permute-start(bf16[64,1792]{1,0:T(8,128)(2,1)S(1)} %get-tuple-element.35), channel_id=1, source_target_pairs={{0,4},{4,0},{8,12},{12,8},{1,5},{5,1},{9,13},{13,9},{2,6},{6,2},{1... | collective-permute-start | bytes 688136 | tf_op jit(solution)/shard_map/ppermute | solution.py:462
  88.2 4.9 %collective-permute-start.14 = (bf16[32,1792]{1,0:T(8,128)(2,1)S(1)}, bf16[32,1792]{1,0:T(8,128)(2,1)S(1)}, u32[]{:S(2)}, u32[]{:S(2)}) collective-permute-start(bf16[32,1792]{1,0:T(8,128)(2,1)S(1)} %get-tuple-element.37), channel_id=1, source_target_pairs={{0,3},{3,0},{1,2},{2,1},{4,7},{7,4},{5,6},{6,5},{8,11},{11,8},{9,1... | collective-permute-start | bytes 344072 | tf_op jit(solution)/shard_map/ppermute | solution.py:462
  88.4 4.9 %collective-permute-start.15 = (bf16[32,1792]{1,0:T(8,128)(2,1)S(1)}, bf16[32,1792]{1,0:T(8,128)(2,1)S(1)}, u32[]{:S(2)}, u32[]{:S(2)}) collective-permute-start(bf16[32,1792]{1,0:T(8,128)(2,1)S(1)} %get-tuple-element.38), channel_id=1, source_target_pairs={{0,12},{12,0},{4,8},{8,4},{1,13},{13,1},{5,9},{9,5},{2,14},{14,2},... | collective-permute-start | bytes 344072 | tf_op jit(solution)/shard_map/ppermute | solution.py:462
  93.4 8.4 %collective-permute-start.16 = (bf16[8,3584]{1,0:T(8,128)(2,1)S(1)}, bf16[8,3584]{1,0:T(8,128)(2,1)S(1)}, u32[]{:S(2)}, u32[]{:S(2)}) collective-permute-start(bf16[8,3584]{1,0:T(8,128)(2,1)S(1)} %get-tuple-element.39), channel_id=1, source_target_pairs={{0,16},{16,0},{32,48},{48,32},{64,80},{80,64},{96,112},{112,96},{1... | collective-permute-start | bytes 172040 | tf_op jit(solution)/shard_map/ppermute | solution.py:479
  101.9 5.9 %collective-permute-start.17 = (bf16[8,3584]{1,0:T(8,128)(2,1)S(1)}, bf16[8,3584]{1,0:T(8,128)(2,1)S(1)}, u32[]{:S(2)}, u32[]{:S(2)}) collective-permute-start(bf16[8,3584]{1,0:T(8,128)(2,1)S(1)} %broadcast_select_fusion), channel_id=1, source_target_pairs={{0,32},{16,48},{32,64},{48,80},{64,96},{80,112},{96,0},{112,16},{1... | collective-permute-start | bytes 172040 | tf_op jit(solution)/shard_map/ppermute | solution.py:475
  103.6 5.8 %collective-permute-start.18 = (bf16[8,3584]{1,0:T(8,128)(2,1)S(1)}, bf16[8,3584]{1,0:T(8,128)(2,1)S(1)}, u32[]{:S(2)}, u32[]{:S(2)}) collective-permute-start(bf16[8,3584]{1,0:T(8,128)(2,1)S(1)} %broadcast_select_fusion), channel_id=1, source_target_pairs={{0,64},{16,80},{32,96},{48,112},{64,0},{80,16},{96,32},{112,48},{1... | collective-permute-start | bytes 172040 | tf_op jit(solution)/shard_map/ppermute | solution.py:475
  106.8 3.3 %collective-permute-start.19 = (bf16[8,3584]{1,0:T(8,128)(2,1)S(1)}, bf16[8,3584]{1,0:T(8,128)(2,1)S(1)}, u32[]{:S(2)}, u32[]{:S(2)}) collective-permute-start(bf16[8,3584]{1,0:T(8,128)(2,1)S(1)} %broadcast_select_fusion), channel_id=1, source_target_pairs={{0,96},{16,112},{32,0},{48,16},{64,32},{80,48},{96,64},{112,80},{1... | collective-permute-start | bytes 172040 | tf_op jit(solution)/shard_map/ppermute | solution.py:475
  110.1 58.3 %slice-start = ((s8[7340032]{0:T(1024)(128)(4,1)}), s8[4194304]{0:T(1024)(128)(4,1)S(1)}, s32[]{:S(2)}) async-start(s8[7340032]{0:T(1024)(128)(4,1)} %bitcast.44), calls=%async_computation.3 | async-start | bytes 8388608
  111.1 57.3 %slice-start.1 = ((s8[7340032]{0:T(1024)(128)(4,1)}), s8[3145728]{0:T(1024)(128)(4,1)S(1)}, s32[]{:S(2)}) async-start(s8[7340032]{0:T(1024)(128)(4,1)} %bitcast.44), calls=%async_computation.4 | async-start | bytes 6291456
  180.3 4.8 %copy-start.4 = (f32[32,8]{0,1:T(8,128)S(1)}, f32[32,8]{0,1:T(8,128)}, u32[]{:S(2)}) copy-start(f32[32,8]{0,1:T(8,128)} %param.27) | copy-start | bytes 3076
  180.3 51.4 %all-to-all-start.2 = ((bf16[128,8,1792]{2,1,0:T(8,128)(2,1)}), bf16[128,8,1792]{2,1,0:T(8,128)(2,1)}, u32[]{:S(2)}, u32[]{:S(2)}) async-start(bf16[128,8,1792]{2,1,0:T(8,128)(2,1)} %bitcast.46), calls=%async_computation.2 | async-start | bytes 7340032 | tf_op jit(solution)/shard_map/all_to_all | solution.py:571

commit v4 on v3

--- a/solution.py
+++ b/solution.py
@@ -309,27 +309,30 @@
     return *sent, kept
 
 
-def add_body(rows, split_at, joined, kept_ref, *rest):
-    came, send, stay = rest[:split_at], rest[split_at:-1], rest[-1]
-    split = 4 // split_at
+def add_body(spread, kept_ref, *rest):
+    came, send, stay = rest[:4], rest[4:-1], rest[-1]
     for band in range(4):
-        piece = came[band // split]
-        columns = slice(band % split * BAND, (band % split + 1) * BAND)
-        total = kept_ref[band].astype(F32) + piece[:, columns].astype(F32)
+        total = kept_ref[band].astype(F32) + came[band][...].astype(F32)
+        rows = stay.shape[1]
         stay[band] = total[:rows]
-        if joined:
-            send[band // 2][:, band % 2 * BAND : (band % 2 + 1) * BAND] = total[rows:].astype(BF)
+        if spread:
+            columns = slice(band % 2 * BAND, (band % 2 + 1) * BAND)
+            for place in range(1, 4):
+                send[band // 2 * 3 + place - 1][:, columns] = total[
+                    place * rows : (place + 1) * rows
+                ].astype(BF)
         else:
             send[band][...] = total[rows:].astype(BF)
 
 
-def add_pieces(kept, came, joined):
-    rows = kept.shape[1] // 2
-    shape, count = ((rows, 2 * BAND), 2) if joined else ((rows, BAND), 4)
+def add_pieces(kept, came, spread):
+    parts = 4 if spread else 2
+    rows = kept.shape[1] // parts
+    shape, count = ((rows, 2 * BAND), 6) if spread else ((rows, BAND), 4)
     whole = pl.BlockSpec(memory_space=pltpu.VMEM)
     outs = pl.pallas_call(
-        functools.partial(add_body, rows, len(came), joined),
-        in_specs=[whole] * (1 + len(came)),
+        functools.partial(add_body, spread),
+        in_specs=[whole] * 5,
         out_specs=[whole] * (count + 1),
         out_shape=[jax.ShapeDtypeStruct(shape, BF)] * count
         + [jax.ShapeDtypeStruct((4, rows, BAND), F32)],
@@ -342,20 +345,23 @@
     return outs[:-1], outs[-1]
 
 
-def finish_body(pick_ref, kept_ref, first_ref, second_ref, own_ref, offer_ref):
+def finish_body(pick_ref, kept_ref, *rest):
+    came, own_ref, offer_ref = rest[:6], rest[6], rest[7]
     for band in range(4):
-        piece = (first_ref, second_ref)[band // 2]
         columns = slice(band % 2 * BAND, (band % 2 + 1) * BAND)
-        total = (kept_ref[band] + piece[:, columns].astype(F32)).astype(BF)
+        total = kept_ref[band]
+        for piece in came[band // 2 * 3 : band // 2 * 3 + 3]:
+            total = total + piece[:, columns].astype(F32)
+        total = total.astype(BF)
         own_ref[:, band * BAND : (band + 1) * BAND] = total
         offer_ref[:, band * BAND : (band + 1) * BAND] = mm(pick_ref[...], total).astype(BF)
 
 
-def finish(pick, kept, first, second):
+def finish(pick, kept, came):
     whole = pl.BlockSpec(memory_space=pltpu.VMEM)
     return pl.pallas_call(
         finish_body,
-        in_specs=[whole] * 4,
+        in_specs=[whole] * 8,
         out_specs=[whole] * 2,
         out_shape=[
             jax.ShapeDtypeStruct((TOK_DEV, D), BF),
@@ -364,7 +370,7 @@
         compiler_params=pltpu.CompilerParams(vmem_limit_bytes=4 << 20),
         cost_estimate=pl.CostEstimate(flops=4 << 20, bytes_accessed=1 << 20, transcendentals=0),
         name="finish",
-    )(near(pick), near(kept), near(first), near(second))
+    )(near(pick), near(kept), *[near(piece) for piece in came])
 
 
 def expert_body(x_ref, in_ref, out_hbm, o_hbm, x_s, h_s, o_ref, out_ref, sems, out_sem):
@@ -432,7 +438,7 @@
 
 NEAR = [(0, 1), (1, 0), (2, 3), (3, 2)]
 FAR = [(0, 3), (3, 0), (1, 2), (2, 1)]
-PAIRS = {1: NEAR, 3: FAR}
+PAIRS = {1: NEAR, 3: FAR, 2: [(0, 2), (2, 0), (1, 3), (3, 1)]}
 ROUTES = (
     (("ep_0", 1), ("ep_0", 3), ("ep_1", 1), ("ep_1", 3)),
     (("ep_0", 3), ("ep_0", 1), ("ep_1", 1), ("ep_1", 3)),
@@ -455,19 +461,24 @@
 
 
 def exchange(pieces, step):
-    every = 4 // len(pieces)
     out = []
-    for at, piece in enumerate(pieces):
-        axis, flip = ROUTES[at * every][step]
+    for band, piece in enumerate(pieces):
+        axis, flip = ROUTES[band][step]
         out.append(lax.ppermute(piece, axis, PAIRS[flip]))
     return out
 
 
 def sum_over_columns(pick, parts):
     *send, kept = parts
-    for step in range(3):
-        send, kept = add_pieces(kept, exchange(send, step), joined=step > 0)
-    return finish(pick, kept, *exchange(send, 3))
+    for step in range(2):
+        send, kept = add_pieces(kept, exchange(send, step), spread=step > 0)
+    came = []
+    for at, piece in enumerate(send):
+        axis, third = ROUTES[at // 3 * 2][2]
+        _, last = ROUTES[at // 3 * 2][3]
+        flip = (last, third, third ^ last)[at % 3]
+        came.append(lax.ppermute(piece, axis, PAIRS[flip]))
+    return finish(pick, kept, came)
 
 
 def shifted(value, axis, steps):

time: 236 us -> 241 us (1.021)
  waiting for transfers between devices: 87.4 us -> 79.6 us
  local copies, waits for them, and re-layouts: 4.65 us -> 11.4 us
  other arithmetic: 2.72 us -> 6.2 us
  blocking collectives: 56.1 us -> 53.4 us
  starting transfers between devices: 44.8 us -> 47.4 us
    ppermute x12 -> x8, waiting for transfers between devices: 17.3 us -> 6.99 us  [exchange(): out.append(lax.ppermute(piece, axis, PAIRS[flip]))]
    ppermute x0 -> x6, starting transfers between devices: none -> 7.8 us  [sum_over_columns(): came.append(lax.ppermute(piece, axis, PAIRS[flip]))]
    unnamed x23 -> x49, local copies, waits for them, and re-layouts: 0.87 us -> 6.98 us
    ppermute x0 -> x6, waiting for transfers between devices: none -> 3.29 us  [sum_over_columns(): came.append(lax.ppermute(piece, axis, PAIRS[flip]))]
    ppermute x12 -> x8, starting transfers between devices: 12.6 us -> 9.46 us  [exchange(): out.append(lax.ppermute(piece, axis, PAIRS[flip]))]
    all_to_all x1, blocking collectives: 56.1 us -> 53.4 us  [per_device(): lax.all_to_all(outgoing, REP_EP, split_axis=0, concat_axis=0, tiled=True)]
  transfers between devices with their start and end apart: 22 -> 24, of which waited for: 19 -> 17; matrix products, arithmetic and copies ran while one was open for 2% -> 4% of each run, Pallas kernels for 7% -> 7%
where the time goes in v4:
time: 241 us; the launch traced here: 240 us
  waiting for transfers between devices  79.6 us (33%)
  blocking collectives  53.4 us (22%)
  starting transfers between devices  47.4 us (20%)
  Pallas kernels  34.7 us (14%)
  local copies, waits for them, and re-layouts  11.4 us (5%)
  other arithmetic  6.2 us (3%)
  matrix products  6.09 us (3%)
    all_to_all x1, blocking collectives, per_device(): lax.all_to_all(outgoing, REP_EP, split_axis=0, concat_axis=0, tiled=True)  53.4 us
    all_to_all x1, waiting for transfers between devices, per_device(): lax.all_to_all(outer, REP_EP, split_axis=0, concat_axis=0, tiled=True)  46 us
    all_to_all x1, waiting for transfers between devices, per_device(): latent = lax.all_to_all(latent, EP, split_axis=0, concat_axis=0, tiled=True)  17 us
    pallas_call x1, Pallas kernels, attention(): pl.pallas_call(attention_body, in_specs=[few, few, few, far, far], out_sp...  12.4 us
    pallas_call x1, Pallas kernels, expert(): pl.pallas_call(expert_body, in_specs=[whole, whole, far], out_specs=far,...  11.8 us
    ppermute x6, starting transfers between devices, shifted(): lax.ppermute(value, axis, [(s, (s + steps) % count) for s in range(count)])  10.9 us
    ppermute x8, starting transfers between devices, exchange(): out.append(lax.ppermute(piece, axis, PAIRS[flip]))  9.46 us
    ppermute x6, starting transfers between devices, sum_over_columns(): came.append(lax.ppermute(piece, axis, PAIRS[flip]))  7.8 us
  transfers between devices with their start and end apart: 24, of which 17 were waited for; matrix products, arithmetic and copies ran while one was open for 4% of the time, Pallas kernels for 7%

profile of v4, /device:TPU:1, one launch (start us, length us, event | category | flops | bytes accessed | tf_op | source)
XLA Modules:
  0.0 240.0 jit_solution(10641473880514006294)
XLA Ops:
  0.7 0.7 copy-done
  1.7 0.9 fusion.67
  2.6 0.6 copy-done.9
  3.4 1.5 collective-permute-start
  4.9 12.4 %attention.1 = bf16[16,128,512]{2,1,0:T(8,128)(2,1)} custom-call(s32[1,48]{1,0:T(1,128)} %pick_ref.1, s32[8,1,8]{2,1,0:T(1,128)} %count_ref.1, s32[8,1,8]{2,1,0:T(1,128)} %fill_ref.1, bf16[8,147456]{1,0:T(8,128)(2,1)} %query_hbm.1, bf16[48,36864]{1,0:T(8,128)(2,1)} %page_hbm.1), custom_call_target="tpu_custom_call" | custom-call | flops 7516192768 | bytes 8388608 | tf_op jit(solution)/shard_map/attention/pallas_call | solution.py:181
  17.3 7.1 %all-to-all-start = ((bf16[16,128,512]{2,1,0:T(8,128)(2,1)}), bf16[16,128,512]{2,1,0:T(8,128)(2,1)S(1)}, u32[]{:S(2)}, u32[]{:S(2)}) async-start(bf16[16,128,512]{2,1,0:T(8,128)(2,1)} %attention.1), calls=%async_computation | async-start | bytes 4194304 | tf_op jit(solution)/shard_map/all_to_all | solution.py:524
  24.8 1.9 gather_fusion
  26.8 0.9 fusion.26
  27.7 1.6 collective-permute-start.1
  29.4 3.3 %collective-permute-start.2 = (bf16[8,3584]{1,0:T(8,128)(2,1)S(1)}, bf16[8,3584]{1,0:T(8,128)(2,1)S(1)}, u32[]{:S(2)}, u32[]{:S(2)}) collective-permute-start(bf16[8,3584]{1,0:T(8,128)(2,1)S(1)} %broadcast_select_fusion.1), channel_id=1, source_target_pairs={{0,64},{16,80},{32,96},{48,112},{64,0},{80,16},{96,32},{112,48},{1... | collective-permute-start | bytes 172040 | tf_op jit(solution)/shard_map/ppermute | solution.py:486
  32.6 0.7 collective-permute-start.3
  33.5 2.1 collective-permute-done.2
  35.6 0.4 collective-permute-done.3
  36.0 0.7 pad_maximum_fusion.2
  36.7 17.0 %all-to-all-done = bf16[16,128,512]{2,1,0:T(8,128)(2,1)S(1)} async-done(((bf16[16,128,512]{2,1,0:T(8,128)(2,1)}), bf16[16,128,512]{2,1,0:T(8,128)(2,1)S(1)}, u32[]{:S(2)}, u32[]{:S(2)}) %all-to-all-start) | async-done | bytes 2097184 | tf_op jit(solution)/shard_map/all_to_all | solution.py:524
  53.6 5.0 %project_sent.1 = (bf16[256,896]{1,0:T(8,128)(2,1)}, bf16[256,896]{1,0:T(8,128)(2,1)}, bf16[256,896]{1,0:T(8,128)(2,1)}, bf16[256,896]{1,0:T(8,128)(2,1)}, bf16[16,32,512]{2,1,0:T(8,128)(2,1)S(1)}) custom-call(s32[64]{0:T(128)S(1)} %xor_add_fusion.order_ref, bf16[8,256,512]{2,1,0:T(8,128)(2,1)S(1)} %bitcast.43, bf16[4,512,128]{2,1,0:T(8,128)(2,1)} %up_hbm.1, ...), custom_call_target="tpu_custom_call" | custom-call | flops 2147483648 | bytes 8388608 | tf_op jit(solution)/shard_map/project_sent/pallas_call | solution.py:273
  58.7 2.1 collective-permute-start.5
  60.8 3.1 %collective-permute-start.7 = (bf16[256,896]{1,0:T(8,128)(2,1)}, bf16[256,896]{1,0:T(8,128)(2,1)S(1)}, u32[]{:S(2)}, u32[]{:S(2)}) collective-permute-start(bf16[256,896]{1,0:T(8,128)(2,1)} %get-tuple-element.28), channel_id=1, source_target_pairs={{0,3},{3,0},{1,2},{2,1},{4,7},{7,4},{5,6},{6,5},{8,11},{11,8},{9,1... | collective-permute-start | bytes 1376264 | tf_op jit(solution)/shard_map/ppermute | solution.py:467
  63.9 0.7 slice_bitcast_fusion
  64.6 0.9 broadcast_add_fusion
  65.7 3.6 %project_kept.1.kept_ref = bf16[4,256,896]{2,1,0:T(8,128)(2,1)S(1)} custom-call(s32[64]{0:T(128)S(1)} %xor_add_fusion.order_ref, bf16[16,32,512]{2,1,0:T(8,128)(2,1)S(1)} %get-tuple-element.24.lifted_ref, bf16[512,3584]{1,0:T(8,128)(2,1)} %weight_hbm.3), custom_call_target="tpu_custom_call" | custom-call | flops 1073741824 | bytes 6291456 | tf_op jit(solution)/shard_map/project_kept/pallas_call | solution.py:293
  69.3 0.7 collective-permute-done.5.rest_1_
  70.0 0.7 collective-permute-done.6.rest_2_
  70.7 0.8 copy-done.1
  71.5 0.8 collective-permute-done.7.rest_3_
  72.3 0.8 copy-done.3
  73.1 1.0 copy-done.2
  74.1 1.0 copy-done.4
  75.1 1.0 add_pieces.2
  76.1 3.1 %collective-permute-start.10 = (bf16[128,896]{1,0:T(8,128)(2,1)}, bf16[128,896]{1,0:T(8,128)(2,1)S(1)}, u32[]{:S(2)}, u32[]{:S(2)}) collective-permute-start(bf16[128,896]{1,0:T(8,128)(2,1)} %get-tuple-element.32), channel_id=1, source_target_pairs={{0,3},{3,0},{1,2},{2,1},{4,7},{7,4},{5,6},{6,5},{8,11},{11,8},{9,1... | collective-permute-start | bytes 688136 | tf_op jit(solution)/shard_map/ppermute | solution.py:467
  79.2 1.1 collective-permute-start.8
  80.4 0.7 iota_compare_fusion.1
  81.1 1.8 collective-permute-done.10.rest_2_
  82.8 1.8 collective-permute-done.11.rest_3_
  84.6 1.2 collective-permute-done.8.rest_0_
  85.8 0.8 add_pieces.3
  86.6 0.6 copy-done.5
  87.2 0.6 copy-done.6
  87.9 0.6 copy-done.7
  88.7 0.6 and_select_fusion.2
  89.6 1.3 collective-permute-start.13
  90.9 2.5 %collective-permute-start.14 = (bf16[32,1792]{1,0:T(8,128)(2,1)}, bf16[32,1792]{1,0:T(8,128)(2,1)S(1)}, u32[]{:S(2)}, u32[]{:S(2)}) collective-permute-start(bf16[32,1792]{1,0:T(8,128)(2,1)} %copy-done.6), channel_id=1, source_target_pairs={{0,2},{2,0},{1,3},{3,1},{4,6},{6,4},{5,7},{7,5},{8,10},{10,8},{9,1... | collective-permute-start | bytes 344072 | tf_op jit(solution)/shard_map/ppermute | solution.py:480
  93.4 1.5 collective-permute-start.15
  94.9 2.4 collective-permute-start.17
  97.3 0.4 compare_reduce_fusion
  97.7 0.9 collective-permute-done.15.rest_3_
  98.6 2.4 collective-permute-done.17.rest_5_
  101.2 6.0 %collective-permute-start.18 = (bf16[8,3584]{1,0:T(8,128)(2,1)S(1)}, bf16[8,3584]{1,0:T(8,128)(2,1)S(1)}, u32[]{:S(2)}, u32[]{:S(2)}) collective-permute-start(bf16[8,3584]{1,0:T(8,128)(2,1)S(1)} %get-tuple-element.41), channel_id=1, source_target_pairs={{0,16},{16,0},{32,48},{48,32},{64,80},{80,64},{96,112},{112,96},{1... | collective-permute-start | bytes 172040 | tf_op jit(solution)/shard_map/ppermute | solution.py:490
  107.2 0.9 collective-permute-done.18
  108.1 1.4 collective-permute-start.19
  109.5 3.4 %collective-permute-start.20 = (bf16[8,3584]{1,0:T(8,128)(2,1)S(1)}, bf16[8,3584]{1,0:T(8,128)(2,1)S(1)}, u32[]{:S(2)}, u32[]{:S(2)}) collective-permute-start(bf16[8,3584]{1,0:T(8,128)(2,1)S(1)} %broadcast_select_fusion), channel_id=1, source_target_pairs={{0,64},{16,80},{32,96},{48,112},{64,0},{80,16},{96,32},{112,48},{1... | collective-permute-start | bytes 172040 | tf_op jit(solution)/shard_map/ppermute | solution.py:486
  112.9 0.5 collective-permute-start.21
  113.7 1.8 collective-permute-done.20
  115.5 0.7 collective-permute-done.21
  116.2 0.3 fusion
  116.6 1.6 multiply_reduce_fusion
  118.4 1.2 fusion.5
  119.6 53.4 %all_to_all.28 = bf16[128,8,1792]{2,1,0:T(8,128)(2,1)S(1)} all-to-all(bf16[128,8,1792]{2,1,0:T(8,128)(2,1)S(1)} %fusion.5), channel_id=1, replica_groups=mesh['rep'=8,'ep_0'=4,'ep_1'=4] {'rep','ep_0','ep_1'}, dimensions={0} | all-to-all | bytes 7340032 | tf_op jit(solution)/shard_map/all_to_all | solution.py:580
  173.1 11.8 %expert.1 = bf16[1024,1792]{1,0:T(8,128)(2,1)} custom-call(bf16[1024,1792]{1,0:T(8,128)(2,1)S(1)} %bitcast.42, bf16[1,3584,1024]{2,1,0:T(8,128)(2,1)S(1)} %bitcast.45, bf16[1,1024,3584]{2,1,0:T(8,128)(2,1)} %out_hbm.1), custom_call_target="tpu_custom_call" | custom-call | flops 8589934592 | bytes 23068672 | tf_op jit(solution)/shard_map/expert/pallas_call | solution.py:418
  184.9 4.7 %all-to-all-start.2 = ((bf16[128,8,1792]{2,1,0:T(8,128)(2,1)}), bf16[128,8,1792]{2,1,0:T(8,128)(2,1)}, u32[]{:S(2)}, u32[]{:S(2)}) async-start(bf16[128,8,1792]{2,1,0:T(8,128)(2,1)} %bitcast.46), calls=%async_computation.2 | async-start | bytes 7340032 | tf_op jit(solution)/shard_map/all_to_all | solution.py:582
  189.7 0.4 fusion.6
  190.3 46.0 %all-to-all-done.2 = bf16[128,8,1792]{2,1,0:T(8,128)(2,1)} async-done(((bf16[128,8,1792]{2,1,0:T(8,128)(2,1)}), bf16[128,8,1792]{2,1,0:T(8,128)(2,1)}, u32[]{:S(2)}, u32[]{:S(2)}) %all-to-all-start.2) | async-done | bytes 3670048 | tf_op jit(solution)/shard_map/all_to_all | solution.py:582
  236.3 2.7 %fusion.3 = f32[128,1792]{1,0:T(8,128)S(1)} fusion(bf16[128,8,1792]{2,1,0:T(8,128)(2,1)} %all-to-all-done.2, bf16[64,1024]{1,0:T(8,128)(2,1)S(1)} %get-tuple-element.62, bf16[64,1024]{1,0:T(8,128)(2,1)S(1)} %get-tuple-element.61), kind=kOutput, calls=%fused_computation.8 | convolution fusion | flops 470286336 | bytes 4849664 | tf_op jit(solution)/shard_map/dot_general | solution.py:46
  239.2 0.8 fusion.15
  (97 shorter events, 3.2 us)
Async XLA Ops:
  0.6 0.7 copy-start
  1.7 15.6 %copy-start.18 = (s32[8]{0:T(128)}, s32[8]{0:T(128)S(1)}, u32[]{:S(2)}) copy-start(s32[8]{0:T(128)S(1)} %add.152) | copy-start | bytes 100
  2.6 0.6 copy-start.9
  2.6 0.8 copy-start.10
  2.6 0.8 copy-start.11
  2.6 0.8 copy-start.12
  3.4 24.2 %collective-permute-start = (bf16[8,3584]{1,0:T(8,128)(2,1)S(1)}, bf16[8,3584]{1,0:T(8,128)(2,1)S(1)}, u32[]{:S(2)}, u32[]{:S(2)}) collective-permute-start(bf16[8,3584]{1,0:T(8,128)(2,1)S(1)} %convolution_convert_fusion.2), channel_id=1, source_target_pairs={{0,16},{16,0},{32,48},{48,32},{64,80},{80,64},{96,112},{112,96},{1... | collective-permute-start | bytes 172040 | tf_op jit(solution)/shard_map/ppermute | solution.py:490
  17.3 7.1 %copy-start.19 = (s32[1,2]{1,0:T(1,128)S(1)}, s32[1,2]{1,0:T(1,128)}, u32[]{:S(2)}) copy-start(s32[1,2]{1,0:T(1,128)} %param.25) | copy-start | bytes 28
  17.3 7.3 %copy-start.14 = (s32[32,8]{0,1:T(8,128)S(1)}, s32[32,8]{0,1:T(8,128)}, u32[]{:S(2)}) copy-start(s32[32,8]{0,1:T(8,128)} %param.26) | copy-start | bytes 3076
  17.3 7.5 %copy-start.8 = (s32[128]{0:T(128)S(1)}, s32[128]{0:T(128)}, u32[]{:S(2)}) copy-start(s32[128]{0:T(128)} %param.28) | copy-start | bytes 1540
  17.3 16.0 %copy-start.16 = (s32[64]{0:T(128)S(1)}, s32[64]{0:T(128)}, u32[]{:S(2)}) copy-start(s32[64]{0:T(128)} %constant.136.clone) | copy-start | bytes 772
  17.3 16.0 %copy-start.17 = (s32[64]{0:T(128)S(1)}, s32[64]{0:T(128)}, u32[]{:S(2)}) copy-start(s32[64]{0:T(128)} %constant.137.clone) | copy-start | bytes 772
  17.3 36.3 %all-to-all-start = ((bf16[16,128,512]{2,1,0:T(8,128)(2,1)}), bf16[16,128,512]{2,1,0:T(8,128)(2,1)S(1)}, u32[]{:S(2)}, u32[]{:S(2)}) async-start(bf16[16,128,512]{2,1,0:T(8,128)(2,1)} %attention.1), calls=%async_computation | async-start | bytes 4194304 | tf_op jit(solution)/shard_map/all_to_all | solution.py:524
  24.6 4.8 %copy-start.20 = (s32[8]{0:T(128)}, s32[8]{0:T(128)S(1)}, u32[]{:S(2)}) copy-start(s32[8]{0:T(128)S(1)} %reshape.261) | copy-start | bytes 100
  27.7 5.7 %collective-permute-start.1 = (bf16[8,3584]{1,0:T(8,128)(2,1)S(1)}, bf16[8,3584]{1,0:T(8,128)(2,1)S(1)}, u32[]{:S(2)}, u32[]{:S(2)}) collective-permute-start(bf16[8,3584]{1,0:T(8,128)(2,1)S(1)} %broadcast_select_fusion.1), channel_id=1, source_target_pairs={{0,32},{16,48},{32,64},{48,80},{64,96},{80,112},{96,0},{112,16},{1... | collective-permute-start | bytes 172040 | tf_op jit(solution)/shard_map/ppermute | solution.py:486
  29.4 6.3 %collective-permute-start.2 = (bf16[8,3584]{1,0:T(8,128)(2,1)S(1)}, bf16[8,3584]{1,0:T(8,128)(2,1)S(1)}, u32[]{:S(2)}, u32[]{:S(2)}) collective-permute-start(bf16[8,3584]{1,0:T(8,128)(2,1)S(1)} %broadcast_select_fusion.1), channel_id=1, source_target_pairs={{0,64},{16,80},{32,96},{48,112},{64,0},{80,16},{96,32},{112,48},{1... | collective-permute-start | bytes 172040 | tf_op jit(solution)/shard_map/ppermute | solution.py:486
  32.6 3.3 %collective-permute-start.3 = (bf16[8,3584]{1,0:T(8,128)(2,1)S(1)}, bf16[8,3584]{1,0:T(8,128)(2,1)S(1)}, u32[]{:S(2)}, u32[]{:S(2)}) collective-permute-start(bf16[8,3584]{1,0:T(8,128)(2,1)S(1)} %broadcast_select_fusion.1), channel_id=1, source_target_pairs={{0,96},{16,112},{32,0},{48,16},{64,32},{80,48},{96,64},{112,80},{1... | collective-permute-start | bytes 172040 | tf_op jit(solution)/shard_map/ppermute | solution.py:486
  58.6 10.7 %collective-permute-start.4 = (bf16[256,896]{1,0:T(8,128)(2,1)}, bf16[256,896]{1,0:T(8,128)(2,1)S(1)}, u32[]{:S(2)}, u32[]{:S(2)}) collective-permute-start(bf16[256,896]{1,0:T(8,128)(2,1)} %get-tuple-element.25), channel_id=1, source_target_pairs={{0,4},{4,0},{8,12},{12,8},{1,5},{5,1},{9,13},{13,9},{2,6},{6,2},{1... | collective-permute-start | bytes 1376264 | tf_op jit(solution)/shard_map/ppermute | solution.py:467
  58.7 11.3 %collective-permute-start.5 = (bf16[256,896]{1,0:T(8,128)(2,1)}, bf16[256,896]{1,0:T(8,128)(2,1)S(1)}, u32[]{:S(2)}, u32[]{:S(2)}) collective-permute-start(bf16[256,896]{1,0:T(8,128)(2,1)} %get-tuple-element.26), channel_id=1, source_target_pairs={{0,12},{12,0},{4,8},{8,4},{1,13},{13,1},{5,9},{9,5},{2,14},{14,2},... | collective-permute-start | bytes 1376264 | tf_op jit(solution)/shard_map/ppermute | solution.py:467
  60.8 9.9 %collective-permute-start.6 = (bf16[256,896]{1,0:T(8,128)(2,1)}, bf16[256,896]{1,0:T(8,128)(2,1)S(1)}, u32[]{:S(2)}, u32[]{:S(2)}) collective-permute-start(bf16[256,896]{1,0:T(8,128)(2,1)} %get-tuple-element.27), channel_id=1, source_target_pairs={{0,1},{1,0},{2,3},{3,2},{4,5},{5,4},{6,7},{7,6},{8,9},{9,8},{10,11... | collective-permute-start | bytes 1376264 | tf_op jit(solution)/shard_map/ppermute | solution.py:467
  60.8 11.5 %collective-permute-start.7 = (bf16[256,896]{1,0:T(8,128)(2,1)}, bf16[256,896]{1,0:T(8,128)(2,1)S(1)}, u32[]{:S(2)}, u32[]{:S(2)}) collective-permute-start(bf16[256,896]{1,0:T(8,128)(2,1)} %get-tuple-element.28), channel_id=1, source_target_pairs={{0,3},{3,0},{1,2},{2,1},{4,7},{7,4},{5,6},{6,5},{8,11},{11,8},{9,1... | collective-permute-start | bytes 1376264 | tf_op jit(solution)/shard_map/ppermute | solution.py:467
  70.7 0.8 copy-start.1
  72.3 0.8 copy-start.3
  73.1 1.0 copy-start.2
  74.1 1.0 copy-start.4
  76.1 42.1 %copy-start.13 = (f32[3584]{0:T(1024)S(1)}, f32[3584]{0:T(1024)}, u32[]{:S(2)}) copy-start(f32[3584]{0:T(1024)} %param.29) | copy-start | bytes 43012
  76.1 6.7 %collective-permute-start.10 = (bf16[128,896]{1,0:T(8,128)(2,1)}, bf16[128,896]{1,0:T(8,128)(2,1)S(1)}, u32[]{:S(2)}, u32[]{:S(2)}) collective-permute-start(bf16[128,896]{1,0:T(8,128)(2,1)} %get-tuple-element.32), channel_id=1, source_target_pairs={{0,3},{3,0},{1,2},{2,1},{4,7},{7,4},{5,6},{6,5},{8,11},{11,8},{9,1... | collective-permute-start | bytes 688136 | tf_op jit(solution)/shard_map/ppermute | solution.py:467
  79.2 5.4 %collective-permute-start.11 = (bf16[128,896]{1,0:T(8,128)(2,1)}, bf16[128,896]{1,0:T(8,128)(2,1)S(1)}, u32[]{:S(2)}, u32[]{:S(2)}) collective-permute-start(bf16[128,896]{1,0:T(8,128)(2,1)} %get-tuple-element.33), channel_id=1, source_target_pairs={{0,1},{1,0},{2,3},{3,2},{4,5},{5,4},{6,7},{7,6},{8,9},{9,8},{10,11... | collective-permute-start | bytes 688136 | tf_op jit(solution)/shard_map/ppermute | solution.py:467
  79.2 6.6 %collective-permute-start.8 = (bf16[128,896]{1,0:T(8,128)(2,1)}, bf16[128,896]{1,0:T(8,128)(2,1)S(1)}, u32[]{:S(2)}, u32[]{:S(2)}) collective-permute-start(bf16[128,896]{1,0:T(8,128)(2,1)} %get-tuple-element.30), channel_id=1, source_target_pairs={{0,12},{12,0},{4,8},{8,4},{1,13},{13,1},{5,9},{9,5},{2,14},{14,2},... | collective-permute-start | bytes 688136 | tf_op jit(solution)/shard_map/ppermute | solution.py:467
  80.4 5.5 %collective-permute-start.9 = (bf16[128,896]{1,0:T(8,128)(2,1)}, bf16[128,896]{1,0:T(8,128)(2,1)S(1)}, u32[]{:S(2)}, u32[]{:S(2)}) collective-permute-start(bf16[128,896]{1,0:T(8,128)(2,1)} %get-tuple-element.31), channel_id=1, source_target_pairs={{0,4},{4,0},{8,12},{12,8},{1,5},{5,1},{9,13},{13,9},{2,6},{6,2},{1... | collective-permute-start | bytes 688136 | tf_op jit(solution)/shard_map/ppermute | solution.py:467
  86.6 0.6 copy-start.5
  87.2 0.6 copy-start.6
  87.9 0.6 copy-start.7
  88.5 6.3 %collective-permute-start.12 = (bf16[32,1792]{1,0:T(8,128)(2,1)}, bf16[32,1792]{1,0:T(8,128)(2,1)S(1)}, u32[]{:S(2)}, u32[]{:S(2)}) collective-permute-start(bf16[32,1792]{1,0:T(8,128)(2,1)} %get-tuple-element.35), channel_id=1, source_target_pairs={{0,3},{3,0},{1,2},{2,1},{4,7},{7,4},{5,6},{6,5},{8,11},{11,8},{9,1... | collective-permute-start | bytes 344072 | tf_op jit(solution)/shard_map/ppermute | solution.py:480
  89.6 8.1 %collective-permute-start.13 = (bf16[32,1792]{1,0:T(8,128)(2,1)}, bf16[32,1792]{1,0:T(8,128)(2,1)S(1)}, u32[]{:S(2)}, u32[]{:S(2)}) collective-permute-start(bf16[32,1792]{1,0:T(8,128)(2,1)} %copy-done.7), channel_id=1, source_target_pairs={{0,1},{1,0},{2,3},{3,2},{4,5},{5,4},{6,7},{7,6},{8,9},{9,8},{10,11... | collective-permute-start | bytes 344072 | tf_op jit(solution)/shard_map/ppermute | solution.py:480
  90.9 6.7 %collective-permute-start.14 = (bf16[32,1792]{1,0:T(8,128)(2,1)}, bf16[32,1792]{1,0:T(8,128)(2,1)S(1)}, u32[]{:S(2)}, u32[]{:S(2)}) collective-permute-start(bf16[32,1792]{1,0:T(8,128)(2,1)} %copy-done.6), channel_id=1, source_target_pairs={{0,2},{2,0},{1,3},{3,1},{4,6},{6,4},{5,7},{7,5},{8,10},{10,8},{9,1... | collective-permute-start | bytes 344072 | tf_op jit(solution)/shard_map/ppermute | solution.py:480
  93.4 5.1 %collective-permute-start.15 = (bf16[32,1792]{1,0:T(8,128)(2,1)}, bf16[32,1792]{1,0:T(8,128)(2,1)S(1)}, u32[]{:S(2)}, u32[]{:S(2)}) collective-permute-start(bf16[32,1792]{1,0:T(8,128)(2,1)} %copy-done.5), channel_id=1, source_target_pairs={{0,12},{12,0},{4,8},{8,4},{1,13},{13,1},{5,9},{9,5},{2,14},{14,2},... | collective-permute-start | bytes 344072 | tf_op jit(solution)/shard_map/ppermute | solution.py:480
  94.9 3.7 %collective-permute-start.16 = (bf16[32,1792]{1,0:T(8,128)(2,1)S(1)}, bf16[32,1792]{1,0:T(8,128)(2,1)S(1)}, u32[]{:S(2)}, u32[]{:S(2)}) collective-permute-start(bf16[32,1792]{1,0:T(8,128)(2,1)S(1)} %get-tuple-element.39), channel_id=1, source_target_pairs={{0,4},{4,0},{8,12},{12,8},{1,5},{5,1},{9,13},{13,9},{2,6},{6,2},{1... | collective-permute-start | bytes 344072 | tf_op jit(solution)/shard_map/ppermute | solution.py:480
  94.9 6.1 %collective-permute-start.17 = (bf16[32,1792]{1,0:T(8,128)(2,1)S(1)}, bf16[32,1792]{1,0:T(8,128)(2,1)S(1)}, u32[]{:S(2)}, u32[]{:S(2)}) collective-permute-start(bf16[32,1792]{1,0:T(8,128)(2,1)S(1)} %get-tuple-element.40), channel_id=1, source_target_pairs={{0,8},{8,0},{4,12},{12,4},{1,9},{9,1},{5,13},{13,5},{2,10},{10,2},... | collective-permute-start | bytes 344072 | tf_op jit(solution)/shard_map/ppermute | solution.py:480
  101.2 6.9 %collective-permute-start.18 = (bf16[8,3584]{1,0:T(8,128)(2,1)S(1)}, bf16[8,3584]{1,0:T(8,128)(2,1)S(1)}, u32[]{:S(2)}, u32[]{:S(2)}) collective-permute-start(bf16[8,3584]{1,0:T(8,128)(2,1)S(1)} %get-tuple-element.41), channel_id=1, source_target_pairs={{0,16},{16,0},{32,48},{48,32},{64,80},{80,64},{96,112},{112,96},{1... | collective-permute-start | bytes 172040 | tf_op jit(solution)/shard_map/ppermute | solution.py:490
  108.1 5.5 %collective-permute-start.19 = (bf16[8,3584]{1,0:T(8,128)(2,1)S(1)}, bf16[8,3584]{1,0:T(8,128)(2,1)S(1)}, u32[]{:S(2)}, u32[]{:S(2)}) collective-permute-start(bf16[8,3584]{1,0:T(8,128)(2,1)S(1)} %broadcast_select_fusion), channel_id=1, source_target_pairs={{0,32},{16,48},{32,64},{48,80},{64,96},{80,112},{96,0},{112,16},{1... | collective-permute-start | bytes 172040 | tf_op jit(solution)/shard_map/ppermute | solution.py:486
  109.5 6.0 %collective-permute-start.20 = (bf16[8,3584]{1,0:T(8,128)(2,1)S(1)}, bf16[8,3584]{1,0:T(8,128)(2,1)S(1)}, u32[]{:S(2)}, u32[]{:S(2)}) collective-permute-start(bf16[8,3584]{1,0:T(8,128)(2,1)S(1)} %broadcast_select_fusion), channel_id=1, source_target_pairs={{0,64},{16,80},{32,96},{48,112},{64,0},{80,16},{96,32},{112,48},{1... | collective-permute-start | bytes 172040 | tf_op jit(solution)/shard_map/ppermute | solution.py:486
  112.9 3.3 %collective-permute-start.21 = (bf16[8,3584]{1,0:T(8,128)(2,1)S(1)}, bf16[8,3584]{1,0:T(8,128)(2,1)S(1)}, u32[]{:S(2)}, u32[]{:S(2)}) collective-permute-start(bf16[8,3584]{1,0:T(8,128)(2,1)S(1)} %broadcast_select_fusion), channel_id=1, source_target_pairs={{0,96},{16,112},{32,0},{48,16},{64,32},{80,48},{96,64},{112,80},{1... | collective-permute-start | bytes 172040 | tf_op jit(solution)/shard_map/ppermute | solution.py:486
  116.2 56.8 %slice-start = ((s8[7340032]{0:T(1024)(128)(4,1)}), s8[4194304]{0:T(1024)(128)(4,1)S(1)}, s32[]{:S(2)}) async-start(s8[7340032]{0:T(1024)(128)(4,1)} %bitcast.44), calls=%async_computation.3 | async-start | bytes 8388608
  118.4 54.7 %slice-start.1 = ((s8[7340032]{0:T(1024)(128)(4,1)}), s8[3145728]{0:T(1024)(128)(4,1)S(1)}, s32[]{:S(2)}) async-start(s8[7340032]{0:T(1024)(128)(4,1)} %bitcast.44), calls=%async_computation.4 | async-start | bytes 6291456
  184.9 4.8 %copy-start.15 = (f32[32,8]{0,1:T(8,128)S(1)}, f32[32,8]{0,1:T(8,128)}, u32[]{:S(2)}) copy-start(f32[32,8]{0,1:T(8,128)} %param.27) | copy-start | bytes 3076
  184.9 51.4 %all-to-all-start.2 = ((bf16[128,8,1792]{2,1,0:T(8,128)(2,1)}), bf16[128,8,1792]{2,1,0:T(8,128)(2,1)}, u32[]{:S(2)}, u32[]{:S(2)}) async-start(bf16[128,8,1792]{2,1,0:T(8,128)(2,1)} %bitcast.46), calls=%async_computation.2 | async-start | bytes 7340032 | tf_op jit(solution)/shard_map/all_to_all | solution.py:582
